TPU v7x, 8 devices: a whole 2x2x1 slice. The times are simulated.
8 devices in a mesh: ens: 1 (over z), part: 2 (over y), feat: 4 (over x, core).
Axes of the slice: x: 2, y: 2, z: 1, core: 2. Of those that a mesh axis runs over, the one named last changes fastest.
Arguments:
- particles: float32 [2048, 28672], P(('ens', 'part'), 'feat')
- prec_diag: float32 [28672], P(('ens', 'feat'))
- target_mean: float32 [28672], P(('ens', 'feat'))
- low_factor: bfloat16 [28672, 32], P(('ens', 'feat'))
Outputs:
- output: float32 [2048, 28672], P(('ens', 'part'), 'feat')
All inputs are finite; a program needn't handle non-finite values.
Results may differ from a plain program's by a relative error of at most 0.00356208.
Values are sent between devices in bfloat16 or wider.
A program may use at most 1 GiB of HBM per device.

v0:
```python
import functools
import math
import jax
import jax.numpy as jnp
from jax import lax
from jax.experimental import pallas as pl
from jax.experimental.pallas import tpu as pltpu
from jax.sharding import PartitionSpec as P

NUM_STEPS = 3
BLK = 256
HALF = BLK // 2
REACH = 5
WIDE = 9 * HALF
MESH = pl.DeviceIdType.MESH
F32 = jnp.float32
BF16 = jnp.bfloat16
ANY = pl.BlockSpec(memory_space=pl.ANY)
VMEM = pl.BlockSpec(memory_space=pltpu.VMEM)
VMEM_LIMIT = 63 * 1024 * 1024
NT = (((1,), (1,)), ((), ()))


def band_parts(k, val):
    top, low = val[:HALF], val[HALF:]
    if k == 0:
        return (0, 0, top), (1, 0, low[:, HALF:])
    if k == REACH - 1:
        top = top[:, :HALF]
    return (0, k * BLK, top), (1, k * BLK - HALF, low)


def exchange_kernel(n_chunk, theta_ref, mean_ref, fact_ref, col_ref, gram_ref, proj_ref,
                    buf, tb, send_sem, recv_sem, own_sem, put_sem, other_sem):
    part = lax.axis_index("part")
    other = 1 - part
    feat = lax.axis_index("feat")
    peer = (lax.axis_index("ens"), other, feat)
    rows, width = theta_ref.shape[0], col_ref.shape[1]
    n_rows = col_ref.shape[0]
    cw = width // n_chunk
    n_blk = n_rows // BLK
    barrier = pltpu.get_barrier_semaphore()
    pl.semaphore_signal(barrier, inc=1, device_id=peer, device_id_type=MESH)
    pl.semaphore_wait(barrier, 1)
    own_rows = pl.ds(pl.multiple_of(part * rows, BLK), rows)
    other_rows = pl.ds(pl.multiple_of(other * rows, BLK), rows)

    def remote(c):
        return pltpu.make_async_remote_copy(
            src_ref=theta_ref.at[:, pl.ds(pl.multiple_of(other * width + c * cw, 128), cw)],
            dst_ref=col_ref.at[own_rows, pl.ds(pl.multiple_of(c * cw, 128), cw)],
            send_sem=send_sem.at[c], recv_sem=recv_sem.at[c], device_id=peer, device_id_type=MESH)

    def fetch_own(c):
        return pltpu.make_async_copy(
            theta_ref.at[:, pl.ds(pl.multiple_of(part * width + c * cw, 128), cw)],
            buf.at[own_rows, :], own_sem)

    def put_own(c):
        return pltpu.make_async_copy(
            buf.at[own_rows, :], col_ref.at[own_rows, pl.ds(pl.multiple_of(c * cw, 128), cw)], put_sem)

    def fetch_other(c):
        return pltpu.make_async_copy(
            col_ref.at[other_rows, pl.ds(pl.multiple_of(c * cw, 128), cw)], buf.at[other_rows, :], other_sem)

    @pl.loop(0, n_chunk)
    def _(c):
        remote(c).start()

    gram_ref[...] = jnp.zeros_like(gram_ref)
    proj_ref[...] = jnp.zeros_like(proj_ref)

    @pl.loop(0, n_chunk)
    def _(c):
        fetch_own(c).start()
        fetch_own(c).wait()
        put_own(c).start()
        remote(c).wait_recv()
        fetch_other(c).start()
        fetch_other(c).wait()
        cols = pl.ds(pl.multiple_of(c * cw, 128), cw)
        fact = fact_ref[:, cols]
        mean = mean_ref[:, cols]

        @pl.loop(0, n_blk)
        def _(b):
            rs = pl.ds(pl.multiple_of(b * BLK, BLK), BLK)
            th = buf[rs, :]
            tb[rs, :] = th.astype(BF16)
            proj_ref[:, rs] += lax.dot_general(fact, (th - mean).astype(BF16), NT, preferred_element_type=F32)

        for b in range(n_blk):
            rows_b = tb[b * BLK:(b + 1) * BLK, :]
            for k in range(REACH):
                j = (b + k) % n_blk
                val = lax.dot_general(rows_b, tb[j * BLK:(j + 1) * BLK, :], NT, preferred_element_type=F32)
                for h, col, piece in band_parts(k, val):
                    gram_ref[b, h, :, col:col + piece.shape[1]] += piece
        put_own(c).wait()

    @pl.loop(0, n_chunk)
    def _(c):
        remote(c).wait_send()


def exchange(theta, mean, fact_t, n_chunk):
    rows, feat = theta.shape
    width = feat // 2
    n_rows = rows * 2
    rank = fact_t.shape[0]
    return pl.pallas_call(
        functools.partial(exchange_kernel, n_chunk),
        out_shape=(jax.ShapeDtypeStruct((n_rows, width), F32),
                   jax.ShapeDtypeStruct((n_rows // BLK, 2, HALF, WIDE), F32),
                   jax.ShapeDtypeStruct((rank, n_rows), F32)),
        in_specs=[ANY, VMEM, VMEM], out_specs=(ANY, VMEM, VMEM),
        scratch_shapes=[
            pltpu.VMEM((n_rows, width // n_chunk), F32),
            pltpu.VMEM((n_rows, width // n_chunk), BF16),
            pltpu.SemaphoreType.DMA((n_chunk,)), pltpu.SemaphoreType.DMA((n_chunk,)),
            pltpu.SemaphoreType.DMA, pltpu.SemaphoreType.DMA, pltpu.SemaphoreType.DMA],
        compiler_params=pltpu.CompilerParams(collective_id=0, has_side_effects=True, vmem_limit_bytes=VMEM_LIMIT),
        name="exchange",
    )(theta, mean, fact_t)


def build_rhs(theta_ref, mean, prec, fact, zb_ref, rhs, rs):
    tile = theta_ref.shape[1]
    th = theta_ref[rs, :]
    low = jnp.dot(zb_ref[rs, :], fact, preferred_element_type=F32)
    rhs[rs, :tile] = (-((th - mean) * prec + low)).astype(BF16)
    rhs[rs, tile:] = th.astype(BF16)


def stepped(theta_ref, acc, mass_ref, rs, inv_n, two_over_h, step_size):
    tile = theta_ref.shape[1]
    th = theta_ref[rs, :]
    pull = mass_ref[rs, :] * th.astype(BF16).astype(F32) - acc[:, tile:]
    return th + step_size * ((acc[:, :tile] + two_over_h * pull) * inv_n)


def update_kernel(consts, theta_ref, next_ref, kern_ref, mass_ref, zb_ref, mean_ref, prec_ref, fact_ref,
                  mean_n, prec_n, fact_n, out_ref, tb_ref, proj_ref, rhs):
    n_rows = theta_ref.shape[0]
    big = n_rows // 2
    slot = lax.rem(pl.program_id(0), 2)

    @pl.when(pl.program_id(0) == 0)
    def _():
        proj_ref[...] = jnp.zeros_like(proj_ref)

        @pl.loop(0, n_rows // BLK)
        def _(b):
            build_rhs(theta_ref, mean_ref[...], prec_ref[...], fact_ref[...], zb_ref, rhs.at[0],
                      pl.ds(pl.multiple_of(b * BLK, BLK), BLK))

    @pl.loop(0, 2)
    def _(b):
        rs = pl.ds(pl.multiple_of(b * big, big), big)
        acc = jnp.dot(kern_ref[rs, :], rhs[slot], preferred_element_type=F32)
        build_rhs(next_ref, mean_n[...], prec_n[...], fact_n[...], zb_ref, rhs.at[1 - slot], rs)
        new = stepped(theta_ref, acc, mass_ref, rs, *consts)
        out_ref[rs, :] = new
        tb_ref[rs, :] = new.astype(BF16)
        proj_ref[:, rs] += lax.dot_general(fact_ref[...], (new - mean_ref[...]).astype(BF16), NT, preferred_element_type=F32)


def update(consts, theta, kern, mass, zb, mean, prec, fact_t, tile):
    n_rows, width = theta.shape
    rank = fact_t.shape[0]
    steps = width // tile
    col = lambda r: pl.BlockSpec((r, tile), lambda i: (0, i))
    nxt = lambda r: pl.BlockSpec((r, tile), lambda i: (0, jnp.minimum(i + 1, steps - 1)))
    return pl.pallas_call(
        functools.partial(update_kernel, consts),
        grid=(steps,),
        out_shape=(jax.ShapeDtypeStruct((n_rows, width), F32),
                   jax.ShapeDtypeStruct((n_rows, width), BF16),
                   jax.ShapeDtypeStruct((rank, n_rows), F32)),
        in_specs=[col(n_rows), nxt(n_rows), VMEM, VMEM, VMEM, col(1), col(1), col(rank), nxt(1), nxt(1), nxt(rank)],
        out_specs=(col(n_rows), col(n_rows), VMEM),
        scratch_shapes=[pltpu.VMEM((2, n_rows, 2 * tile), BF16)],
        compiler_params=pltpu.CompilerParams(vmem_limit_bytes=VMEM_LIMIT),
        cost_estimate=pl.CostEstimate(flops=4 * n_rows * n_rows * width, bytes_accessed=10 * n_rows * width, transcendentals=0),
        name="update",
    )(theta, theta, kern, mass, zb, mean, prec, fact_t, mean, prec, fact_t)


def last_kernel(consts, pos_ref, theta_ref, kern_ref, mass_ref, zb_ref, mean_ref, prec_ref, fact_ref, *rest):
    out_ref, send_ref, rhs = rest[-3:]
    rows = out_ref.shape[0]
    n_blk = theta_ref.shape[0] // BLK
    part = pos_ref[0]
    fact, mean, prec = fact_ref[...], mean_ref[...], prec_ref[...]

    @pl.loop(0, n_blk)
    def _(b):
        build_rhs(theta_ref, mean, prec, fact, zb_ref, rhs, pl.ds(pl.multiple_of(b * BLK, BLK), BLK))

    for dst, which in ((send_ref, 1 - part), (out_ref, part)):
        @pl.loop(0, rows // BLK)
        def _(b):
            rs = pl.ds(pl.multiple_of(which * rows + b * BLK, BLK), BLK)
            acc = jnp.dot(kern_ref[rs, :], rhs[...], preferred_element_type=F32)
            dst[pl.ds(pl.multiple_of(b * BLK, BLK), BLK), :] = stepped(theta_ref, acc, mass_ref, rs, *consts)


def last_update(consts, pos, theta, kern, mass, zb, mean, prec, fact_t, out, start, tile):
    n_rows, width = theta.shape
    chunk = start // tile
    rank = fact_t.shape[0]
    rows, feat = n_rows // 2, width * 2
    per = width // tile
    col = lambda r: pl.BlockSpec((r, tile), lambda i, pos: (0, chunk))
    in_specs = [col(n_rows), VMEM, VMEM, VMEM, col(1), col(1), col(rank)]
    args = [theta, kern, mass, zb, mean, prec, fact_t]
    alias = {}
    if out is not None:
        in_specs.append(ANY)
        args.append(out)
        alias = {8: 0}
    return pl.pallas_call(
        functools.partial(last_kernel, consts),
        grid_spec=pltpu.PrefetchScalarGridSpec(
            num_scalar_prefetch=1, grid=(1,), in_specs=in_specs,
            out_specs=(pl.BlockSpec((rows, tile), lambda i, pos: (0, pos[0] * per + chunk)),
                       pl.BlockSpec((rows, tile), lambda i, pos: (0, 0))),
            scratch_shapes=[pltpu.VMEM((n_rows, 2 * tile), BF16)]),
        out_shape=(jax.ShapeDtypeStruct((rows, feat), F32), jax.ShapeDtypeStruct((rows, tile), F32)),
        input_output_aliases=alias,
        compiler_params=pltpu.CompilerParams(vmem_limit_bytes=VMEM_LIMIT),
        cost_estimate=pl.CostEstimate(flops=4 * n_rows * n_rows * tile, bytes_accessed=10 * n_rows * tile, transcendentals=0),
    )(pos, *args)


def place_kernel(pos_ref, recv_ref, base_ref, out_ref):
    out_ref[...] = recv_ref[...]


def place(pos, recv, out, start):
    rows, tile = recv.shape
    per = out.shape[1] // 256
    sub = tile // 128
    first = start // 128
    return pl.pallas_call(
        place_kernel,
        grid_spec=pltpu.PrefetchScalarGridSpec(
            num_scalar_prefetch=1, grid=(sub,), in_specs=[pl.BlockSpec((rows, 128), lambda i, pos: (0, i)), ANY],
            out_specs=pl.BlockSpec((rows, 128), lambda i, pos: (0, (1 - pos[0]) * per + first + i))),
        out_shape=jax.ShapeDtypeStruct(out.shape, out.dtype),
        input_output_aliases={2: 0},
        cost_estimate=pl.CostEstimate(flops=1000 * rows * tile, bytes_accessed=8 * rows * tile, transcendentals=0),
    )(pos, recv, out)


def kmat_kernel(from_gram, two_over_h, src_ref, proj_ref, kern_ref, zb_ref, mass_ref, *scratch):
    if from_gram:
        tb, sib_out = None, None
    else:
        tb, sib_out, load_sem = scratch[-3:]
    (gbuf, sib_in, r_x1, r_y1, r_x2, r_y2, sq_parts, sq, z_in, z_all, kbuf,
     sib_send, sib_recv, rs_send, rs_recv, sq_send, sq_recv, z_send, z_recv, zb_send, zb_recv,
     k_send, k_recv, loc_sem) = scratch[:24]
    n_rows = kern_ref.shape[0]
    n_blk = n_rows // BLK
    ens, part, feat = lax.axis_index("ens"), lax.axis_index("part"), lax.axis_index("feat")
    x, core = feat // 2, lax.rem(feat, 2)

    def chip(rel):
        return lax.rem(part + rel // 2, 2), lax.rem(x + rel % 2, 2)

    def block(rel, flip):
        cy, cx = chip(rel)
        return cy * 4 + cx * 2 + lax.rem(core + flip, 2)

    def device(rel, flip):
        cy, cx = chip(rel)
        return (ens, cy, cx * 2 + lax.rem(core + flip, 2))

    me = block(0, 0)
    sibling, dev_x, dev_y = device(0, 1), device(1, 0), device(2, 0)
    others = [(rel, flip) for rel in (3, 1, 2, 0) for flip in (0, 1) if (rel, flip) != (0, 0)]

    def rcopy(src, dst, ssem, rsem, dev):
        return pltpu.make_async_remote_copy(src_ref=src, dst_ref=dst, send_sem=ssem, recv_sem=rsem,
                                            device_id=dev, device_id_type=MESH)

    barrier = pltpu.get_barrier_semaphore()
    for rel, flip in others:
        pl.semaphore_signal(barrier, inc=1, device_id=device(rel, flip), device_id_type=MESH)

    def load(b):
        rs = pl.ds(b * BLK, BLK)
        return pltpu.make_async_copy(src_ref.at[rs, :], tb.at[rs, :], load_sem.at[b])

    def own_gram(rel):
        return pltpu.make_async_copy(src_ref.at[block(rel, 0)], gbuf.at[rel], loc_sem.at[rel])

    if from_gram:
        for rel in (3, 2, 1, 0):
            own_gram(rel).start()
    else:
        for b in range(n_blk):
            load(b).start()
    pl.semaphore_wait(barrier, len(others))

    def z_cols(b):
        return proj_ref.at[:, pl.ds(pl.multiple_of(b * BLK, BLK), BLK)]

    def z_copy(i):
        rel, flip = others[i]
        return rcopy(z_cols(block(rel, flip)), z_in.at[me], z_send.at[i], z_recv.at[me], device(rel, flip))

    for i in range(len(others)):
        z_copy(i).start()
    z_own = pltpu.make_async_copy(z_cols(me), z_in.at[me], z_recv.at[me])
    z_own.start()

    def sib_copy(rel):
        src = src_ref.at[block(rel, 1)] if from_gram else sib_out.at[rel]
        return rcopy(src, sib_in.at[rel], sib_send.at[rel], sib_recv.at[rel], sibling)

    lo, hi = 0, 1
    rs_copies = {
        "d_lo": rcopy(gbuf.at[3, lo], r_x1.at[0], rs_send.at[0], rs_recv.at[0], dev_x),
        "d_hi": rcopy(gbuf.at[3, hi], r_y1.at[0], rs_send.at[1], rs_recv.at[1], dev_y),
        "y_hi": rcopy(gbuf.at[2, hi], r_y1.at[1], rs_send.at[2], rs_recv.at[2], dev_y),
        "x_lo": rcopy(gbuf.at[1, lo], r_x1.at[1], rs_send.at[3], rs_recv.at[3], dev_x),
        "y_lo": rcopy(gbuf.at[2, lo], r_y2, rs_send.at[4], rs_recv.at[4], dev_y),
        "x_hi": rcopy(gbuf.at[1, hi], r_x2, rs_send.at[5], rs_recv.at[5], dev_x),
    }
    eye = (lax.broadcasted_iota(jnp.int32, (HALF, HALF), 0) == lax.broadcasted_iota(jnp.int32, (HALF, HALF), 1)).astype(F32)

    def merge(rel):
        sib_copy(rel).wait_recv()
        gbuf[rel] += sib_in[rel]

    def first_sends(rel):
        for name in {3: ("d_lo", "d_hi"), 2: ("y_hi",), 1: ("x_lo",), 0: ()}[rel]:
            rs_copies[name].start()

    if from_gram:
        for rel in (3, 2, 1, 0):
            sib_copy(rel).start()
        for rel in (3, 2, 1, 0):
            own_gram(rel).wait()
            merge(rel)
            first_sends(rel)
    else:
        def bands_of(b, dst):
            rows = tb[pl.ds(pl.multiple_of(b * BLK, BLK), BLK), :]
            for k in range(REACH):
                j = lax.rem(b + k, n_blk)
                val = lax.dot_general(
                    rows, tb[pl.ds(pl.multiple_of(j * BLK, BLK), BLK), :], NT, preferred_element_type=F32)
                for h, col, piece in band_parts(k, val):
                    dst[h, :, col:col + piece.shape[1]] = piece

        for b in range(n_blk):
            load(b).wait()

        @pl.loop(0, 4)
        def _(i):
            rel = 3 - i
            cy, cx = lax.rem(part + rel // 2, 2), lax.rem(x + lax.rem(rel, 2), 2)
            base = cy * 4 + cx * 2
            bands_of(base + 1 - core, sib_out.at[rel])
            rcopy(sib_out.at[rel], sib_in.at[rel], sib_send.at[rel], sib_recv.at[rel], sibling).start()
            bands_of(base + core, gbuf.at[rel])
            rcopy(sib_out.at[rel], sib_in.at[rel], sib_send.at[rel], sib_recv.at[rel], sibling).wait_recv()
            gbuf[rel] += sib_in[rel]
            for r in (3, 2, 1):
                @pl.when(rel == r)
                def _():
                    first_sends(r)

    for rel in range(4):
        cy, cx = chip(rel)
        for h in range(2):
            sq_parts[me, cy * 2 + cx, :, h * HALF:(h + 1) * HALF] = jnp.sum(gbuf[rel, h, :, :HALF] * eye, axis=0, keepdims=True)

    def sq_copy(i):
        rel, flip = others[i]
        return rcopy(sq_parts.at[me], sq_parts.at[me], sq_send.at[i], sq_recv.at[me], device(rel, flip))

    def recv_from(buf, sem, rel, flip):
        b = block(rel, flip)
        return rcopy(buf.at[b], buf.at[b], sq_send.at[0], sem.at[b], sibling)

    for i in range(len(others)):
        sq_copy(i).start()

    rs_copies["d_lo"].wait_recv()
    gbuf[2, 0] += r_x1[0]
    rs_copies["y_lo"].start()
    rs_copies["d_hi"].wait_recv()
    gbuf[1, 1] += r_y1[0]
    rs_copies["x_hi"].start()

    z_own.wait()
    for rel, flip in others:
        recv_from(z_in, z_recv, rel, flip).wait_recv()
    z_sum = z_in[0]
    for b in range(1, n_blk):
        z_sum = z_sum + z_in[b]
    z_all[me] = z_sum.astype(BF16)

    def zb_copy(i):
        rel, flip = others[i]
        return rcopy(z_all.at[me], z_all.at[me], zb_send.at[i], zb_recv.at[me], device(rel, flip))

    for i in range(len(others)):
        zb_copy(i).start()
    for rel, flip in others:
        recv_from(sq_parts, sq_recv, rel, flip).wait_recv()
    for c in range(2):
        for q in range(4):
            s = sq_parts[c, q] + sq_parts[2 + c, q] + sq_parts[4 + c, q] + sq_parts[6 + c, q]
            b = 2 * q + c
            sq[:, b * BLK:(b + 1) * BLK] = s
            if b < REACH - 1:
                sq[:, n_rows + b * BLK:n_rows + (b + 1) * BLK] = s

    def kernel_of(h, gram):
        row = sq[:, pl.ds(pl.multiple_of((2 * me + h) * HALF, HALF), WIDE)]
        col = jnp.sum(eye * row[:, :HALF], axis=1, keepdims=True)
        return jnp.exp(-jnp.maximum(col + row - 2.0 * gram, 0.0) * (0.5 * two_over_h)).astype(BF16)

    slots = iter(range(14))
    sent = []

    def send_band(idx, dev):
        s = next(slots)
        cp = rcopy(kbuf.at[idx], kbuf.at[idx], k_send.at[s], k_recv.at[idx], dev)
        cp.start()
        sent.append(cp)

    def wait_band(idx):
        rcopy(kbuf.at[idx], kbuf.at[idx], k_send.at[0], k_recv.at[idx], sibling).wait_recv()

    def spread(b, h):
        idx = 2 * b + h
        row0 = pl.multiple_of(idx * HALF, HALF)
        for k in range(REACH * 2 - 1):
            col0 = pl.multiple_of(lax.rem(idx + k, 2 * n_blk) * HALF, HALF)
            tile = kbuf[idx, :, k * HALF:(k + 1) * HALF]
            kern_ref[pl.ds(row0, HALF), pl.ds(col0, HALF)] = tile
            if 0 < k < REACH * 2 - 2:
                kern_ref[pl.ds(col0, HALF), pl.ds(row0, HALF)] = tile.T

    rs_copies["x_lo"].wait_recv()
    rs_copies["y_lo"].wait_recv()
    kbuf[2 * me] = kernel_of(0, gbuf[0, 0] + (r_x1[1] + r_y2[...]))
    for dev in (dev_y, sibling):
        send_band(2 * me, dev)
    rs_copies["y_hi"].wait_recv()
    rs_copies["x_hi"].wait_recv()
    kbuf[2 * me + 1] = kernel_of(1, gbuf[0, 1] + (r_y1[1] + r_x2[...]))
    for dev in (dev_x, sibling):
        send_band(2 * me + 1, dev)
    send_band(2 * me, dev_x)
    send_band(2 * me + 1, dev_y)
    spread(me, 0)
    spread(me, 1)
    sib = block(0, 1)
    for h in range(2):
        wait_band(2 * sib + h)
        spread(sib, h)
    bx, by, bd = block(1, 0), block(2, 0), block(3, 0)
    wait_band(2 * by)
    send_band(2 * by, dev_x)
    send_band(2 * by, sibling)
    wait_band(2 * bx + 1)
    send_band(2 * bx + 1, dev_y)
    send_band(2 * bx + 1, sibling)
    spread(by, 0)
    spread(bx, 1)
    for b, h in ((bx, 0), (by, 1), (bd, 0), (bd, 1)):
        wait_band(2 * b + h)
        send_band(2 * b + h, sibling)
        spread(b, h)
    for rel, h in ((2, 0), (1, 1), (1, 0), (2, 1), (3, 0), (3, 1)):
        b = block(rel, 1)
        wait_band(2 * b + h)
        spread(b, h)
    for rel, flip in others:
        recv_from(z_all, zb_recv, rel, flip).wait_recv()
    for b in range(n_blk):
        rs = slice(b * BLK, (b + 1) * BLK)
        zb_ref[rs, :] = z_all[b].astype(F32).T.astype(BF16)
        mass_ref[rs, :] = jnp.sum(kern_ref[rs, :].astype(F32), axis=1, keepdims=True)
    for rel in range(4):
        sib_copy(rel).wait_send()
    for cp in rs_copies.values():
        cp.wait_send()
    for i in range(len(others)):
        z_copy(i).wait_send()
        sq_copy(i).wait_send()
        zb_copy(i).wait_send()
    for cp in sent:
        cp.wait_send()


def kernel_matrix(src, proj, two_over_h, collective_id, from_gram):
    rank, n_rows = proj.shape
    n_blk = n_rows // BLK
    dma = lambda *n: pltpu.SemaphoreType.DMA(n)
    scratch = [
        pltpu.VMEM((4, 2, HALF, WIDE), F32), pltpu.VMEM((4, 2, HALF, WIDE), F32),
        pltpu.VMEM((2, HALF, WIDE), F32), pltpu.VMEM((2, HALF, WIDE), F32),
        pltpu.VMEM((HALF, WIDE), F32), pltpu.VMEM((HALF, WIDE), F32),
        pltpu.VMEM((8, 4, 1, BLK), F32), pltpu.VMEM((1, n_rows + (REACH - 1) * BLK), F32),
        pltpu.VMEM((n_blk, rank, BLK), F32), pltpu.VMEM((n_blk, rank, BLK), BF16),
        pltpu.VMEM((2 * n_blk, HALF, WIDE), BF16),
        dma(4), dma(4), dma(6), dma(6), dma(7), dma(8), dma(7), dma(8), dma(7), dma(8), dma(14), dma(16), dma(4)]
    if not from_gram:
        scratch += [pltpu.VMEM(src.shape, BF16), pltpu.VMEM((4, 2, HALF, WIDE), F32), dma(n_blk)]
    return pl.pallas_call(
        functools.partial(kmat_kernel, from_gram, two_over_h),
        out_shape=(jax.ShapeDtypeStruct((n_rows, n_rows), BF16), jax.ShapeDtypeStruct((n_rows, rank), BF16),
                   jax.ShapeDtypeStruct((n_rows, 1), F32)),
        in_specs=[ANY, VMEM], out_specs=(VMEM, VMEM, VMEM), scratch_shapes=scratch,
        compiler_params=pltpu.CompilerParams(collective_id=collective_id, has_side_effects=True, vmem_limit_bytes=VMEM_LIMIT),
    )(src, proj)


def solution(mesh):
    part_size = mesh.shape["part"]
    feat_size = mesh.shape["feat"]

    def local_steps(theta, prec_loc, mean_loc, factor_loc):
        rows, feat_loc = theta.shape
        n_total = rows * part_size
        feat_total = feat_loc * feat_size
        width = feat_loc // part_size
        kern_width = 2.0 * feat_total / math.log(n_total)
        step_size = 0.15 * n_total * feat_total / math.log(n_total)
        consts = (1.0 / n_total, 2.0 / kern_width, step_size)
        part = lax.axis_index("part")
        pos = part.astype(jnp.int32).reshape(1)
        mean = lax.dynamic_slice_in_dim(mean_loc, part * width, width).reshape(1, width)
        prec = lax.dynamic_slice_in_dim(prec_loc, part * width, width).reshape(1, width)
        fact_t = lax.dynamic_slice_in_dim(factor_loc, part * width, width, axis=0).T
        chunks = [(0, BLK)] + [(at, 2 * BLK) for at in range(2 * BLK, width, 2 * BLK)] + [(BLK, BLK)]
        assert chunks[-2][0] + 2 * BLK == width

        cur, gram, proj = exchange(theta, mean, fact_t, 7)
        src = gram
        for step in range(NUM_STEPS):
            kern, zb, mass = kernel_matrix(src, proj, consts[1], 1 + step, step == 0)
            if step < NUM_STEPS - 1:
                cur, src, proj = update(consts, cur, kern, mass, zb, mean, prec, fact_t, BLK)
        out = None
        received = []
        for start, tile in chunks:
            out, send = last_update(consts, pos, cur, kern, mass, zb, mean, prec, fact_t, out, start, tile)
            received.append(lax.ppermute(send, "part", [(0, 1), (1, 0)]))
        for (start, tile), recv in zip(chunks, received):
            out = place(pos, recv, out, start)
        return out

    row_spec = P(("ens", "part"), "feat")
    vec_spec = P(("ens", "feat"))
    fac_spec = P(("ens", "feat"), None)
    return jax.shard_map(local_steps, mesh=mesh, in_specs=(row_spec, vec_spec, vec_spec, fac_spec), out_specs=row_spec, check_vma=False)
```

profile of v0, /device:TPU:0, one launch (start us, length us, event | category | flops | bytes accessed | tf_op | source)
XLA Modules:
  0.0 1089.5 jit_solution(12005016806262027492)
XLA Ops:
  0.0 0.0 copy-start
  0.0 0.9 dynamic_slice.11
  0.9 0.6 reshape.11.prec_ref.prec_n
  1.5 0.8 dynamic_slice.9
  2.3 0.6 reshape.10.mean_ref.mean_n
  2.9 0.0 copy-done
  2.9 0.7 dynamic-slice_bitcast_fusion.fact_ref.fact_n
  3.6 329.8 %exchange.1 = (f32[2048,3584]{1,0:T(8,128)}, f32[8,2,128,1152]{3,2,1,0:T(8,128)}, f32[32,2048]{1,0:T(8,128)}) custom-call(f32[1024,7168]{1,0:T(8,128)} %theta_ref.1, f32[1,3584]{1,0:T(1,128)} %reshape.10.mean_ref.mean_n, bf16[32,3584]{1,0:T(8,128)(2,1)} %dynamic-slice_bitcast_fusion.fact_ref.fact_n), custom_call_target="tpu_custom_call" | custom-call | tf_op jit(solution)/shard_map/exchange/pallas_call | solution.py:113
  333.4 75.2 %shard_map.46 = (bf16[2048,2048]{1,0:T(8,128)(2,1)}, bf16[2048,32]{1,0:T(8,128)(2,1)}, f32[2048,1]{1,0:T(8,128)}) custom-call(f32[8,2,128,1152]{3,2,1,0:T(8,128)} %get-tuple-element.40.src_ref, f32[32,2048]{1,0:T(8,128)} %get-tuple-element.41.proj_ref), custom_call_target="tpu_custom_call" | custom-call | tf_op jit(solution)/shard_map/pallas_call | solution.py:520
  408.6 83.2 %update.2 = (f32[2048,3584]{1,0:T(8,128)}, bf16[2048,3584]{1,0:T(8,128)(2,1)}, f32[32,2048]{1,0:T(8,128)}) custom-call(f32[2048,3584]{1,0:T(8,128)} %get-tuple-element.39.theta_ref.next_ref, f32[2048,3584]{1,0:T(8,128)} %get-tuple-element.39.theta_ref.next_ref, bf16[2048,2048]{1,0:T(8,128)(2,1)} %get-tuple-element.42.kern_ref, ...), custom_call_target="tpu_custom_call" | custom-call | flops 60129542144 | bytes 73400320 | tf_op jit(solution)/shard_map/update/pallas_call | solution.py:176
  491.8 83.1 %shard_map.47 = (bf16[2048,2048]{1,0:T(8,128)(2,1)}, bf16[2048,32]{1,0:T(8,128)(2,1)}, f32[2048,1]{1,0:T(8,128)}) custom-call(bf16[2048,3584]{1,0:T(8,128)(2,1)} %get-tuple-element.46.src_ref, f32[32,2048]{1,0:T(8,128)} %get-tuple-element.47.proj_ref), custom_call_target="tpu_custom_call" | custom-call | tf_op jit(solution)/shard_map/pallas_call | solution.py:520
  574.9 83.3 %update.3 = (f32[2048,3584]{1,0:T(8,128)}, bf16[2048,3584]{1,0:T(8,128)(2,1)}, f32[32,2048]{1,0:T(8,128)}) custom-call(f32[2048,3584]{1,0:T(8,128)} %get-tuple-element.45.theta_ref.next_ref, f32[2048,3584]{1,0:T(8,128)} %get-tuple-element.45.theta_ref.next_ref, bf16[2048,2048]{1,0:T(8,128)(2,1)} %get-tuple-element.48.kern_ref, ...), custom_call_target="tpu_custom_call" | custom-call | flops 60129542144 | bytes 73400320 | tf_op jit(solution)/shard_map/update/pallas_call | solution.py:176
  658.1 82.3 %shard_map.48 = (bf16[2048,2048]{1,0:T(8,128)(2,1)}, bf16[2048,32]{1,0:T(8,128)(2,1)}, f32[2048,1]{1,0:T(8,128)}) custom-call(bf16[2048,3584]{1,0:T(8,128)(2,1)} %get-tuple-element.52.src_ref, f32[32,2048]{1,0:T(8,128)} %get-tuple-element.53.proj_ref), custom_call_target="tpu_custom_call" | custom-call | tf_op jit(solution)/shard_map/pallas_call | solution.py:520
  740.4 12.6 %shard_map.49 = (f32[1024,7168]{1,0:T(8,128)}, f32[1024,256]{1,0:T(8,128)}) custom-call(s32[1]{0:T(128)} %bitcast.pos_ref, f32[2048,3584]{1,0:T(8,128)} %get-tuple-element.51.theta_ref, bf16[2048,2048]{1,0:T(8,128)(2,1)} %get-tuple-element.54.kern_ref, f32[2048,1]{1,0:T(8,128)} %get-tuple-element.55.mass_ref, bf16[2048,32]{1,0:T(8,128)(2,1)} %get-tuple-element.56.zb_ref, ...), custom_call_target="tpu_custom_call" | custom-call | flops 4294967296 | bytes 5242880 | tf_op jit(solution)/shard_map/pallas_call | solution.py:224
  753.0 0.8 collective-permute-start.7
  753.8 18.5 %shard_map.50 = (f32[1024,7168]{1,0:T(8,128)}, f32[1024,512]{1,0:T(8,128)}) custom-call(s32[1]{0:T(128)} %bitcast.pos_ref, f32[2048,3584]{1,0:T(8,128)} %get-tuple-element.51.theta_ref, bf16[2048,2048]{1,0:T(8,128)(2,1)} %get-tuple-element.54.kern_ref, f32[2048,1]{1,0:T(8,128)} %get-tuple-element.55.mass_ref, ...), custom_call_target="tpu_custom_call", output_to_operand_aliasing={{0}: (8, {})} | custom-call | flops 8589934592 | bytes 10485760 | tf_op jit(solution)/shard_map/pallas_call | solution.py:224
  772.2 18.6 %shard_map.51 = (f32[1024,7168]{1,0:T(8,128)}, f32[1024,512]{1,0:T(8,128)}) custom-call(s32[1]{0:T(128)} %bitcast.pos_ref, f32[2048,3584]{1,0:T(8,128)} %get-tuple-element.51.theta_ref, bf16[2048,2048]{1,0:T(8,128)(2,1)} %get-tuple-element.54.kern_ref, f32[2048,1]{1,0:T(8,128)} %get-tuple-element.55.mass_ref, ...), custom_call_target="tpu_custom_call", output_to_operand_aliasing={{0}: (8, {})} | custom-call | flops 8589934592 | bytes 10485760 | tf_op jit(solution)/shard_map/pallas_call | solution.py:224
  790.8 1.3 collective-permute-start.5
  792.1 0.7 collective-permute-start.6
  792.9 18.5 %shard_map.52 = (f32[1024,7168]{1,0:T(8,128)}, f32[1024,512]{1,0:T(8,128)}) custom-call(s32[1]{0:T(128)} %bitcast.pos_ref, f32[2048,3584]{1,0:T(8,128)} %get-tuple-element.51.theta_ref, bf16[2048,2048]{1,0:T(8,128)(2,1)} %get-tuple-element.54.kern_ref, f32[2048,1]{1,0:T(8,128)} %get-tuple-element.55.mass_ref, ...), custom_call_target="tpu_custom_call", output_to_operand_aliasing={{0}: (8, {})} | custom-call | flops 8589934592 | bytes 10485760 | tf_op jit(solution)/shard_map/pallas_call | solution.py:224
  811.3 18.6 %shard_map.53 = (f32[1024,7168]{1,0:T(8,128)}, f32[1024,512]{1,0:T(8,128)}) custom-call(s32[1]{0:T(128)} %bitcast.pos_ref, f32[2048,3584]{1,0:T(8,128)} %get-tuple-element.51.theta_ref, bf16[2048,2048]{1,0:T(8,128)(2,1)} %get-tuple-element.54.kern_ref, f32[2048,1]{1,0:T(8,128)} %get-tuple-element.55.mass_ref, ...), custom_call_target="tpu_custom_call", output_to_operand_aliasing={{0}: (8, {})} | custom-call | flops 8589934592 | bytes 10485760 | tf_op jit(solution)/shard_map/pallas_call | solution.py:224
  829.9 18.6 %shard_map.54 = (f32[1024,7168]{1,0:T(8,128)}, f32[1024,512]{1,0:T(8,128)}) custom-call(s32[1]{0:T(128)} %bitcast.pos_ref, f32[2048,3584]{1,0:T(8,128)} %get-tuple-element.51.theta_ref, bf16[2048,2048]{1,0:T(8,128)(2,1)} %get-tuple-element.54.kern_ref, f32[2048,1]{1,0:T(8,128)} %get-tuple-element.55.mass_ref, ...), custom_call_target="tpu_custom_call", output_to_operand_aliasing={{0}: (8, {})} | custom-call | flops 8589934592 | bytes 10485760 | tf_op jit(solution)/shard_map/pallas_call | solution.py:224
  848.5 1.3 collective-permute-start.2
  849.8 0.7 collective-permute-start.3
  850.5 0.0 collective-permute-done.7.recv_ref
  850.5 1.3 collective-permute-start.4
  851.8 18.5 %shard_map.55 = (f32[1024,7168]{1,0:T(8,128)}, f32[1024,512]{1,0:T(8,128)}) custom-call(s32[1]{0:T(128)} %bitcast.pos_ref, f32[2048,3584]{1,0:T(8,128)} %get-tuple-element.51.theta_ref, bf16[2048,2048]{1,0:T(8,128)(2,1)} %get-tuple-element.54.kern_ref, f32[2048,1]{1,0:T(8,128)} %get-tuple-element.55.mass_ref, ...), custom_call_target="tpu_custom_call", output_to_operand_aliasing={{0}: (8, {})} | custom-call | flops 8589934592 | bytes 10485760 | tf_op jit(solution)/shard_map/pallas_call | solution.py:224
  870.3 0.0 collective-permute-done.5.recv_ref
  870.3 0.7 collective-permute-start.1
  871.1 12.6 %shard_map.56 = (f32[1024,7168]{1,0:T(8,128)}, f32[1024,256]{1,0:T(8,128)}) custom-call(s32[1]{0:T(128)} %bitcast.pos_ref, f32[2048,3584]{1,0:T(8,128)} %get-tuple-element.51.theta_ref, bf16[2048,2048]{1,0:T(8,128)(2,1)} %get-tuple-element.54.kern_ref, f32[2048,1]{1,0:T(8,128)} %get-tuple-element.55.mass_ref, ...), custom_call_target="tpu_custom_call", output_to_operand_aliasing={{0}: (8, {})} | custom-call | flops 4294967296 | bytes 5242880 | tf_op jit(solution)/shard_map/pallas_call | solution.py:224
  883.7 0.9 collective-permute-done.6.recv_ref
  884.6 1.3 collective-permute-start
  885.9 2.0 shard_map.57.base_ref
  887.9 3.8 shard_map.58.base_ref
  891.7 3.8 shard_map.59.base_ref
  895.5 123.9 %collective-permute-done.4.recv_ref = f32[1024,512]{1,0:T(8,128)} collective-permute-done((f32[1024,512]{1,0:T(8,128)}, f32[1024,512]{1,0:T(8,128)}, u32[]{:S(2)}, u32[]{:S(2)}) %collective-permute-start.4) | collective-permute-done | bytes 2097184 | tf_op jit(solution)/shard_map/ppermute | solution.py:559
  1019.4 3.8 shard_map.60.base_ref
  1023.2 0.0 collective-permute-done.3.recv_ref
  1023.2 3.8 shard_map.61.base_ref
  1027.0 0.0 collective-permute-done.2.recv_ref
  1027.0 3.8 shard_map.62.base_ref
  1030.8 33.6 %collective-permute-done.1.recv_ref = f32[1024,512]{1,0:T(8,128)} collective-permute-done((f32[1024,512]{1,0:T(8,128)}, f32[1024,512]{1,0:T(8,128)}, u32[]{:S(2)}, u32[]{:S(2)}) %collective-permute-start.1) | collective-permute-done | bytes 2097184 | tf_op jit(solution)/shard_map/ppermute | solution.py:559
  1064.4 0.0 copy-start.1
  1064.4 3.8 shard_map.63.base_ref
  1068.2 18.0 %collective-permute-done.recv_ref = f32[1024,256]{1,0:T(8,128)S(1)} collective-permute-done((f32[1024,256]{1,0:T(8,128)}, f32[1024,256]{1,0:T(8,128)S(1)}, u32[]{:S(2)}, u32[]{:S(2)}) %collective-permute-start) | collective-permute-done | bytes 1048608 | tf_op jit(solution)/shard_map/ppermute | solution.py:559
  1086.2 1.0 copy-done.2
  1087.2 2.0 shard_map.64
  1089.3 0.0 copy-done.1
  (1 shorter events, 0.0 us)
Async XLA Ops:
  0.0 2.9 copy-start
  753.0 97.5 %collective-permute-start.7 = (f32[1024,256]{1,0:T(8,128)}, f32[1024,256]{1,0:T(8,128)}, u32[]{:S(2)}, u32[]{:S(2)}) collective-permute-start(f32[1024,256]{1,0:T(8,128)} %get-tuple-element.71), channel_id=1, source_target_pairs={{0,4},{4,0},{1,5},{5,1},{2,6},{6,2},{3,7},{7,3}} | collective-permute-start | bytes 3145736 | tf_op jit(solution)/shard_map/ppermute | solution.py:559
  790.8 79.5 %collective-permute-start.5 = (f32[1024,512]{1,0:T(8,128)}, f32[1024,512]{1,0:T(8,128)}, u32[]{:S(2)}, u32[]{:S(2)}) collective-permute-start(f32[1024,512]{1,0:T(8,128)} %get-tuple-element.69), channel_id=1, source_target_pairs={{0,4},{4,0},{1,5},{5,1},{2,6},{6,2},{3,7},{7,3}} | collective-permute-start | bytes 6291464 | tf_op jit(solution)/shard_map/ppermute | solution.py:559
  792.1 92.5 %collective-permute-start.6 = (f32[1024,512]{1,0:T(8,128)}, f32[1024,512]{1,0:T(8,128)}, u32[]{:S(2)}, u32[]{:S(2)}) collective-permute-start(f32[1024,512]{1,0:T(8,128)} %get-tuple-element.70), channel_id=1, source_target_pairs={{0,4},{4,0},{1,5},{5,1},{2,6},{6,2},{3,7},{7,3}} | collective-permute-start | bytes 6291464 | tf_op jit(solution)/shard_map/ppermute | solution.py:559
  848.5 178.5 %collective-permute-start.2 = (f32[1024,512]{1,0:T(8,128)}, f32[1024,512]{1,0:T(8,128)}, u32[]{:S(2)}, u32[]{:S(2)}) collective-permute-start(f32[1024,512]{1,0:T(8,128)} %get-tuple-element.66), channel_id=1, source_target_pairs={{0,4},{4,0},{1,5},{5,1},{2,6},{6,2},{3,7},{7,3}} | collective-permute-start | bytes 6291464 | tf_op jit(solution)/shard_map/ppermute | solution.py:559
  849.8 173.4 %collective-permute-start.3 = (f32[1024,512]{1,0:T(8,128)}, f32[1024,512]{1,0:T(8,128)}, u32[]{:S(2)}, u32[]{:S(2)}) collective-permute-start(f32[1024,512]{1,0:T(8,128)} %get-tuple-element.67), channel_id=1, source_target_pairs={{0,4},{4,0},{1,5},{5,1},{2,6},{6,2},{3,7},{7,3}} | collective-permute-start | bytes 6291464 | tf_op jit(solution)/shard_map/ppermute | solution.py:559
  850.5 168.9 %collective-permute-start.4 = (f32[1024,512]{1,0:T(8,128)}, f32[1024,512]{1,0:T(8,128)}, u32[]{:S(2)}, u32[]{:S(2)}) collective-permute-start(f32[1024,512]{1,0:T(8,128)} %get-tuple-element.68), channel_id=1, source_target_pairs={{0,4},{4,0},{1,5},{5,1},{2,6},{6,2},{3,7},{7,3}} | collective-permute-start | bytes 6291464 | tf_op jit(solution)/shard_map/ppermute | solution.py:559
  870.3 194.0 %collective-permute-start.1 = (f32[1024,512]{1,0:T(8,128)}, f32[1024,512]{1,0:T(8,128)}, u32[]{:S(2)}, u32[]{:S(2)}) collective-permute-start(f32[1024,512]{1,0:T(8,128)} %get-tuple-element.65), channel_id=1, source_target_pairs={{0,4},{4,0},{1,5},{5,1},{2,6},{6,2},{3,7},{7,3}} | collective-permute-start | bytes 6291464 | tf_op jit(solution)/shard_map/ppermute | solution.py:559
  884.6 201.6 %collective-permute-start = (f32[1024,256]{1,0:T(8,128)}, f32[1024,256]{1,0:T(8,128)S(1)}, u32[]{:S(2)}, u32[]{:S(2)}) collective-permute-start(f32[1024,256]{1,0:T(8,128)} %get-tuple-element.64), channel_id=1, source_target_pairs={{0,4},{4,0},{1,5},{5,1},{2,6},{6,2},{3,7},{7,3}} | collective-permute-start | bytes 3145736 | tf_op jit(solution)/shard_map/ppermute | solution.py:559
  1064.4 24.9 %copy-start.1 = (bf16[7168,32]{0,1:T(8,128)(2,1)S(1)}, bf16[7168,32]{0,1:T(8,128)(2,1)}, u32[]{:S(2)}) copy-start(bf16[7168,32]{0,1:T(8,128)(2,1)} %param.7) | copy-start | bytes 1376260
  1086.2 1.0 copy-start.2
where the time goes:
time: 1100 us; the launch traced here: 1090 us
  Pallas kernels  900 us (82%)
  waiting for transfers between devices  177 us (16%)
    pallas_call x1, Pallas kernels, exchange(): pl.pallas_call(functools.partial(exchange_kernel, n_chunk), out_shape=(ja...  330 us
    pallas_call x3, Pallas kernels, kernel_matrix(): pl.pallas_call(functools.partial(kmat_kernel, from_gram, two_over_h), out...  241 us
    ppermute x8, waiting for transfers between devices, local_steps(): received.append(lax.ppermute(send, 'part', [(0, 1), (1, 0)]))  177 us
    pallas_call x2, Pallas kernels, update(): pl.pallas_call(functools.partial(update_kernel, consts), grid=(steps,), o...  166 us
    pallas_call x8, Pallas kernels, last_update(): pl.pallas_call(functools.partial(last_kernel, consts), grid_spec=pltpu.Pr...  136 us
    pallas_call x8, Pallas kernels, place(): pl.pallas_call(place_kernel, grid_spec=pltpu.PrefetchScalarGridSpec(num_s...  26.8 us
  transfers between devices with their start and end apart: 8, of which 4 were waited for; matrix products, arithmetic and copies ran while one was open for 0% of the time, Pallas kernels for 14%

commit v1 on v0

--- a/solution.py
+++ b/solution.py
@@ -7,7 +7,6 @@
 from jax.experimental.pallas import tpu as pltpu
 from jax.sharding import PartitionSpec as P
 
-NUM_STEPS = 3
 BLK = 256
 HALF = BLK // 2
 REACH = 5
@@ -142,14 +141,15 @@
 
 
 def update_kernel(consts, theta_ref, next_ref, kern_ref, mass_ref, zb_ref, mean_ref, prec_ref, fact_ref,
-                  mean_n, prec_n, fact_n, out_ref, tb_ref, proj_ref, rhs):
+                  mean_n, prec_n, fact_n, *rest):
+    out_ref, tb_ref, proj_ref, rhs = rest[-4:]
     n_rows = theta_ref.shape[0]
     big = n_rows // 2
     slot = lax.rem(pl.program_id(0), 2)
 
     @pl.when(pl.program_id(0) == 0)
     def _():
-        proj_ref[...] = jnp.zeros_like(proj_ref)
+        proj_ref[...] = rest[0][...] if len(rest) > 4 else jnp.zeros_like(proj_ref)
 
         @pl.loop(0, n_rows // BLK)
         def _(b):
@@ -167,25 +167,32 @@
         proj_ref[:, rs] += lax.dot_general(fact_ref[...], (new - mean_ref[...]).astype(BF16), NT, preferred_element_type=F32)
 
 
-def update(consts, theta, kern, mass, zb, mean, prec, fact_t, tile):
+def update(consts, theta, kern, mass, zb, mean, prec, fact_t, tile, start, stop, own_out, before=None):
     n_rows, width = theta.shape
     rank = fact_t.shape[0]
-    steps = width // tile
-    col = lambda r: pl.BlockSpec((r, tile), lambda i: (0, i))
-    nxt = lambda r: pl.BlockSpec((r, tile), lambda i: (0, jnp.minimum(i + 1, steps - 1)))
+    first, steps = start // tile, (stop - start) // tile
+    col = lambda r: pl.BlockSpec((r, tile), lambda i: (0, first + i))
+    nxt = lambda r: pl.BlockSpec((r, tile), lambda i: (0, first + jnp.minimum(i + 1, steps - 1)))
+    in_specs = [col(n_rows), nxt(n_rows), VMEM, VMEM, VMEM, col(1), col(1), col(rank), nxt(1), nxt(1), nxt(rank)]
+    args = [theta, theta, kern, mass, zb, mean, prec, fact_t, mean, prec, fact_t]
+    alias = {}
+    if before is not None:
+        in_specs += [VMEM, ANY]
+        args += [before[1], before[0]]
+        alias = {12: 1}
     return pl.pallas_call(
         functools.partial(update_kernel, consts),
         grid=(steps,),
-        out_shape=(jax.ShapeDtypeStruct((n_rows, width), F32),
+        out_shape=(jax.ShapeDtypeStruct((n_rows, stop - start if own_out else width), F32),
                    jax.ShapeDtypeStruct((n_rows, width), BF16),
                    jax.ShapeDtypeStruct((rank, n_rows), F32)),
-        in_specs=[col(n_rows), nxt(n_rows), VMEM, VMEM, VMEM, col(1), col(1), col(rank), nxt(1), nxt(1), nxt(rank)],
-        out_specs=(col(n_rows), col(n_rows), VMEM),
+        in_specs=in_specs,
+        out_specs=(pl.BlockSpec((n_rows, tile), lambda i: (0, i)) if own_out else col(n_rows), col(n_rows), VMEM),
         scratch_shapes=[pltpu.VMEM((2, n_rows, 2 * tile), BF16)],
+        input_output_aliases=alias,
         compiler_params=pltpu.CompilerParams(vmem_limit_bytes=VMEM_LIMIT),
-        cost_estimate=pl.CostEstimate(flops=4 * n_rows * n_rows * width, bytes_accessed=10 * n_rows * width, transcendentals=0),
-        name="update",
-    )(theta, theta, kern, mass, zb, mean, prec, fact_t, mean, prec, fact_t)
+        cost_estimate=pl.CostEstimate(flops=4 * n_rows * n_rows * (stop - start), bytes_accessed=10 * n_rows * (stop - start), transcendentals=0),
+    )(*args)
 
 
 def last_kernel(consts, pos_ref, theta_ref, kern_ref, mass_ref, zb_ref, mean_ref, prec_ref, fact_ref, *rest):
@@ -233,6 +240,43 @@
         compiler_params=pltpu.CompilerParams(vmem_limit_bytes=VMEM_LIMIT),
         cost_estimate=pl.CostEstimate(flops=4 * n_rows * n_rows * tile, bytes_accessed=10 * n_rows * tile, transcendentals=0),
     )(pos, *args)
+
+
+def own_kernel(consts, pos_ref, theta_ref, kern_ref, mass_ref, zb_ref, mean_ref, prec_ref, fact_ref, base_ref, out_ref, rhs):
+    rows = out_ref.shape[0]
+    fact, mean, prec = fact_ref[...], mean_ref[...], prec_ref[...]
+
+    @pl.loop(0, theta_ref.shape[0] // BLK)
+    def _(b):
+        build_rhs(theta_ref, mean, prec, fact, zb_ref, rhs, pl.ds(pl.multiple_of(b * BLK, BLK), BLK))
+
+    @pl.loop(0, rows // BLK)
+    def _(b):
+        rs = pl.ds(pl.multiple_of(pos_ref[0] * rows + b * BLK, BLK), BLK)
+        acc = jnp.dot(kern_ref[rs, :], rhs[...], preferred_element_type=F32)
+        out_ref[pl.ds(pl.multiple_of(b * BLK, BLK), BLK), :] = stepped(theta_ref, acc, mass_ref, rs, *consts)
+
+
+def own_update(consts, pos, theta, kern, mass, zb, mean, prec, fact_t, out, foreign):
+    n_rows, cols = theta.shape
+    rank = fact_t.shape[0]
+    rows, feat = out.shape
+    per = feat // (2 * BLK)
+    col = lambda r: pl.BlockSpec((r, BLK), lambda i, pos: (0, i))
+    where = (lambda i, pos: (0, (1 - pos[0]) * per + i)) if foreign else (lambda i, pos: (0, pos[0] * per + i))
+    return pl.pallas_call(
+        functools.partial(own_kernel, consts),
+        grid_spec=pltpu.PrefetchScalarGridSpec(
+            num_scalar_prefetch=1, grid=(cols // BLK,),
+            in_specs=[col(n_rows), VMEM, VMEM, VMEM, col(1), col(1), col(rank), ANY],
+            out_specs=pl.BlockSpec((rows, BLK), where),
+            scratch_shapes=[pltpu.VMEM((n_rows, 2 * BLK), BF16)]),
+        out_shape=jax.ShapeDtypeStruct(out.shape, F32),
+        input_output_aliases={8: 0},
+        compiler_params=pltpu.CompilerParams(vmem_limit_bytes=VMEM_LIMIT),
+        cost_estimate=pl.CostEstimate(flops=4 * rows * n_rows * cols, bytes_accessed=10 * n_rows * cols, transcendentals=0),
+        name="own_foreign" if foreign else "own_shared",
+    )(pos, theta, kern, mass, zb, mean, prec, fact_t, out)
 
 
 def place_kernel(pos_ref, recv_ref, base_ref, out_ref):
@@ -543,20 +587,29 @@
         mean = lax.dynamic_slice_in_dim(mean_loc, part * width, width).reshape(1, width)
         prec = lax.dynamic_slice_in_dim(prec_loc, part * width, width).reshape(1, width)
         fact_t = lax.dynamic_slice_in_dim(factor_loc, part * width, width, axis=0).T
-        chunks = [(0, BLK)] + [(at, 2 * BLK) for at in range(2 * BLK, width, 2 * BLK)] + [(BLK, BLK)]
-        assert chunks[-2][0] + 2 * BLK == width
+        shared = 2 * BLK
+        chunks = [(shared, HALF)] + [(at, 2 * BLK) for at in range(2 * shared, width, 2 * BLK)] + [(shared + BLK, BLK), (shared + HALF, HALF)]
+        swap = [(0, 1), (1, 0)]
+        mean_f = lax.dynamic_slice_in_dim(mean_loc, (1 - part) * width, shared).reshape(1, shared)
+        prec_f = lax.dynamic_slice_in_dim(prec_loc, (1 - part) * width, shared).reshape(1, shared)
+        fact_f = lax.dynamic_slice_in_dim(factor_loc, (1 - part) * width, shared, axis=0).T
 
         cur, gram, proj = exchange(theta, mean, fact_t, 7)
-        src = gram
-        for step in range(NUM_STEPS):
-            kern, zb, mass = kernel_matrix(src, proj, consts[1], 1 + step, step == 0)
-            if step < NUM_STEPS - 1:
-                cur, src, proj = update(consts, cur, kern, mass, zb, mean, prec, fact_t, BLK)
+        params = (mean, prec, fact_t)
+        kern, zb, mass = kernel_matrix(gram, proj, consts[1], 1, True)
+        cur, tb, proj = update(consts, cur, kern, mass, zb, *params, BLK, 0, width, False)
+        kern, zb, mass = kernel_matrix(tb, proj, consts[1], 2, False)
+        both, tb, proj = update(consts, cur, kern, mass, zb, *params, BLK, 0, shared, True)
+        foreign = lax.ppermute(both, "part", swap)
+        cur, tb, proj = update(consts, cur, kern, mass, zb, *params, BLK, shared, width, False, (tb, proj))
+        kern, zb, mass = kernel_matrix(tb, proj, consts[1], 3, False)
         out = None
         received = []
         for start, tile in chunks:
-            out, send = last_update(consts, pos, cur, kern, mass, zb, mean, prec, fact_t, out, start, tile)
-            received.append(lax.ppermute(send, "part", [(0, 1), (1, 0)]))
+            out, send = last_update(consts, pos, cur, kern, mass, zb, *params, out, start, tile)
+            received.append(lax.ppermute(send, "part", swap))
+        out = own_update(consts, pos, both, kern, mass, zb, *params, out, False)
+        out = own_update(consts, pos, foreign, kern, mass, zb, mean_f, prec_f, fact_f, out, True)
         for (start, tile), recv in zip(chunks, received):
             out = place(pos, recv, out, start)
         return out

time: 1100 us -> 1060 us (0.964)
  waiting for transfers between devices: 177 us -> 105 us
  Pallas kernels: 900 us -> 929 us
    ppermute x8 -> x9, waiting for transfers between devices: 177 us -> 105 us  [the longest x8 105 us: local_steps(): received.append(lax.ppermute(send, 'part', swap))]
    pallas_call x0 -> x2, Pallas kernels: none -> 27.7 us  [own_update(): pl.pallas_call(functools.partial(own_kernel, consts), grid_spec=pltpu.Pre...]
    pallas_call x8, Pallas kernels: 136 us -> 124 us  [last_update(): pl.pallas_call(functools.partial(last_kernel, consts), grid_spec=pltpu.Pr...]
    pallas_call x2 -> x3, Pallas kernels: 166 us -> 175 us  [update(): pl.pallas_call(functools.partial(update_kernel, consts), grid=(steps,), o...]
  transfers between devices with their start and end apart: 8 -> 9, of which waited for: 4 -> 4; matrix products, arithmetic and copies ran while one was open for 0% -> 0% of each run, Pallas kernels for 14% -> 32%
where the time goes in v1:
time: 1060 us; the launch traced here: 1050 us
  Pallas kernels  929 us (88%)
  waiting for transfers between devices  105 us (10%)
    pallas_call x1, Pallas kernels, exchange(): pl.pallas_call(functools.partial(exchange_kernel, n_chunk), out_shape=(ja...  330 us
    pallas_call x3, Pallas kernels, kernel_matrix(): pl.pallas_call(functools.partial(kmat_kernel, from_gram, two_over_h), out...  248 us
    pallas_call x3, Pallas kernels, update(): pl.pallas_call(functools.partial(update_kernel, consts), grid=(steps,), o...  175 us
    pallas_call x8, Pallas kernels, last_update(): pl.pallas_call(functools.partial(last_kernel, consts), grid_spec=pltpu.Pr...  124 us
    ppermute x8, waiting for transfers between devices, local_steps(): received.append(lax.ppermute(send, 'part', swap))  105 us
    pallas_call x2, Pallas kernels, own_update(): pl.pallas_call(functools.partial(own_kernel, consts), grid_spec=pltpu.Pre...  27.7 us
    pallas_call x8, Pallas kernels, place(): pl.pallas_call(place_kernel, grid_spec=pltpu.PrefetchScalarGridSpec(num_s...  24.7 us
  transfers between devices with their start and end apart: 9, of which 4 were waited for; matrix products, arithmetic and copies ran while one was open for 0% of the time, Pallas kernels for 32%

profile of v1, /device:TPU:0, one launch (start us, length us, event | category | flops | bytes accessed | tf_op | source)
XLA Modules:
  0.0 1052.5 jit_solution(11529722675397637873)
XLA Ops:
  0.0 1.0 copy-done
  1.0 0.7 dynamic-slice_bitcast_fusion.fact_ref.fact_n
  1.7 0.8 dynamic_slice.18
  2.5 0.6 reshape.16.mean_ref.mean_n
  3.1 0.8 dynamic_slice.20
  3.9 0.6 reshape.17.prec_ref.prec_n
  4.5 329.8 %exchange.1 = (f32[2048,3584]{1,0:T(8,128)}, f32[8,2,128,1152]{3,2,1,0:T(8,128)}, f32[32,2048]{1,0:T(8,128)}) custom-call(f32[1024,7168]{1,0:T(8,128)} %theta_ref.1, f32[1,3584]{1,0:T(1,128)} %reshape.16.mean_ref.mean_n, bf16[32,3584]{1,0:T(8,128)(2,1)} %dynamic-slice_bitcast_fusion.fact_ref.fact_n), custom_call_target="tpu_custom_call" | custom-call | tf_op jit(solution)/shard_map/exchange/pallas_call | solution.py:112
  334.3 75.2 %shard_map.46 = (bf16[2048,2048]{1,0:T(8,128)(2,1)}, bf16[2048,32]{1,0:T(8,128)(2,1)}, f32[2048,1]{1,0:T(8,128)}) custom-call(f32[8,2,128,1152]{3,2,1,0:T(8,128)} %get-tuple-element.43.src_ref, f32[32,2048]{1,0:T(8,128)} %get-tuple-element.44.proj_ref), custom_call_target="tpu_custom_call" | custom-call | tf_op jit(solution)/shard_map/pallas_call | solution.py:564
  409.6 83.1 %shard_map.47 = (f32[2048,3584]{1,0:T(8,128)}, bf16[2048,3584]{1,0:T(8,128)(2,1)}, f32[32,2048]{1,0:T(8,128)}) custom-call(f32[2048,3584]{1,0:T(8,128)} %get-tuple-element.42.theta_ref.next_ref, f32[2048,3584]{1,0:T(8,128)} %get-tuple-element.42.theta_ref.next_ref, bf16[2048,2048]{1,0:T(8,128)(2,1)} %get-tuple-element.45.kern_ref, ...), custom_call_target="tpu_custom_call" | custom-call | flops 60129542144 | bytes 73400320 | tf_op jit(solution)/shard_map/pallas_call | solution.py:183
  492.7 83.1 %shard_map.48 = (bf16[2048,2048]{1,0:T(8,128)(2,1)}, bf16[2048,32]{1,0:T(8,128)(2,1)}, f32[2048,1]{1,0:T(8,128)}) custom-call(bf16[2048,3584]{1,0:T(8,128)(2,1)} %get-tuple-element.49.src_ref, f32[32,2048]{1,0:T(8,128)} %get-tuple-element.50.proj_ref), custom_call_target="tpu_custom_call" | custom-call | tf_op jit(solution)/shard_map/pallas_call | solution.py:564
  575.9 18.9 %shard_map.49 = (f32[2048,512]{1,0:T(8,128)}, bf16[2048,3584]{1,0:T(8,128)(2,1)}, f32[32,2048]{1,0:T(8,128)}) custom-call(f32[2048,3584]{1,0:T(8,128)} %get-tuple-element.48.theta_ref.next_ref, f32[2048,3584]{1,0:T(8,128)} %get-tuple-element.48.theta_ref.next_ref, bf16[2048,2048]{1,0:T(8,128)(2,1)} %get-tuple-element.51.kern_ref, ...), custom_call_target="tpu_custom_call" | custom-call | flops 8589934592 | bytes 10485760 | tf_op jit(solution)/shard_map/pallas_call | solution.py:183
  594.8 0.6 collective-permute-start.8
  595.3 73.0 %shard_map.50 = (f32[2048,3584]{1,0:T(8,128)}, bf16[2048,3584]{1,0:T(8,128)(2,1)}, f32[32,2048]{1,0:T(8,128)}) custom-call(f32[2048,3584]{1,0:T(8,128)} %get-tuple-element.48.theta_ref.next_ref, f32[2048,3584]{1,0:T(8,128)} %get-tuple-element.48.theta_ref.next_ref, bf16[2048,2048]{1,0:T(8,128)(2,1)} %get-tuple-element.51.kern_ref, ...), custom_call_target="tpu_custom_call", output_to_operand_aliasing={{1}: (12, {})} | custom-call | flops 51539607552 | bytes 62914560 | tf_op jit(solution)/shard_map/pallas_call | solution.py:183
  668.4 90.0 %shard_map.51 = (bf16[2048,2048]{1,0:T(8,128)(2,1)}, bf16[2048,32]{1,0:T(8,128)(2,1)}, f32[2048,1]{1,0:T(8,128)}) custom-call(bf16[2048,3584]{1,0:T(8,128)(2,1)} %get-tuple-element.57.src_ref, f32[32,2048]{1,0:T(8,128)} %get-tuple-element.58.proj_ref), custom_call_target="tpu_custom_call" | custom-call | tf_op jit(solution)/shard_map/pallas_call | solution.py:564
  758.4 9.7 shard_map.52
  768.0 1.1 collective-permute-start.7
  769.2 18.6 %shard_map.53 = (f32[1024,7168]{1,0:T(8,128)}, f32[1024,512]{1,0:T(8,128)}) custom-call(s32[1]{0:T(128)} %bitcast.pos_ref, f32[2048,3584]{1,0:T(8,128)} %get-tuple-element.56.theta_ref, bf16[2048,2048]{1,0:T(8,128)(2,1)} %get-tuple-element.59.kern_ref, f32[2048,1]{1,0:T(8,128)} %get-tuple-element.60.mass_ref, ...), custom_call_target="tpu_custom_call", output_to_operand_aliasing={{0}: (8, {})} | custom-call | flops 8589934592 | bytes 10485760 | tf_op jit(solution)/shard_map/pallas_call | solution.py:231
  787.8 0.9 collective-permute-start.6
  788.7 18.4 %shard_map.54 = (f32[1024,7168]{1,0:T(8,128)}, f32[1024,512]{1,0:T(8,128)}) custom-call(s32[1]{0:T(128)} %bitcast.pos_ref, f32[2048,3584]{1,0:T(8,128)} %get-tuple-element.56.theta_ref, bf16[2048,2048]{1,0:T(8,128)(2,1)} %get-tuple-element.59.kern_ref, f32[2048,1]{1,0:T(8,128)} %get-tuple-element.60.mass_ref, ...), custom_call_target="tpu_custom_call", output_to_operand_aliasing={{0}: (8, {})} | custom-call | flops 8589934592 | bytes 10485760 | tf_op jit(solution)/shard_map/pallas_call | solution.py:231
  807.0 1.1 collective-permute-start.5
  808.2 18.4 %shard_map.55 = (f32[1024,7168]{1,0:T(8,128)}, f32[1024,512]{1,0:T(8,128)}) custom-call(s32[1]{0:T(128)} %bitcast.pos_ref, f32[2048,3584]{1,0:T(8,128)} %get-tuple-element.56.theta_ref, bf16[2048,2048]{1,0:T(8,128)(2,1)} %get-tuple-element.59.kern_ref, f32[2048,1]{1,0:T(8,128)} %get-tuple-element.60.mass_ref, ...), custom_call_target="tpu_custom_call", output_to_operand_aliasing={{0}: (8, {})} | custom-call | flops 8589934592 | bytes 10485760 | tf_op jit(solution)/shard_map/pallas_call | solution.py:231
  826.6 0.9 collective-permute-start.4
  827.5 18.3 %shard_map.56 = (f32[1024,7168]{1,0:T(8,128)}, f32[1024,512]{1,0:T(8,128)}) custom-call(s32[1]{0:T(128)} %bitcast.pos_ref, f32[2048,3584]{1,0:T(8,128)} %get-tuple-element.56.theta_ref, bf16[2048,2048]{1,0:T(8,128)(2,1)} %get-tuple-element.59.kern_ref, f32[2048,1]{1,0:T(8,128)} %get-tuple-element.60.mass_ref, ...), custom_call_target="tpu_custom_call", output_to_operand_aliasing={{0}: (8, {})} | custom-call | flops 8589934592 | bytes 10485760 | tf_op jit(solution)/shard_map/pallas_call | solution.py:231
  845.8 1.2 collective-permute-start.3
  847.0 18.3 %shard_map.57 = (f32[1024,7168]{1,0:T(8,128)}, f32[1024,512]{1,0:T(8,128)}) custom-call(s32[1]{0:T(128)} %bitcast.pos_ref, f32[2048,3584]{1,0:T(8,128)} %get-tuple-element.56.theta_ref, bf16[2048,2048]{1,0:T(8,128)(2,1)} %get-tuple-element.59.kern_ref, f32[2048,1]{1,0:T(8,128)} %get-tuple-element.60.mass_ref, ...), custom_call_target="tpu_custom_call", output_to_operand_aliasing={{0}: (8, {})} | custom-call | flops 8589934592 | bytes 10485760 | tf_op jit(solution)/shard_map/pallas_call | solution.py:231
  865.3 0.9 collective-permute-start.2
  866.2 1.3 dynamic_slice.21
  867.6 1.4 dynamic_slice.22
  868.9 0.6 dynamic-slice_bitcast_fusion.1.fact_ref
  869.5 12.4 %shard_map.58 = (f32[1024,7168]{1,0:T(8,128)}, f32[1024,256]{1,0:T(8,128)}) custom-call(s32[1]{0:T(128)} %bitcast.pos_ref, f32[2048,3584]{1,0:T(8,128)} %get-tuple-element.56.theta_ref, bf16[2048,2048]{1,0:T(8,128)(2,1)} %get-tuple-element.59.kern_ref, f32[2048,1]{1,0:T(8,128)} %get-tuple-element.60.mass_ref, ...), custom_call_target="tpu_custom_call", output_to_operand_aliasing={{0}: (8, {})} | custom-call | flops 4294967296 | bytes 5242880 | tf_op jit(solution)/shard_map/pallas_call | solution.py:231
  881.9 9.8 shard_map.59
  891.7 1.1 collective-permute-start.1
  892.8 13.8 %own_shared.1.base_ref = f32[1024,7168]{1,0:T(8,128)} custom-call(s32[1]{0:T(128)} %bitcast.pos_ref, f32[2048,512]{1,0:T(8,128)} %get-tuple-element.77.theta_ref, bf16[2048,2048]{1,0:T(8,128)(2,1)} %get-tuple-element.59.kern_ref, f32[2048,1]{1,0:T(8,128)} %get-tuple-element.60.mass_ref, ...), custom_call_target="tpu_custom_call", output_to_operand_aliasing={{}: (8, {})} | custom-call | flops 4294967296 | bytes 10485760 | tf_op jit(solution)/shard_map/own_shared/pallas_call | solution.py:267
  906.6 0.9 collective-permute-start
  907.5 13.9 %own_foreign.1.base_ref = f32[1024,7168]{1,0:T(8,128)} custom-call(s32[1]{0:T(128)} %bitcast.pos_ref, f32[2048,512]{1,0:T(8,128)} %collective-permute-done.8.theta_ref, bf16[2048,2048]{1,0:T(8,128)(2,1)} %get-tuple-element.59.kern_ref, f32[2048,1]{1,0:T(8,128)} %get-tuple-element.60.mass_ref, ...), custom_call_target="tpu_custom_call", output_to_operand_aliasing={{}: (8, {})} | custom-call | flops 4294967296 | bytes 10485760 | tf_op jit(solution)/shard_map/own_foreign/pallas_call | solution.py:267
  921.4 1.9 shard_map.60.base_ref
  923.2 3.8 shard_map.61.base_ref
  927.0 3.8 shard_map.62.base_ref
  930.8 3.8 shard_map.63.base_ref
  934.6 36.8 %collective-permute-done.3.recv_ref = f32[1024,512]{1,0:T(8,128)} collective-permute-done((f32[1024,512]{1,0:T(8,128)}, f32[1024,512]{1,0:T(8,128)}, u32[]{:S(2)}, u32[]{:S(2)}) %collective-permute-start.3) | collective-permute-done | bytes 2097184 | tf_op jit(solution)/shard_map/ppermute | solution.py:610
  971.4 3.8 shard_map.64.base_ref
  975.2 41.2 %collective-permute-done.2.recv_ref = f32[1024,512]{1,0:T(8,128)} collective-permute-done((f32[1024,512]{1,0:T(8,128)}, f32[1024,512]{1,0:T(8,128)}, u32[]{:S(2)}, u32[]{:S(2)}) %collective-permute-start.2) | collective-permute-done | bytes 2097184 | tf_op jit(solution)/shard_map/ppermute | solution.py:610
  1016.4 3.8 shard_map.65.base_ref
  1020.1 18.7 %collective-permute-done.1.recv_ref = f32[1024,256]{1,0:T(8,128)} collective-permute-done((f32[1024,256]{1,0:T(8,128)}, f32[1024,256]{1,0:T(8,128)}, u32[]{:S(2)}, u32[]{:S(2)}) %collective-permute-start.1) | collective-permute-done | bytes 1048608 | tf_op jit(solution)/shard_map/ppermute | solution.py:610
  1038.8 2.1 shard_map.66.base_ref
  1040.9 8.7 collective-permute-done.recv_ref
  1049.6 0.8 copy-done.3
  1050.4 1.9 shard_map.67
  (11 shorter events, 0.0 us)
Async XLA Ops:
  0.0 1.0 copy-start
  594.8 311.8 %collective-permute-start.8 = (f32[2048,512]{1,0:T(8,128)}, f32[2048,512]{1,0:T(8,128)}, u32[]{:S(2)}, u32[]{:S(2)}) collective-permute-start(f32[2048,512]{1,0:T(8,128)} %get-tuple-element.77.theta_ref), channel_id=1, source_target_pairs={{0,4},{4,0},{1,5},{5,1},{2,6},{6,2},{3,7},{7,3}} | collective-permute-start | bytes 12582920 | tf_op jit(solution)/shard_map/ppermute | solution.py:603
  768.0 77.8 %collective-permute-start.7 = (f32[1024,128]{1,0:T(8,128)}, f32[1024,128]{1,0:T(8,128)S(1)}, u32[]{:S(2)}, u32[]{:S(2)}) collective-permute-start(f32[1024,128]{1,0:T(8,128)} %get-tuple-element.76), channel_id=1, source_target_pairs={{0,4},{4,0},{1,5},{5,1},{2,6},{6,2},{3,7},{7,3}} | collective-permute-start | bytes 1572872 | tf_op jit(solution)/shard_map/ppermute | solution.py:610
  787.8 77.5 %collective-permute-start.6 = (f32[1024,512]{1,0:T(8,128)}, f32[1024,512]{1,0:T(8,128)}, u32[]{:S(2)}, u32[]{:S(2)}) collective-permute-start(f32[1024,512]{1,0:T(8,128)} %get-tuple-element.75), channel_id=1, source_target_pairs={{0,4},{4,0},{1,5},{5,1},{2,6},{6,2},{3,7},{7,3}} | collective-permute-start | bytes 6291464 | tf_op jit(solution)/shard_map/ppermute | solution.py:610
  807.0 84.6 %collective-permute-start.5 = (f32[1024,512]{1,0:T(8,128)}, f32[1024,512]{1,0:T(8,128)}, u32[]{:S(2)}, u32[]{:S(2)}) collective-permute-start(f32[1024,512]{1,0:T(8,128)} %get-tuple-element.74), channel_id=1, source_target_pairs={{0,4},{4,0},{1,5},{5,1},{2,6},{6,2},{3,7},{7,3}} | collective-permute-start | bytes 6291464 | tf_op jit(solution)/shard_map/ppermute | solution.py:610
  826.6 104.2 %collective-permute-start.4 = (f32[1024,512]{1,0:T(8,128)}, f32[1024,512]{1,0:T(8,128)}, u32[]{:S(2)}, u32[]{:S(2)}) collective-permute-start(f32[1024,512]{1,0:T(8,128)} %get-tuple-element.73), channel_id=1, source_target_pairs={{0,4},{4,0},{1,5},{5,1},{2,6},{6,2},{3,7},{7,3}} | collective-permute-start | bytes 6291464 | tf_op jit(solution)/shard_map/ppermute | solution.py:610
  845.8 19.5 %copy-start.2 = (f32[1024,128]{1,0:T(8,128)}, f32[1024,128]{1,0:T(8,128)S(1)}, u32[]{:S(2)}) copy-start(f32[1024,128]{1,0:T(8,128)S(1)} %collective-permute-done.7.recv_ref) | copy-start | bytes 1572868
  845.8 125.6 %collective-permute-start.3 = (f32[1024,512]{1,0:T(8,128)}, f32[1024,512]{1,0:T(8,128)}, u32[]{:S(2)}, u32[]{:S(2)}) collective-permute-start(f32[1024,512]{1,0:T(8,128)} %get-tuple-element.72), channel_id=1, source_target_pairs={{0,4},{4,0},{1,5},{5,1},{2,6},{6,2},{3,7},{7,3}} | collective-permute-start | bytes 6291464 | tf_op jit(solution)/shard_map/ppermute | solution.py:610
  865.3 151.0 %collective-permute-start.2 = (f32[1024,512]{1,0:T(8,128)}, f32[1024,512]{1,0:T(8,128)}, u32[]{:S(2)}, u32[]{:S(2)}) collective-permute-start(f32[1024,512]{1,0:T(8,128)} %get-tuple-element.71), channel_id=1, source_target_pairs={{0,4},{4,0},{1,5},{5,1},{2,6},{6,2},{3,7},{7,3}} | collective-permute-start | bytes 6291464 | tf_op jit(solution)/shard_map/ppermute | solution.py:610
  891.7 147.2 %collective-permute-start.1 = (f32[1024,256]{1,0:T(8,128)}, f32[1024,256]{1,0:T(8,128)}, u32[]{:S(2)}, u32[]{:S(2)}) collective-permute-start(f32[1024,256]{1,0:T(8,128)} %get-tuple-element.70), channel_id=1, source_target_pairs={{0,4},{4,0},{1,5},{5,1},{2,6},{6,2},{3,7},{7,3}} | collective-permute-start | bytes 3145736 | tf_op jit(solution)/shard_map/ppermute | solution.py:610
  906.6 143.0 %collective-permute-start = (f32[1024,128]{1,0:T(8,128)}, f32[1024,128]{1,0:T(8,128)S(1)}, u32[]{:S(2)}, u32[]{:S(2)}) collective-permute-start(f32[1024,128]{1,0:T(8,128)} %get-tuple-element.69), channel_id=1, source_target_pairs={{0,4},{4,0},{1,5},{5,1},{2,6},{6,2},{3,7},{7,3}} | collective-permute-start | bytes 1572872 | tf_op jit(solution)/shard_map/ppermute | solution.py:610
  1038.8 13.5 %copy-start.1 = (bf16[7168,32]{0,1:T(8,128)(2,1)S(1)}, bf16[7168,32]{0,1:T(8,128)(2,1)}, u32[]{:S(2)}) copy-start(bf16[7168,32]{0,1:T(8,128)(2,1)} %param.7) | copy-start | bytes 1376260
  1049.6 0.8 copy-start.3

commit v2 on v1

--- a/solution.py
+++ b/solution.py
@@ -29,15 +29,14 @@
     return (0, k * BLK, top), (1, k * BLK - HALF, low)
 
 
-def exchange_kernel(n_chunk, theta_ref, mean_ref, fact_ref, col_ref, gram_ref, proj_ref,
-                    buf, tb, send_sem, recv_sem, own_sem, put_sem, other_sem):
+def exchange_kernel(n_early, n_late, theta_ref, mean_ref, fact_ref, col_ref, gram_ref, proj_ref,
+                    buf, tb, away, away_b, late_b, send_sem, recv_sem, lsend_sem, lrecv_sem, own_sem, put_sem, other_sem):
     part = lax.axis_index("part")
     other = 1 - part
-    feat = lax.axis_index("feat")
-    peer = (lax.axis_index("ens"), other, feat)
+    peer = (lax.axis_index("ens"), other, lax.axis_index("feat"))
     rows, width = theta_ref.shape[0], col_ref.shape[1]
     n_rows = col_ref.shape[0]
-    cw = width // n_chunk
+    cw = width // (n_early + n_late)
     n_blk = n_rows // BLK
     barrier = pltpu.get_barrier_semaphore()
     pl.semaphore_signal(barrier, inc=1, device_id=peer, device_id_type=MESH)
@@ -45,51 +44,34 @@
     own_rows = pl.ds(pl.multiple_of(part * rows, BLK), rows)
     other_rows = pl.ds(pl.multiple_of(other * rows, BLK), rows)
 
+    def chunk(half, c):
+        return pl.ds(pl.multiple_of(half * width + c * cw, 128), cw)
+
     def remote(c):
         return pltpu.make_async_remote_copy(
-            src_ref=theta_ref.at[:, pl.ds(pl.multiple_of(other * width + c * cw, 128), cw)],
-            dst_ref=col_ref.at[own_rows, pl.ds(pl.multiple_of(c * cw, 128), cw)],
+            src_ref=theta_ref.at[:, chunk(other, c)], dst_ref=col_ref.at[own_rows, chunk(0, c)],
             send_sem=send_sem.at[c], recv_sem=recv_sem.at[c], device_id=peer, device_id_type=MESH)
 
+    def remote_late(c):
+        return pltpu.make_async_remote_copy(
+            src_ref=away_b.at[c], dst_ref=late_b.at[c],
+            send_sem=lsend_sem.at[c], recv_sem=lrecv_sem.at[c], device_id=peer, device_id_type=MESH)
+
     def fetch_own(c):
-        return pltpu.make_async_copy(
-            theta_ref.at[:, pl.ds(pl.multiple_of(part * width + c * cw, 128), cw)],
-            buf.at[own_rows, :], own_sem)
+        return pltpu.make_async_copy(theta_ref.at[:, chunk(part, c)], buf.at[own_rows, :], own_sem)
 
     def put_own(c):
-        return pltpu.make_async_copy(
-            buf.at[own_rows, :], col_ref.at[own_rows, pl.ds(pl.multiple_of(c * cw, 128), cw)], put_sem)
+        return pltpu.make_async_copy(buf.at[own_rows, :], col_ref.at[own_rows, chunk(0, c)], put_sem)
 
     def fetch_other(c):
-        return pltpu.make_async_copy(
-            col_ref.at[other_rows, pl.ds(pl.multiple_of(c * cw, 128), cw)], buf.at[other_rows, :], other_sem)
-
-    @pl.loop(0, n_chunk)
-    def _(c):
-        remote(c).start()
-
-    gram_ref[...] = jnp.zeros_like(gram_ref)
-    proj_ref[...] = jnp.zeros_like(proj_ref)
-
-    @pl.loop(0, n_chunk)
-    def _(c):
-        fetch_own(c).start()
-        fetch_own(c).wait()
-        put_own(c).start()
-        remote(c).wait_recv()
-        fetch_other(c).start()
-        fetch_other(c).wait()
-        cols = pl.ds(pl.multiple_of(c * cw, 128), cw)
-        fact = fact_ref[:, cols]
-        mean = mean_ref[:, cols]
-
-        @pl.loop(0, n_blk)
-        def _(b):
-            rs = pl.ds(pl.multiple_of(b * BLK, BLK), BLK)
-            th = buf[rs, :]
-            tb[rs, :] = th.astype(BF16)
-            proj_ref[:, rs] += lax.dot_general(fact, (th - mean).astype(BF16), NT, preferred_element_type=F32)
-
+        return pltpu.make_async_copy(col_ref.at[other_rows, chunk(0, c)], buf.at[other_rows, :], other_sem)
+
+    def project(src, row0, half, c, dst_row0):
+        x = src[pl.ds(pl.multiple_of(row0, BLK), BLK), :] - mean_ref[:, chunk(half, c)]
+        proj_ref[:, pl.ds(pl.multiple_of(dst_row0, BLK), BLK)] += lax.dot_general(
+            fact_ref[:, chunk(half, c)], x.astype(BF16), NT, preferred_element_type=F32)
+
+    def add_gram():
         for b in range(n_blk):
             rows_b = tb[b * BLK:(b + 1) * BLK, :]
             for k in range(REACH):
@@ -97,32 +79,98 @@
                 val = lax.dot_general(rows_b, tb[j * BLK:(j + 1) * BLK, :], NT, preferred_element_type=F32)
                 for h, col, piece in band_parts(k, val):
                     gram_ref[b, h, :, col:col + piece.shape[1]] += piece
+
+    @pl.loop(0, n_early)
+    def _(c):
+        remote(c).start()
+
+    gram_ref[...] = jnp.zeros_like(gram_ref)
+    proj_ref[...] = jnp.zeros_like(proj_ref)
+
+    @pl.loop(0, n_late)
+    def _(c):
+        fetch = pltpu.make_async_copy(theta_ref.at[:, chunk(other, n_early + c)], away, other_sem)
+        fetch.start()
+        fetch.wait()
+
+        @pl.loop(0, rows // BLK)
+        def _(b):
+            rs = pl.ds(pl.multiple_of(b * BLK, BLK), BLK)
+            away_b[c, rs, :] = away[rs, :].astype(BF16)
+            project(away, b * BLK, other, n_early + c, part * rows + b * BLK)
+
+    @pl.loop(0, n_late)
+    def _(c):
+        remote_late(c).start()
+
+    @pl.loop(0, n_early + n_late)
+    def _(c):
+        fetch_own(c).start()
+        fetch_own(c).wait()
+        put_own(c).start()
+
+        @pl.loop(0, rows // BLK)
+        def _(b):
+            row0 = part * rows + b * BLK
+            rs = pl.ds(pl.multiple_of(row0, BLK), BLK)
+            tb[rs, :] = buf[rs, :].astype(BF16)
+            project(buf, row0, part, c, row0)
+
+        @pl.when(c < n_early)
+        def _():
+            remote(c).wait_recv()
+            fetch_other(c).start()
+            fetch_other(c).wait()
+
+            @pl.loop(0, rows // BLK)
+            def _(b):
+                row0 = other * rows + b * BLK
+                rs = pl.ds(pl.multiple_of(row0, BLK), BLK)
+                tb[rs, :] = buf[rs, :].astype(BF16)
+                project(buf, row0, part, c, row0)
+
+        @pl.when(c >= n_early)
+        def _():
+            remote_late(c - n_early).wait_recv()
+            tb[other_rows, :] = late_b[c - n_early]
+
+        add_gram()
         put_own(c).wait()
 
-    @pl.loop(0, n_chunk)
+    @pl.loop(0, n_early)
     def _(c):
         remote(c).wait_send()
 
-
-def exchange(theta, mean, fact_t, n_chunk):
+    @pl.loop(0, n_late)
+    def _(c):
+        remote_late(c).wait_send()
+
+
+def exchange(theta, mean, fact_t, n_early, n_late):
     rows, feat = theta.shape
     width = feat // 2
     n_rows = rows * 2
-    rank = fact_t.shape[0]
+    cw = width // (n_early + n_late)
+    dma = lambda *n: pltpu.SemaphoreType.DMA(n)
     return pl.pallas_call(
-        functools.partial(exchange_kernel, n_chunk),
+        functools.partial(exchange_kernel, n_early, n_late),
         out_shape=(jax.ShapeDtypeStruct((n_rows, width), F32),
                    jax.ShapeDtypeStruct((n_rows // BLK, 2, HALF, WIDE), F32),
-                   jax.ShapeDtypeStruct((rank, n_rows), F32)),
+                   jax.ShapeDtypeStruct((fact_t.shape[0], n_rows), F32)),
         in_specs=[ANY, VMEM, VMEM], out_specs=(ANY, VMEM, VMEM),
         scratch_shapes=[
-            pltpu.VMEM((n_rows, width // n_chunk), F32),
-            pltpu.VMEM((n_rows, width // n_chunk), BF16),
-            pltpu.SemaphoreType.DMA((n_chunk,)), pltpu.SemaphoreType.DMA((n_chunk,)),
+            pltpu.VMEM((n_rows, cw), F32), pltpu.VMEM((n_rows, cw), BF16), pltpu.VMEM((rows, cw), F32),
+            pltpu.VMEM((n_late, rows, cw), BF16), pltpu.VMEM((n_late, rows, cw), BF16),
+            dma(n_early), dma(n_early), dma(n_late), dma(n_late),
             pltpu.SemaphoreType.DMA, pltpu.SemaphoreType.DMA, pltpu.SemaphoreType.DMA],
         compiler_params=pltpu.CompilerParams(collective_id=0, has_side_effects=True, vmem_limit_bytes=VMEM_LIMIT),
         name="exchange",
     )(theta, mean, fact_t)
+
+
+def columns(half, start, tile, refs):
+    cols = pl.ds(pl.multiple_of(half * (refs[0].shape[1] // 2) + start, 128), tile)
+    return tuple(ref[:, cols] for ref in refs)
 
 
 def build_rhs(theta_ref, mean, prec, fact, zb_ref, rhs, rs):
@@ -140,31 +188,40 @@
     return th + step_size * ((acc[:, :tile] + two_over_h * pull) * inv_n)
 
 
-def update_kernel(consts, theta_ref, next_ref, kern_ref, mass_ref, zb_ref, mean_ref, prec_ref, fact_ref,
-                  mean_n, prec_n, fact_n, *rest):
-    out_ref, tb_ref, proj_ref, rhs = rest[-4:]
-    n_rows = theta_ref.shape[0]
+def update_kernel(consts, first, theta_ref, next_ref, kern_hbm, mass_ref, zb_ref, mean_ref, prec_ref, fact_ref, *rest):
+    out_ref, tb_ref, proj_ref, rhs, kern_ref, kern_sem = rest[-6:]
+    n_rows, tile = theta_ref.shape
     big = n_rows // 2
-    slot = lax.rem(pl.program_id(0), 2)
-
-    @pl.when(pl.program_id(0) == 0)
+    i = pl.program_id(0)
+    slot = lax.rem(i, 2)
+    part = lax.axis_index("part")
+    refs = (mean_ref, prec_ref, fact_ref)
+
+    @pl.when(i == 0)
     def _():
-        proj_ref[...] = rest[0][...] if len(rest) > 4 else jnp.zeros_like(proj_ref)
+        kern_copy = pltpu.make_async_copy(kern_hbm, kern_ref, kern_sem)
+        kern_copy.start()
+        proj_ref[...] = rest[0][...] if len(rest) > 6 else jnp.zeros_like(proj_ref)
+        now = columns(part, first * tile, tile, refs)
 
         @pl.loop(0, n_rows // BLK)
         def _(b):
-            build_rhs(theta_ref, mean_ref[...], prec_ref[...], fact_ref[...], zb_ref, rhs.at[0],
-                      pl.ds(pl.multiple_of(b * BLK, BLK), BLK))
+            build_rhs(theta_ref, *now, zb_ref, rhs.at[0], pl.ds(pl.multiple_of(b * BLK, BLK), BLK))
+
+        kern_copy.wait()
+
+    mean, _, fact = columns(part, (first + i) * tile, tile, refs)
+    after = columns(part, (first + jnp.minimum(i + 1, pl.num_programs(0) - 1)) * tile, tile, refs)
 
     @pl.loop(0, 2)
     def _(b):
         rs = pl.ds(pl.multiple_of(b * big, big), big)
         acc = jnp.dot(kern_ref[rs, :], rhs[slot], preferred_element_type=F32)
-        build_rhs(next_ref, mean_n[...], prec_n[...], fact_n[...], zb_ref, rhs.at[1 - slot], rs)
+        build_rhs(next_ref, *after, zb_ref, rhs.at[1 - slot], rs)
         new = stepped(theta_ref, acc, mass_ref, rs, *consts)
         out_ref[rs, :] = new
         tb_ref[rs, :] = new.astype(BF16)
-        proj_ref[:, rs] += lax.dot_general(fact_ref[...], (new - mean_ref[...]).astype(BF16), NT, preferred_element_type=F32)
+        proj_ref[:, rs] += lax.dot_general(fact, (new - mean).astype(BF16), NT, preferred_element_type=F32)
 
 
 def update(consts, theta, kern, mass, zb, mean, prec, fact_t, tile, start, stop, own_out, before=None):
@@ -173,39 +230,46 @@
     first, steps = start // tile, (stop - start) // tile
     col = lambda r: pl.BlockSpec((r, tile), lambda i: (0, first + i))
     nxt = lambda r: pl.BlockSpec((r, tile), lambda i: (0, first + jnp.minimum(i + 1, steps - 1)))
-    in_specs = [col(n_rows), nxt(n_rows), VMEM, VMEM, VMEM, col(1), col(1), col(rank), nxt(1), nxt(1), nxt(rank)]
-    args = [theta, theta, kern, mass, zb, mean, prec, fact_t, mean, prec, fact_t]
+    in_specs = [col(n_rows), nxt(n_rows), ANY, VMEM, VMEM, VMEM, VMEM, VMEM]
+    args = [theta, theta, kern, mass, zb, mean, prec, fact_t]
     alias = {}
     if before is not None:
         in_specs += [VMEM, ANY]
         args += [before[1], before[0]]
-        alias = {12: 1}
+        alias = {9: 1}
+        if len(before) > 2:
+            in_specs.append(ANY)
+            args.append(before[2])
+            alias[10] = 0
     return pl.pallas_call(
-        functools.partial(update_kernel, consts),
+        functools.partial(update_kernel, consts, first),
         grid=(steps,),
         out_shape=(jax.ShapeDtypeStruct((n_rows, stop - start if own_out else width), F32),
                    jax.ShapeDtypeStruct((n_rows, width), BF16),
                    jax.ShapeDtypeStruct((rank, n_rows), F32)),
         in_specs=in_specs,
         out_specs=(pl.BlockSpec((n_rows, tile), lambda i: (0, i)) if own_out else col(n_rows), col(n_rows), VMEM),
-        scratch_shapes=[pltpu.VMEM((2, n_rows, 2 * tile), BF16)],
+        scratch_shapes=[pltpu.VMEM((2, n_rows, 2 * tile), BF16), pltpu.VMEM(kern.shape, BF16), pltpu.SemaphoreType.DMA],
         input_output_aliases=alias,
         compiler_params=pltpu.CompilerParams(vmem_limit_bytes=VMEM_LIMIT),
         cost_estimate=pl.CostEstimate(flops=4 * n_rows * n_rows * (stop - start), bytes_accessed=10 * n_rows * (stop - start), transcendentals=0),
     )(*args)
 
 
-def last_kernel(consts, pos_ref, theta_ref, kern_ref, mass_ref, zb_ref, mean_ref, prec_ref, fact_ref, *rest):
-    out_ref, send_ref, rhs = rest[-3:]
+def last_kernel(consts, start, pos_ref, theta_ref, kern_hbm, mass_ref, zb_ref, mean_ref, prec_ref, fact_ref, *rest):
+    out_ref, send_ref, rhs, kern_ref, kern_sem = rest[-5:]
+    kern_copy = pltpu.make_async_copy(kern_hbm, kern_ref, kern_sem)
+    kern_copy.start()
     rows = out_ref.shape[0]
     n_blk = theta_ref.shape[0] // BLK
     part = pos_ref[0]
-    fact, mean, prec = fact_ref[...], mean_ref[...], prec_ref[...]
+    now = columns(part, start, theta_ref.shape[1], (mean_ref, prec_ref, fact_ref))
 
     @pl.loop(0, n_blk)
     def _(b):
-        build_rhs(theta_ref, mean, prec, fact, zb_ref, rhs, pl.ds(pl.multiple_of(b * BLK, BLK), BLK))
-
+        build_rhs(theta_ref, *now, zb_ref, rhs, pl.ds(pl.multiple_of(b * BLK, BLK), BLK))
+
+    kern_copy.wait()
     for dst, which in ((send_ref, 1 - part), (out_ref, part)):
         @pl.loop(0, rows // BLK)
         def _(b):
@@ -217,11 +281,10 @@
 def last_update(consts, pos, theta, kern, mass, zb, mean, prec, fact_t, out, start, tile):
     n_rows, width = theta.shape
     chunk = start // tile
-    rank = fact_t.shape[0]
     rows, feat = n_rows // 2, width * 2
     per = width // tile
     col = lambda r: pl.BlockSpec((r, tile), lambda i, pos: (0, chunk))
-    in_specs = [col(n_rows), VMEM, VMEM, VMEM, col(1), col(1), col(rank)]
+    in_specs = [col(n_rows), ANY, VMEM, VMEM, VMEM, VMEM, VMEM]
     args = [theta, kern, mass, zb, mean, prec, fact_t]
     alias = {}
     if out is not None:
@@ -229,12 +292,12 @@
         args.append(out)
         alias = {8: 0}
     return pl.pallas_call(
-        functools.partial(last_kernel, consts),
+        functools.partial(last_kernel, consts, start),
         grid_spec=pltpu.PrefetchScalarGridSpec(
             num_scalar_prefetch=1, grid=(1,), in_specs=in_specs,
             out_specs=(pl.BlockSpec((rows, tile), lambda i, pos: (0, pos[0] * per + chunk)),
                        pl.BlockSpec((rows, tile), lambda i, pos: (0, 0))),
-            scratch_shapes=[pltpu.VMEM((n_rows, 2 * tile), BF16)]),
+            scratch_shapes=[pltpu.VMEM((n_rows, 2 * tile), BF16), pltpu.VMEM(kern.shape, BF16), pltpu.SemaphoreType.DMA]),
         out_shape=(jax.ShapeDtypeStruct((rows, feat), F32), jax.ShapeDtypeStruct((rows, tile), F32)),
         input_output_aliases=alias,
         compiler_params=pltpu.CompilerParams(vmem_limit_bytes=VMEM_LIMIT),
@@ -242,13 +305,14 @@
     )(pos, *args)
 
 
-def own_kernel(consts, pos_ref, theta_ref, kern_ref, mass_ref, zb_ref, mean_ref, prec_ref, fact_ref, base_ref, out_ref, rhs):
+def own_kernel(consts, foreign, pos_ref, theta_ref, kern_ref, mass_ref, zb_ref, mean_ref, prec_ref, fact_ref, base_ref, out_ref, rhs):
     rows = out_ref.shape[0]
-    fact, mean, prec = fact_ref[...], mean_ref[...], prec_ref[...]
+    half = 1 - pos_ref[0] if foreign else pos_ref[0]
+    now = columns(half, pl.program_id(0) * BLK, BLK, (mean_ref, prec_ref, fact_ref))
 
     @pl.loop(0, theta_ref.shape[0] // BLK)
     def _(b):
-        build_rhs(theta_ref, mean, prec, fact, zb_ref, rhs, pl.ds(pl.multiple_of(b * BLK, BLK), BLK))
+        build_rhs(theta_ref, *now, zb_ref, rhs, pl.ds(pl.multiple_of(b * BLK, BLK), BLK))
 
     @pl.loop(0, rows // BLK)
     def _(b):
@@ -259,16 +323,15 @@
 
 def own_update(consts, pos, theta, kern, mass, zb, mean, prec, fact_t, out, foreign):
     n_rows, cols = theta.shape
-    rank = fact_t.shape[0]
     rows, feat = out.shape
     per = feat // (2 * BLK)
     col = lambda r: pl.BlockSpec((r, BLK), lambda i, pos: (0, i))
     where = (lambda i, pos: (0, (1 - pos[0]) * per + i)) if foreign else (lambda i, pos: (0, pos[0] * per + i))
     return pl.pallas_call(
-        functools.partial(own_kernel, consts),
+        functools.partial(own_kernel, consts, foreign),
         grid_spec=pltpu.PrefetchScalarGridSpec(
             num_scalar_prefetch=1, grid=(cols // BLK,),
-            in_specs=[col(n_rows), VMEM, VMEM, VMEM, col(1), col(1), col(rank), ANY],
+            in_specs=[col(n_rows), VMEM, VMEM, VMEM, VMEM, VMEM, VMEM, ANY],
             out_specs=pl.BlockSpec((rows, BLK), where),
             scratch_shapes=[pltpu.VMEM((n_rows, 2 * BLK), BF16)]),
         out_shape=jax.ShapeDtypeStruct(out.shape, F32),
@@ -297,6 +360,19 @@
         input_output_aliases={2: 0},
         cost_estimate=pl.CostEstimate(flops=1000 * rows * tile, bytes_accessed=8 * rows * tile, transcendentals=0),
     )(pos, recv, out)
+
+
+def place_rows(pos, recv, cur, start):
+    rows, cols = recv.shape
+    return pl.pallas_call(
+        place_kernel,
+        grid_spec=pltpu.PrefetchScalarGridSpec(
+            num_scalar_prefetch=1, grid=(cols // BLK,), in_specs=[pl.BlockSpec((rows, BLK), lambda i, pos: (0, i)), ANY],
+            out_specs=pl.BlockSpec((rows, BLK), lambda i, pos: (1 - pos[0], start // BLK + i))),
+        out_shape=jax.ShapeDtypeStruct(cur.shape, cur.dtype),
+        input_output_aliases={2: 0},
+        name="place_rows",
+    )(pos, recv, cur)
 
 
 def kmat_kernel(from_gram, two_over_h, src_ref, proj_ref, kern_ref, zb_ref, mass_ref, *scratch):
@@ -584,20 +660,21 @@
         consts = (1.0 / n_total, 2.0 / kern_width, step_size)
         part = lax.axis_index("part")
         pos = part.astype(jnp.int32).reshape(1)
-        mean = lax.dynamic_slice_in_dim(mean_loc, part * width, width).reshape(1, width)
-        prec = lax.dynamic_slice_in_dim(prec_loc, part * width, width).reshape(1, width)
-        fact_t = lax.dynamic_slice_in_dim(factor_loc, part * width, width, axis=0).T
+        params = (mean_loc.reshape(1, feat_loc), prec_loc.reshape(1, feat_loc), factor_loc.T)
         shared = 2 * BLK
         chunks = [(shared, HALF)] + [(at, 2 * BLK) for at in range(2 * shared, width, 2 * BLK)] + [(shared + BLK, BLK), (shared + HALF, HALF)]
         swap = [(0, 1), (1, 0)]
-        mean_f = lax.dynamic_slice_in_dim(mean_loc, (1 - part) * width, shared).reshape(1, shared)
-        prec_f = lax.dynamic_slice_in_dim(prec_loc, (1 - part) * width, shared).reshape(1, shared)
-        fact_f = lax.dynamic_slice_in_dim(factor_loc, (1 - part) * width, shared, axis=0).T
-
-        cur, gram, proj = exchange(theta, mean, fact_t, 7)
-        params = (mean, prec, fact_t)
+        late = 3 * BLK
+        early = width - late
+        late_rows = lax.dynamic_slice_in_dim(theta, (1 - part) * width + early, late, axis=1)
+
+        cur, gram, proj = exchange(theta, params[0], params[2], early // BLK, late // BLK)
         kern, zb, mass = kernel_matrix(gram, proj, consts[1], 1, True)
-        cur, tb, proj = update(consts, cur, kern, mass, zb, *params, BLK, 0, width, False)
+        late_rows, mass = lax.optimization_barrier((late_rows, mass))
+        recv = lax.ppermute(late_rows, "part", swap)
+        new, tb, proj = update(consts, cur, kern, mass, zb, *params, BLK, 0, early, False)
+        cur = place_rows(pos, recv, cur, early)
+        cur, tb, proj = update(consts, cur, kern, mass, zb, *params, BLK, early, width, False, (tb, proj, new))
         kern, zb, mass = kernel_matrix(tb, proj, consts[1], 2, False)
         both, tb, proj = update(consts, cur, kern, mass, zb, *params, BLK, 0, shared, True)
         foreign = lax.ppermute(both, "part", swap)
@@ -609,7 +686,7 @@
             out, send = last_update(consts, pos, cur, kern, mass, zb, *params, out, start, tile)
             received.append(lax.ppermute(send, "part", swap))
         out = own_update(consts, pos, both, kern, mass, zb, *params, out, False)
-        out = own_update(consts, pos, foreign, kern, mass, zb, mean_f, prec_f, fact_f, out, True)
+        out = own_update(consts, pos, foreign, kern, mass, zb, *params, out, True)
         for (start, tile), recv in zip(chunks, received):
             out = place(pos, recv, out, start)
         return out

time: 1060 us -> 1060 us (level)
  Pallas kernels: 929 us -> 899 us
  waiting for transfers between devices: 105 us -> 132 us
    pallas_call x14 -> x16, Pallas kernels: 656 us -> 628 us  [the longest x1 292 us: exchange(): pl.pallas_call(functools.partial(exchange_kernel, n_early, n_late), out_s...]
    ppermute x8, waiting for transfers between devices: 105 us -> 129 us  [local_steps(): received.append(lax.ppermute(send, 'part', swap))]
  transfers between devices with their start and end apart: 9 -> 10, of which waited for: 4 -> 6; matrix products, arithmetic and copies ran while one was open for 0% -> 0% of each run, Pallas kernels for 32% -> 38%
where the time goes in v2:
time: 1060 us; the launch traced here: 1050 us
  Pallas kernels  899 us (85%)
  waiting for transfers between devices  132 us (12%)
    pallas_call x1, Pallas kernels, exchange(): pl.pallas_call(functools.partial(exchange_kernel, n_early, n_late), out_s...  292 us
    pallas_call x3, Pallas kernels, kernel_matrix(): pl.pallas_call(functools.partial(kmat_kernel, from_gram, two_over_h), out...  247 us
    pallas_call x4, Pallas kernels, update(): pl.pallas_call(functools.partial(update_kernel, consts, first), grid=(ste...  183 us
    ppermute x8, waiting for transfers between devices, local_steps(): received.append(lax.ppermute(send, 'part', swap))  129 us
    pallas_call x8, Pallas kernels, last_update(): pl.pallas_call(functools.partial(last_kernel, consts, start), grid_spec=p...  121 us
    pallas_call x2, Pallas kernels, own_update(): pl.pallas_call(functools.partial(own_kernel, consts, foreign), grid_spec=...  27.8 us
    pallas_call x8, Pallas kernels, place(): pl.pallas_call(place_kernel, grid_spec=pltpu.PrefetchScalarGridSpec(num_s...  24.7 us
  transfers between devices with their start and end apart: 10, of which 6 were waited for; matrix products, arithmetic and copies ran while one was open for 0% of the time, Pallas kernels for 38%

profile of v2, /device:TPU:0, one launch (start us, length us, event | category | flops | bytes accessed | tf_op | source)
XLA Modules:
  0.0 1046.1 jit_solution(4782764094037417303)
XLA Ops:
  0.0 3.8 constant_dynamic-slice_fusion
  3.8 291.8 %exchange.1 = (f32[2048,3584]{1,0:T(8,128)}, f32[8,2,128,1152]{3,2,1,0:T(8,128)}, f32[32,2048]{1,0:T(8,128)}) custom-call(f32[1024,7168]{1,0:T(8,128)} %theta_ref.1, f32[1,7168]{1,0:T(1,128)} %bitcast.19, bf16[32,7168]{1,0:T(8,128)(2,1)} %bitcast.4), custom_call_target="tpu_custom_call" | custom-call | tf_op jit(solution)/shard_map/exchange/pallas_call | solution.py:155
  295.6 75.2 %shard_map.46 = (bf16[2048,2048]{1,0:T(8,128)(2,1)}, bf16[2048,32]{1,0:T(8,128)(2,1)}, f32[2048,1]{1,0:T(8,128)}) custom-call(f32[8,2,128,1152]{3,2,1,0:T(8,128)} %get-tuple-element.47.src_ref, f32[32,2048]{1,0:T(8,128)} %get-tuple-element.48.proj_ref), custom_call_target="tpu_custom_call" | custom-call | tf_op jit(solution)/shard_map/pallas_call | solution.py:640
  370.7 0.9 collective-permute-start
  371.6 66.9 %shard_map.47 = (f32[2048,3584]{1,0:T(8,128)}, bf16[2048,3584]{1,0:T(8,128)(2,1)}, f32[32,2048]{1,0:T(8,128)}) custom-call(f32[2048,3584]{1,0:T(8,128)} %get-tuple-element.51.base_ref.theta_ref.next_ref, f32[2048,3584]{1,0:T(8,128)} %get-tuple-element.51.base_ref.theta_ref.next_ref, bf16[2048,2048]{1,0:T(8,128)(2,1)} %get-tuple-element.52.kern_hbm, ...), custom_call_target="tpu_custom_call" | custom-call | flops 47244640256 | bytes 57671680 | tf_op jit(solution)/shard_map/pallas_call | solution.py:244
  438.5 3.4 collective-permute-done.recv_ref
  441.9 4.4 place_rows.1.theta_ref.next_ref
  446.3 24.5 %shard_map.48 = (f32[2048,3584]{1,0:T(8,128)}, bf16[2048,3584]{1,0:T(8,128)(2,1)}, f32[32,2048]{1,0:T(8,128)}) custom-call(f32[2048,3584]{1,0:T(8,128)} %place_rows.1.theta_ref.next_ref, f32[2048,3584]{1,0:T(8,128)} %place_rows.1.theta_ref.next_ref, bf16[2048,2048]{1,0:T(8,128)(2,1)} %get-tuple-element.52.kern_hbm, ...), custom_call_target="tpu_custom_call", output_to_operand_aliasing={{1}: (9, {}), {0}: (10, {})} | custom-call | flops 12884901888 | bytes 15728640 | tf_op jit(solution)/shard_map/pallas_call | solution.py:244
  470.8 81.2 %shard_map.49 = (bf16[2048,2048]{1,0:T(8,128)(2,1)}, bf16[2048,32]{1,0:T(8,128)(2,1)}, f32[2048,1]{1,0:T(8,128)}) custom-call(bf16[2048,3584]{1,0:T(8,128)(2,1)} %get-tuple-element.59.src_ref, f32[32,2048]{1,0:T(8,128)} %get-tuple-element.60.proj_ref), custom_call_target="tpu_custom_call" | custom-call | tf_op jit(solution)/shard_map/pallas_call | solution.py:640
  552.1 18.8 %shard_map.50 = (f32[2048,512]{1,0:T(8,128)}, bf16[2048,3584]{1,0:T(8,128)(2,1)}, f32[32,2048]{1,0:T(8,128)}) custom-call(f32[2048,3584]{1,0:T(8,128)} %get-tuple-element.58.theta_ref.next_ref, f32[2048,3584]{1,0:T(8,128)} %get-tuple-element.58.theta_ref.next_ref, bf16[2048,2048]{1,0:T(8,128)(2,1)} %get-tuple-element.61.kern_hbm, ...), custom_call_target="tpu_custom_call" | custom-call | flops 8589934592 | bytes 10485760 | tf_op jit(solution)/shard_map/pallas_call | solution.py:244
  570.9 0.6 collective-permute-start.9
  571.5 72.8 %shard_map.51 = (f32[2048,3584]{1,0:T(8,128)}, bf16[2048,3584]{1,0:T(8,128)(2,1)}, f32[32,2048]{1,0:T(8,128)}) custom-call(f32[2048,3584]{1,0:T(8,128)} %get-tuple-element.58.theta_ref.next_ref, f32[2048,3584]{1,0:T(8,128)} %get-tuple-element.58.theta_ref.next_ref, bf16[2048,2048]{1,0:T(8,128)(2,1)} %get-tuple-element.61.kern_hbm, ...), custom_call_target="tpu_custom_call", output_to_operand_aliasing={{1}: (9, {})} | custom-call | flops 51539607552 | bytes 62914560 | tf_op jit(solution)/shard_map/pallas_call | solution.py:244
  644.3 90.2 %shard_map.52 = (bf16[2048,2048]{1,0:T(8,128)(2,1)}, bf16[2048,32]{1,0:T(8,128)(2,1)}, f32[2048,1]{1,0:T(8,128)}) custom-call(bf16[2048,3584]{1,0:T(8,128)(2,1)} %get-tuple-element.67.src_ref, f32[32,2048]{1,0:T(8,128)} %get-tuple-element.68.proj_ref), custom_call_target="tpu_custom_call" | custom-call | tf_op jit(solution)/shard_map/pallas_call | solution.py:640
  734.5 9.6 shard_map.53
  744.1 1.4 collective-permute-start.8
  745.5 18.0 %shard_map.54 = (f32[1024,7168]{1,0:T(8,128)}, f32[1024,512]{1,0:T(8,128)}) custom-call(s32[1]{0:T(128)} %bitcast.pos_ref, f32[2048,3584]{1,0:T(8,128)} %get-tuple-element.66.theta_ref, bf16[2048,2048]{1,0:T(8,128)(2,1)} %get-tuple-element.69.kern_hbm.kern_ref, f32[2048,1]{1,0:T(8,128)} %get-tuple-element.70.mass_ref, ...), custom_call_target="tpu_custom_call", output_to_operand_aliasing={{0}: (8, {})} | custom-call | flops 8589934592 | bytes 10485760 | tf_op jit(solution)/shard_map/pallas_call | solution.py:294
  763.6 17.9 %shard_map.55 = (f32[1024,7168]{1,0:T(8,128)}, f32[1024,512]{1,0:T(8,128)}) custom-call(s32[1]{0:T(128)} %bitcast.pos_ref, f32[2048,3584]{1,0:T(8,128)} %get-tuple-element.66.theta_ref, bf16[2048,2048]{1,0:T(8,128)(2,1)} %get-tuple-element.69.kern_hbm.kern_ref, f32[2048,1]{1,0:T(8,128)} %get-tuple-element.70.mass_ref, ...), custom_call_target="tpu_custom_call", output_to_operand_aliasing={{0}: (8, {})} | custom-call | flops 8589934592 | bytes 10485760 | tf_op jit(solution)/shard_map/pallas_call | solution.py:294
  781.5 0.7 collective-permute-start.6
  782.1 1.4 collective-permute-start.7
  783.5 17.9 %shard_map.56 = (f32[1024,7168]{1,0:T(8,128)}, f32[1024,512]{1,0:T(8,128)}) custom-call(s32[1]{0:T(128)} %bitcast.pos_ref, f32[2048,3584]{1,0:T(8,128)} %get-tuple-element.66.theta_ref, bf16[2048,2048]{1,0:T(8,128)(2,1)} %get-tuple-element.69.kern_hbm.kern_ref, f32[2048,1]{1,0:T(8,128)} %get-tuple-element.70.mass_ref, ...), custom_call_target="tpu_custom_call", output_to_operand_aliasing={{0}: (8, {})} | custom-call | flops 8589934592 | bytes 10485760 | tf_op jit(solution)/shard_map/pallas_call | solution.py:294
  801.4 17.9 %shard_map.57 = (f32[1024,7168]{1,0:T(8,128)}, f32[1024,512]{1,0:T(8,128)}) custom-call(s32[1]{0:T(128)} %bitcast.pos_ref, f32[2048,3584]{1,0:T(8,128)} %get-tuple-element.66.theta_ref, bf16[2048,2048]{1,0:T(8,128)(2,1)} %get-tuple-element.69.kern_hbm.kern_ref, f32[2048,1]{1,0:T(8,128)} %get-tuple-element.70.mass_ref, ...), custom_call_target="tpu_custom_call", output_to_operand_aliasing={{0}: (8, {})} | custom-call | flops 8589934592 | bytes 10485760 | tf_op jit(solution)/shard_map/pallas_call | solution.py:294
  819.3 0.7 collective-permute-start.4
  820.0 0.0 collective-permute-done.8.recv_ref
  820.0 1.4 collective-permute-start.5
  821.3 17.9 %shard_map.58 = (f32[1024,7168]{1,0:T(8,128)}, f32[1024,512]{1,0:T(8,128)}) custom-call(s32[1]{0:T(128)} %bitcast.pos_ref, f32[2048,3584]{1,0:T(8,128)} %get-tuple-element.66.theta_ref, bf16[2048,2048]{1,0:T(8,128)(2,1)} %get-tuple-element.69.kern_hbm.kern_ref, f32[2048,1]{1,0:T(8,128)} %get-tuple-element.70.mass_ref, ...), custom_call_target="tpu_custom_call", output_to_operand_aliasing={{0}: (8, {})} | custom-call | flops 8589934592 | bytes 10485760 | tf_op jit(solution)/shard_map/pallas_call | solution.py:294
  839.2 0.0 collective-permute-done.6.recv_ref
  839.3 0.7 collective-permute-start.3
  839.9 12.2 %shard_map.59 = (f32[1024,7168]{1,0:T(8,128)}, f32[1024,256]{1,0:T(8,128)}) custom-call(s32[1]{0:T(128)} %bitcast.pos_ref, f32[2048,3584]{1,0:T(8,128)} %get-tuple-element.66.theta_ref, bf16[2048,2048]{1,0:T(8,128)(2,1)} %get-tuple-element.69.kern_hbm.kern_ref, f32[2048,1]{1,0:T(8,128)} %get-tuple-element.70.mass_ref, ...), custom_call_target="tpu_custom_call", output_to_operand_aliasing={{0}: (8, {})} | custom-call | flops 4294967296 | bytes 5242880 | tf_op jit(solution)/shard_map/pallas_call | solution.py:294
  852.1 9.6 shard_map.60
  861.8 13.5 %collective-permute-done.7.recv_ref = f32[1024,512]{1,0:T(8,128)} collective-permute-done((f32[1024,512]{1,0:T(8,128)}, f32[1024,512]{1,0:T(8,128)}, u32[]{:S(2)}, u32[]{:S(2)}) %collective-permute-start.7) | collective-permute-done | bytes 2097184 | tf_op jit(solution)/shard_map/ppermute | solution.py:687
  875.2 0.6 collective-permute-start.2
  875.9 13.9 %own_shared.1.base_ref = f32[1024,7168]{1,0:T(8,128)} custom-call(s32[1]{0:T(128)} %bitcast.pos_ref, f32[2048,512]{1,0:T(8,128)} %get-tuple-element.87.theta_ref, bf16[2048,2048]{1,0:T(8,128)(2,1)} %get-tuple-element.69.kern_hbm.kern_ref, f32[2048,1]{1,0:T(8,128)} %get-tuple-element.70.mass_ref, ...), custom_call_target="tpu_custom_call", output_to_operand_aliasing={{}: (8, {})} | custom-call | flops 4294967296 | bytes 10485760 | tf_op jit(solution)/shard_map/own_shared/pallas_call | solution.py:330
  889.8 0.0 collective-permute-done.9.theta_ref
  889.8 1.4 collective-permute-start.1
  891.2 13.9 %own_foreign.1.base_ref = f32[1024,7168]{1,0:T(8,128)} custom-call(s32[1]{0:T(128)} %bitcast.pos_ref, f32[2048,512]{1,0:T(8,128)} %collective-permute-done.9.theta_ref, bf16[2048,2048]{1,0:T(8,128)(2,1)} %get-tuple-element.69.kern_hbm.kern_ref, f32[2048,1]{1,0:T(8,128)} %get-tuple-element.70.mass_ref, ...), custom_call_target="tpu_custom_call", output_to_operand_aliasing={{}: (8, {})} | custom-call | flops 4294967296 | bytes 10485760 | tf_op jit(solution)/shard_map/own_foreign/pallas_call | solution.py:330
  905.1 1.9 shard_map.61.base_ref
  907.0 3.8 shard_map.62.base_ref
  910.8 3.8 shard_map.63.base_ref
  914.5 50.6 %collective-permute-done.5.recv_ref = f32[1024,512]{1,0:T(8,128)} collective-permute-done((f32[1024,512]{1,0:T(8,128)}, f32[1024,512]{1,0:T(8,128)}, u32[]{:S(2)}, u32[]{:S(2)}) %collective-permute-start.5) | collective-permute-done | bytes 2097184 | tf_op jit(solution)/shard_map/ppermute | solution.py:687
  965.1 3.8 shard_map.64.base_ref
  968.9 3.8 shard_map.65.base_ref
  972.7 37.4 %collective-permute-done.3.recv_ref = f32[1024,512]{1,0:T(8,128)} collective-permute-done((f32[1024,512]{1,0:T(8,128)}, f32[1024,512]{1,0:T(8,128)}, u32[]{:S(2)}, u32[]{:S(2)}) %collective-permute-start.3) | collective-permute-done | bytes 2097184 | tf_op jit(solution)/shard_map/ppermute | solution.py:687
  1010.1 3.8 shard_map.66.base_ref
  1013.8 18.7 %collective-permute-done.2.recv_ref = f32[1024,256]{1,0:T(8,128)} collective-permute-done((f32[1024,256]{1,0:T(8,128)}, f32[1024,256]{1,0:T(8,128)}, u32[]{:S(2)}, u32[]{:S(2)}) %collective-permute-start.2) | collective-permute-done | bytes 1048608 | tf_op jit(solution)/shard_map/ppermute | solution.py:687
  1032.5 2.0 shard_map.67.base_ref
  1034.6 8.7 collective-permute-done.1.recv_ref
  1043.3 0.8 copy-done.1
  1044.1 1.9 shard_map.68
  (4 shorter events, 0.0 us)
Async XLA Ops:
  370.7 71.2 %collective-permute-start = (f32[1024,768]{1,0:T(8,128)}, f32[1024,768]{1,0:T(8,128)}, u32[]{:S(2)}, u32[]{:S(2)}) collective-permute-start(f32[1024,768]{1,0:T(8,128)} %constant_dynamic-slice_fusion), channel_id=1, source_target_pairs={{0,4},{4,0},{1,5},{5,1},{2,6},{6,2},{3,7},{7,3}} | collective-permute-start | bytes 9437192 | tf_op jit(solution)/shard_map/ppermute | solution.py:674
  570.9 319.0 %collective-permute-start.9 = (f32[2048,512]{1,0:T(8,128)}, f32[2048,512]{1,0:T(8,128)}, u32[]{:S(2)}, u32[]{:S(2)}) collective-permute-start(f32[2048,512]{1,0:T(8,128)} %get-tuple-element.87.theta_ref), channel_id=1, source_target_pairs={{0,4},{4,0},{1,5},{5,1},{2,6},{6,2},{3,7},{7,3}} | collective-permute-start | bytes 12582920 | tf_op jit(solution)/shard_map/ppermute | solution.py:680
  744.1 75.8 %collective-permute-start.8 = (f32[1024,128]{1,0:T(8,128)}, f32[1024,128]{1,0:T(8,128)S(1)}, u32[]{:S(2)}, u32[]{:S(2)}) collective-permute-start(f32[1024,128]{1,0:T(8,128)} %get-tuple-element.86), channel_id=1, source_target_pairs={{0,4},{4,0},{1,5},{5,1},{2,6},{6,2},{3,7},{7,3}} | collective-permute-start | bytes 1572872 | tf_op jit(solution)/shard_map/ppermute | solution.py:687
  781.5 57.8 %collective-permute-start.6 = (f32[1024,512]{1,0:T(8,128)}, f32[1024,512]{1,0:T(8,128)}, u32[]{:S(2)}, u32[]{:S(2)}) collective-permute-start(f32[1024,512]{1,0:T(8,128)} %get-tuple-element.84), channel_id=1, source_target_pairs={{0,4},{4,0},{1,5},{5,1},{2,6},{6,2},{3,7},{7,3}} | collective-permute-start | bytes 6291464 | tf_op jit(solution)/shard_map/ppermute | solution.py:687
  782.1 93.1 %collective-permute-start.7 = (f32[1024,512]{1,0:T(8,128)}, f32[1024,512]{1,0:T(8,128)}, u32[]{:S(2)}, u32[]{:S(2)}) collective-permute-start(f32[1024,512]{1,0:T(8,128)} %get-tuple-element.85), channel_id=1, source_target_pairs={{0,4},{4,0},{1,5},{5,1},{2,6},{6,2},{3,7},{7,3}} | collective-permute-start | bytes 6291464 | tf_op jit(solution)/shard_map/ppermute | solution.py:687
  819.3 149.6 %collective-permute-start.4 = (f32[1024,512]{1,0:T(8,128)}, f32[1024,512]{1,0:T(8,128)}, u32[]{:S(2)}, u32[]{:S(2)}) collective-permute-start(f32[1024,512]{1,0:T(8,128)} %get-tuple-element.82), channel_id=1, source_target_pairs={{0,4},{4,0},{1,5},{5,1},{2,6},{6,2},{3,7},{7,3}} | collective-permute-start | bytes 6291464 | tf_op jit(solution)/shard_map/ppermute | solution.py:687
  820.0 19.3 %copy-start = (f32[1024,128]{1,0:T(8,128)}, f32[1024,128]{1,0:T(8,128)S(1)}, u32[]{:S(2)}) copy-start(f32[1024,128]{1,0:T(8,128)S(1)} %collective-permute-done.8.recv_ref) | copy-start | bytes 1572868
  820.0 145.2 %collective-permute-start.5 = (f32[1024,512]{1,0:T(8,128)}, f32[1024,512]{1,0:T(8,128)}, u32[]{:S(2)}, u32[]{:S(2)}) collective-permute-start(f32[1024,512]{1,0:T(8,128)} %get-tuple-element.83), channel_id=1, source_target_pairs={{0,4},{4,0},{1,5},{5,1},{2,6},{6,2},{3,7},{7,3}} | collective-permute-start | bytes 6291464 | tf_op jit(solution)/shard_map/ppermute | solution.py:687
  839.3 170.8 %collective-permute-start.3 = (f32[1024,512]{1,0:T(8,128)}, f32[1024,512]{1,0:T(8,128)}, u32[]{:S(2)}, u32[]{:S(2)}) collective-permute-start(f32[1024,512]{1,0:T(8,128)} %get-tuple-element.81), channel_id=1, source_target_pairs={{0,4},{4,0},{1,5},{5,1},{2,6},{6,2},{3,7},{7,3}} | collective-permute-start | bytes 6291464 | tf_op jit(solution)/shard_map/ppermute | solution.py:687
  875.2 157.3 %collective-permute-start.2 = (f32[1024,256]{1,0:T(8,128)}, f32[1024,256]{1,0:T(8,128)}, u32[]{:S(2)}, u32[]{:S(2)}) collective-permute-start(f32[1024,256]{1,0:T(8,128)} %get-tuple-element.80), channel_id=1, source_target_pairs={{0,4},{4,0},{1,5},{5,1},{2,6},{6,2},{3,7},{7,3}} | collective-permute-start | bytes 3145736 | tf_op jit(solution)/shard_map/ppermute | solution.py:687
  889.8 153.4 %collective-permute-start.1 = (f32[1024,128]{1,0:T(8,128)}, f32[1024,128]{1,0:T(8,128)S(1)}, u32[]{:S(2)}, u32[]{:S(2)}) collective-permute-start(f32[1024,128]{1,0:T(8,128)} %get-tuple-element.79), channel_id=1, source_target_pairs={{0,4},{4,0},{1,5},{5,1},{2,6},{6,2},{3,7},{7,3}} | collective-permute-start | bytes 1572872 | tf_op jit(solution)/shard_map/ppermute | solution.py:687
  1043.3 0.8 copy-start.1

commit v3 on v2

--- a/solution.py
+++ b/solution.py
@@ -29,12 +29,12 @@
     return (0, k * BLK, top), (1, k * BLK - HALF, low)
 
 
-def exchange_kernel(n_early, n_late, theta_ref, mean_ref, fact_ref, col_ref, gram_ref, proj_ref,
+def exchange_kernel(n_early, n_late, theta_ref, mean_ref, fact_ref, col_ref, late_own_ref, late_away_ref, gram_ref, proj_ref,
                     buf, tb, away, away_b, late_b, send_sem, recv_sem, lsend_sem, lrecv_sem, own_sem, put_sem, other_sem):
     part = lax.axis_index("part")
     other = 1 - part
     peer = (lax.axis_index("ens"), other, lax.axis_index("feat"))
-    rows, width = theta_ref.shape[0], col_ref.shape[1]
+    rows, width = theta_ref.shape[0], theta_ref.shape[1] // 2
     n_rows = col_ref.shape[0]
     cw = width // (n_early + n_late)
     n_blk = n_rows // BLK
@@ -63,6 +63,9 @@
     def put_own(c):
         return pltpu.make_async_copy(buf.at[own_rows, :], col_ref.at[own_rows, chunk(0, c)], put_sem)
 
+    def put_late(c):
+        return pltpu.make_async_copy(buf.at[own_rows, :], late_own_ref.at[:, chunk(0, c - n_early)], put_sem)
+
     def fetch_other(c):
         return pltpu.make_async_copy(col_ref.at[other_rows, chunk(0, c)], buf.at[other_rows, :], other_sem)
 
@@ -92,6 +95,8 @@
         fetch = pltpu.make_async_copy(theta_ref.at[:, chunk(other, n_early + c)], away, other_sem)
         fetch.start()
         fetch.wait()
+        keep = pltpu.make_async_copy(away, late_away_ref.at[:, chunk(0, c)], own_sem)
+        keep.start()
 
         @pl.loop(0, rows // BLK)
         def _(b):
@@ -99,6 +104,8 @@
             away_b[c, rs, :] = away[rs, :].astype(BF16)
             project(away, b * BLK, other, n_early + c, part * rows + b * BLK)
 
+        keep.wait()
+
     @pl.loop(0, n_late)
     def _(c):
         remote_late(c).start()
@@ -107,7 +114,14 @@
     def _(c):
         fetch_own(c).start()
         fetch_own(c).wait()
-        put_own(c).start()
+
+        @pl.when(c < n_early)
+        def _():
+            put_own(c).start()
+
+        @pl.when(c >= n_early)
+        def _():
+            put_late(c).start()
 
         @pl.loop(0, rows // BLK)
         def _(b):
@@ -135,7 +149,14 @@
             tb[other_rows, :] = late_b[c - n_early]
 
         add_gram()
-        put_own(c).wait()
+
+        @pl.when(c < n_early)
+        def _():
+            put_own(c).wait()
+
+        @pl.when(c >= n_early)
+        def _():
+            put_late(c).wait()
 
     @pl.loop(0, n_early)
     def _(c):
@@ -154,10 +175,12 @@
     dma = lambda *n: pltpu.SemaphoreType.DMA(n)
     return pl.pallas_call(
         functools.partial(exchange_kernel, n_early, n_late),
-        out_shape=(jax.ShapeDtypeStruct((n_rows, width), F32),
+        out_shape=(jax.ShapeDtypeStruct((n_rows, n_early * cw), F32),
+                   jax.ShapeDtypeStruct((rows, n_late * cw), F32),
+                   jax.ShapeDtypeStruct((rows, n_late * cw), F32),
                    jax.ShapeDtypeStruct((n_rows // BLK, 2, HALF, WIDE), F32),
                    jax.ShapeDtypeStruct((fact_t.shape[0], n_rows), F32)),
-        in_specs=[ANY, VMEM, VMEM], out_specs=(ANY, VMEM, VMEM),
+        in_specs=[ANY, VMEM, VMEM], out_specs=(ANY, ANY, ANY, VMEM, VMEM),
         scratch_shapes=[
             pltpu.VMEM((n_rows, cw), F32), pltpu.VMEM((n_rows, cw), BF16), pltpu.VMEM((rows, cw), F32),
             pltpu.VMEM((n_late, rows, cw), BF16), pltpu.VMEM((n_late, rows, cw), BF16),
@@ -173,83 +196,103 @@
     return tuple(ref[:, cols] for ref in refs)
 
 
-def build_rhs(theta_ref, mean, prec, fact, zb_ref, rhs, rs):
-    tile = theta_ref.shape[1]
-    th = theta_ref[rs, :]
+def build_rhs(th, mean, prec, fact, zb_ref, rhs, rs):
+    tile = th.shape[1]
     low = jnp.dot(zb_ref[rs, :], fact, preferred_element_type=F32)
     rhs[rs, :tile] = (-((th - mean) * prec + low)).astype(BF16)
     rhs[rs, tile:] = th.astype(BF16)
 
 
-def stepped(theta_ref, acc, mass_ref, rs, inv_n, two_over_h, step_size):
-    tile = theta_ref.shape[1]
-    th = theta_ref[rs, :]
+def stepped(th, acc, mass_ref, rs, inv_n, two_over_h, step_size):
+    tile = th.shape[1]
     pull = mass_ref[rs, :] * th.astype(BF16).astype(F32) - acc[:, tile:]
     return th + step_size * ((acc[:, :tile] + two_over_h * pull) * inv_n)
 
 
-def update_kernel(consts, first, theta_ref, next_ref, kern_hbm, mass_ref, zb_ref, mean_ref, prec_ref, fact_ref, *rest):
-    out_ref, tb_ref, proj_ref, rhs, kern_ref, kern_sem = rest[-6:]
-    n_rows, tile = theta_ref.shape
-    big = n_rows // 2
+def update_kernel(consts, first, split, has_before, *refs):
+    n_in = 2 * (2 if split else 1)
+    kern_hbm, mass_ref, zb_ref = refs[n_in:n_in + 3]
+    params = refs[n_in + 3:n_in + 6]
+    out_ref, tb_ref, proj_ref, rhs, kern_ref, kern_sem = refs[-6:]
+    tile = out_ref.shape[1]
+    big = out_ref.shape[0] // 2
     i = pl.program_id(0)
     slot = lax.rem(i, 2)
     part = lax.axis_index("part")
-    refs = (mean_ref, prec_ref, fact_ref)
+
+    def span(at, size):
+        return pl.ds(pl.multiple_of(at, BLK), size)
 
     @pl.when(i == 0)
     def _():
         kern_copy = pltpu.make_async_copy(kern_hbm, kern_ref, kern_sem)
         kern_copy.start()
-        proj_ref[...] = rest[0][...] if len(rest) > 6 else jnp.zeros_like(proj_ref)
-        now = columns(part, first * tile, tile, refs)
-
-        @pl.loop(0, n_rows // BLK)
-        def _(b):
-            build_rhs(theta_ref, *now, zb_ref, rhs.at[0], pl.ds(pl.multiple_of(b * BLK, BLK), BLK))
-
+        proj_ref[...] = refs[n_in + 6][...] if has_before else jnp.zeros_like(proj_ref)
+        now = columns(part, first * tile, tile, params)
+        if split:
+            for ref, half in ((refs[0], part), (refs[2], 1 - part)):
+                build_rhs(ref[...], *now, zb_ref, rhs.at[0], span(half * big, big))
+        else:
+            @pl.loop(0, 2)
+            def _(b):
+                rs = span(b * big, big)
+                build_rhs(refs[0][rs, :], *now, zb_ref, rhs.at[0], rs)
         kern_copy.wait()
 
-    mean, _, fact = columns(part, (first + i) * tile, tile, refs)
-    after = columns(part, (first + jnp.minimum(i + 1, pl.num_programs(0) - 1)) * tile, tile, refs)
-
-    @pl.loop(0, 2)
-    def _(b):
-        rs = pl.ds(pl.multiple_of(b * big, big), big)
+    mean, _, fact = columns(part, (first + i) * tile, tile, params)
+    after = columns(part, (first + jnp.minimum(i + 1, pl.num_programs(0) - 1)) * tile, tile, params)
+
+    def half_step(ref, next_ref, src, rs):
         acc = jnp.dot(kern_ref[rs, :], rhs[slot], preferred_element_type=F32)
-        build_rhs(next_ref, *after, zb_ref, rhs.at[1 - slot], rs)
-        new = stepped(theta_ref, acc, mass_ref, rs, *consts)
+        build_rhs(next_ref[src, :], *after, zb_ref, rhs.at[1 - slot], rs)
+        new = stepped(ref[src, :], acc, mass_ref, rs, *consts)
         out_ref[rs, :] = new
         tb_ref[rs, :] = new.astype(BF16)
         proj_ref[:, rs] += lax.dot_general(fact, (new - mean).astype(BF16), NT, preferred_element_type=F32)
 
-
-def update(consts, theta, kern, mass, zb, mean, prec, fact_t, tile, start, stop, own_out, before=None):
-    n_rows, width = theta.shape
-    rank = fact_t.shape[0]
-    first, steps = start // tile, (stop - start) // tile
-    col = lambda r: pl.BlockSpec((r, tile), lambda i: (0, first + i))
-    nxt = lambda r: pl.BlockSpec((r, tile), lambda i: (0, first + jnp.minimum(i + 1, steps - 1)))
-    in_specs = [col(n_rows), nxt(n_rows), ANY, VMEM, VMEM, VMEM, VMEM, VMEM]
-    args = [theta, theta, kern, mass, zb, mean, prec, fact_t]
+    if split:
+        for at, half in ((0, part), (2, 1 - part)):
+            half_step(refs[at], refs[at + 1], slice(None), span(half * big, big))
+    else:
+        @pl.loop(0, 2)
+        def _(b):
+            rs = span(b * big, big)
+            half_step(refs[0], refs[1], rs, rs)
+
+
+def update(consts, theta, kern, mass, zb, params, width, start, stop, own_out, before=None):
+    split = isinstance(theta, tuple)
+    n_rows = kern.shape[0]
+    rank = params[2].shape[0]
+    first, steps = start // BLK, (stop - start) // BLK
+    base = 0 if split else first
+    held = n_rows // 2 if split else n_rows
+    in_specs, args = [], []
+    for arr in theta if split else (theta,):
+        in_specs += [pl.BlockSpec((held, BLK), lambda i: (0, base + i)),
+                     pl.BlockSpec((held, BLK), lambda i: (0, base + jnp.minimum(i + 1, steps - 1)))]
+        args += [arr, arr]
+    in_specs += [ANY] + [VMEM] * 5
+    args += [kern, mass, zb, *params]
     alias = {}
     if before is not None:
         in_specs += [VMEM, ANY]
         args += [before[1], before[0]]
-        alias = {9: 1}
+        alias = {len(args) - 1: 1}
         if len(before) > 2:
             in_specs.append(ANY)
             args.append(before[2])
-            alias[10] = 0
+            alias[len(args) - 1] = 0
+    col = pl.BlockSpec((n_rows, BLK), lambda i: (0, first + i))
     return pl.pallas_call(
-        functools.partial(update_kernel, consts, first),
+        functools.partial(update_kernel, consts, first, split, before is not None),
         grid=(steps,),
         out_shape=(jax.ShapeDtypeStruct((n_rows, stop - start if own_out else width), F32),
                    jax.ShapeDtypeStruct((n_rows, width), BF16),
                    jax.ShapeDtypeStruct((rank, n_rows), F32)),
         in_specs=in_specs,
-        out_specs=(pl.BlockSpec((n_rows, tile), lambda i: (0, i)) if own_out else col(n_rows), col(n_rows), VMEM),
-        scratch_shapes=[pltpu.VMEM((2, n_rows, 2 * tile), BF16), pltpu.VMEM(kern.shape, BF16), pltpu.SemaphoreType.DMA],
+        out_specs=(pl.BlockSpec((n_rows, BLK), lambda i: (0, i)) if own_out else col, col, VMEM),
+        scratch_shapes=[pltpu.VMEM((2, n_rows, 2 * BLK), BF16), pltpu.VMEM(kern.shape, BF16), pltpu.SemaphoreType.DMA],
         input_output_aliases=alias,
         compiler_params=pltpu.CompilerParams(vmem_limit_bytes=VMEM_LIMIT),
         cost_estimate=pl.CostEstimate(flops=4 * n_rows * n_rows * (stop - start), bytes_accessed=10 * n_rows * (stop - start), transcendentals=0),
@@ -261,13 +304,13 @@
     kern_copy = pltpu.make_async_copy(kern_hbm, kern_ref, kern_sem)
     kern_copy.start()
     rows = out_ref.shape[0]
-    n_blk = theta_ref.shape[0] // BLK
     part = pos_ref[0]
     now = columns(part, start, theta_ref.shape[1], (mean_ref, prec_ref, fact_ref))
 
-    @pl.loop(0, n_blk)
+    @pl.loop(0, 2)
     def _(b):
-        build_rhs(theta_ref, *now, zb_ref, rhs, pl.ds(pl.multiple_of(b * BLK, BLK), BLK))
+        rs = pl.ds(pl.multiple_of(b * rows, BLK), rows)
+        build_rhs(theta_ref[rs, :], *now, zb_ref, rhs, rs)
 
     kern_copy.wait()
     for dst, which in ((send_ref, 1 - part), (out_ref, part)):
@@ -275,7 +318,7 @@
         def _(b):
             rs = pl.ds(pl.multiple_of(which * rows + b * BLK, BLK), BLK)
             acc = jnp.dot(kern_ref[rs, :], rhs[...], preferred_element_type=F32)
-            dst[pl.ds(pl.multiple_of(b * BLK, BLK), BLK), :] = stepped(theta_ref, acc, mass_ref, rs, *consts)
+            dst[pl.ds(pl.multiple_of(b * BLK, BLK), BLK), :] = stepped(theta_ref[rs, :], acc, mass_ref, rs, *consts)
 
 
 def last_update(consts, pos, theta, kern, mass, zb, mean, prec, fact_t, out, start, tile):
@@ -312,13 +355,14 @@
 
     @pl.loop(0, theta_ref.shape[0] // BLK)
     def _(b):
-        build_rhs(theta_ref, *now, zb_ref, rhs, pl.ds(pl.multiple_of(b * BLK, BLK), BLK))
+        rs = pl.ds(pl.multiple_of(b * BLK, BLK), BLK)
+        build_rhs(theta_ref[rs, :], *now, zb_ref, rhs, rs)
 
     @pl.loop(0, rows // BLK)
     def _(b):
         rs = pl.ds(pl.multiple_of(pos_ref[0] * rows + b * BLK, BLK), BLK)
         acc = jnp.dot(kern_ref[rs, :], rhs[...], preferred_element_type=F32)
-        out_ref[pl.ds(pl.multiple_of(b * BLK, BLK), BLK), :] = stepped(theta_ref, acc, mass_ref, rs, *consts)
+        out_ref[pl.ds(pl.multiple_of(b * BLK, BLK), BLK), :] = stepped(theta_ref[rs, :], acc, mass_ref, rs, *consts)
 
 
 def own_update(consts, pos, theta, kern, mass, zb, mean, prec, fact_t, out, foreign):
@@ -360,19 +404,6 @@
         input_output_aliases={2: 0},
         cost_estimate=pl.CostEstimate(flops=1000 * rows * tile, bytes_accessed=8 * rows * tile, transcendentals=0),
     )(pos, recv, out)
-
-
-def place_rows(pos, recv, cur, start):
-    rows, cols = recv.shape
-    return pl.pallas_call(
-        place_kernel,
-        grid_spec=pltpu.PrefetchScalarGridSpec(
-            num_scalar_prefetch=1, grid=(cols // BLK,), in_specs=[pl.BlockSpec((rows, BLK), lambda i, pos: (0, i)), ANY],
-            out_specs=pl.BlockSpec((rows, BLK), lambda i, pos: (1 - pos[0], start // BLK + i))),
-        out_shape=jax.ShapeDtypeStruct(cur.shape, cur.dtype),
-        input_output_aliases={2: 0},
-        name="place_rows",
-    )(pos, recv, cur)
 
 
 def kmat_kernel(from_gram, two_over_h, src_ref, proj_ref, kern_ref, zb_ref, mass_ref, *scratch):
@@ -666,19 +697,17 @@
         swap = [(0, 1), (1, 0)]
         late = 3 * BLK
         early = width - late
-        late_rows = lax.dynamic_slice_in_dim(theta, (1 - part) * width + early, late, axis=1)
-
-        cur, gram, proj = exchange(theta, params[0], params[2], early // BLK, late // BLK)
+
+        cur, late_own, late_away, gram, proj = exchange(theta, params[0], params[2], early // BLK, late // BLK)
         kern, zb, mass = kernel_matrix(gram, proj, consts[1], 1, True)
-        late_rows, mass = lax.optimization_barrier((late_rows, mass))
-        recv = lax.ppermute(late_rows, "part", swap)
-        new, tb, proj = update(consts, cur, kern, mass, zb, *params, BLK, 0, early, False)
-        cur = place_rows(pos, recv, cur, early)
-        cur, tb, proj = update(consts, cur, kern, mass, zb, *params, BLK, early, width, False, (tb, proj, new))
+        late_away, mass = lax.optimization_barrier((late_away, mass))
+        recv = lax.ppermute(late_away, "part", swap)
+        new, tb, proj = update(consts, cur, kern, mass, zb, params, width, 0, early, False)
+        cur, tb, proj = update(consts, (late_own, recv), kern, mass, zb, params, width, early, width, False, (tb, proj, new))
         kern, zb, mass = kernel_matrix(tb, proj, consts[1], 2, False)
-        both, tb, proj = update(consts, cur, kern, mass, zb, *params, BLK, 0, shared, True)
+        both, tb, proj = update(consts, cur, kern, mass, zb, params, width, 0, shared, True)
         foreign = lax.ppermute(both, "part", swap)
-        cur, tb, proj = update(consts, cur, kern, mass, zb, *params, BLK, shared, width, False, (tb, proj))
+        cur, tb, proj = update(consts, cur, kern, mass, zb, params, width, shared, width, False, (tb, proj))
         kern, zb, mass = kernel_matrix(tb, proj, consts[1], 3, False)
         out = None
         received = []

time: 1060 us -> 1120 us (1.057)
  waiting for transfers between devices: 132 us -> 214 us
  Pallas kernels: 899 us -> 887 us
    ppermute x8, waiting for transfers between devices: 129 us -> 211 us  [local_steps(): received.append(lax.ppermute(send, 'part', swap))]
    pallas_call x5 -> x4, Pallas kernels: 187 us -> 183 us  [update(): pl.pallas_call(functools.partial(update_kernel, consts, first, split, bef...]
  transfers between devices with their start and end apart: 10 -> 10, of which waited for: 6 -> 9; matrix products, arithmetic and copies ran while one was open for 0% -> 0% of each run, Pallas kernels for 38% -> 19%
where the time goes in v3:
time: 1120 us; the launch traced here: 1110 us
  Pallas kernels  887 us (79%)
  waiting for transfers between devices  214 us (19%)
    pallas_call x1, Pallas kernels, exchange(): pl.pallas_call(functools.partial(exchange_kernel, n_early, n_late), out_s...  292 us
    pallas_call x3, Pallas kernels, kernel_matrix(): pl.pallas_call(functools.partial(kmat_kernel, from_gram, two_over_h), out...  239 us
    ppermute x8, waiting for transfers between devices, local_steps(): received.append(lax.ppermute(send, 'part', swap))  211 us
    pallas_call x4, Pallas kernels, update(): pl.pallas_call(functools.partial(update_kernel, consts, first, split, bef...  183 us
    pallas_call x8, Pallas kernels, last_update(): pl.pallas_call(functools.partial(last_kernel, consts, start), grid_spec=p...  121 us
    pallas_call x2, Pallas kernels, own_update(): pl.pallas_call(functools.partial(own_kernel, consts, foreign), grid_spec=...  27.9 us
    pallas_call x8, Pallas kernels, place(): pl.pallas_call(place_kernel, grid_spec=pltpu.PrefetchScalarGridSpec(num_s...  24.7 us
  transfers between devices with their start and end apart: 10, of which 9 were waited for; matrix products, arithmetic and copies ran while one was open for 0% of the time, Pallas kernels for 19%

profile of v3, /device:TPU:0, one launch (start us, length us, event | category | flops | bytes accessed | tf_op | source)
XLA Modules:
  0.0 1111.8 jit_solution(85389170541170682)
XLA Ops:
  0.0 291.8 %exchange.1 = (f32[2048,2816]{1,0:T(8,128)}, f32[1024,768]{1,0:T(8,128)}, f32[1024,768]{1,0:T(8,128)}, f32[8,2,128,1152]{3,2,1,0:T(8,128)}, f32[32,2048]{1,0:T(8,128)}) custom-call(f32[1024,7168]{1,0:T(8,128)} %theta_ref.1, f32[1,7168]{1,0:T(1,128)} %bitcast.19, bf16[32,7168]{1,0:T(8,128)(2,1)} %bitcast.4), custom_call_target="tpu_custom_call" | custom-call | tf_op jit(solution)/shard_map/exchange/pallas_call | solution.py:176
  291.8 75.1 %shard_map.46 = (bf16[2048,2048]{1,0:T(8,128)(2,1)}, bf16[2048,32]{1,0:T(8,128)(2,1)}, f32[2048,1]{1,0:T(8,128)}) custom-call(f32[8,2,128,1152]{3,2,1,0:T(8,128)} %get-tuple-element.51.src_ref, f32[32,2048]{1,0:T(8,128)} %get-tuple-element.52.proj_ref), custom_call_target="tpu_custom_call" | custom-call | tf_op jit(solution)/shard_map/pallas_call | solution.py:671
  366.9 0.9 collective-permute-start
  367.8 66.9 %shard_map.47 = (f32[2048,3584]{1,0:T(8,128)}, bf16[2048,3584]{1,0:T(8,128)(2,1)}, f32[32,2048]{1,0:T(8,128)}) custom-call(f32[2048,2816]{1,0:T(8,128)} %get-tuple-element.58.refs_0_.refs_1_, f32[2048,2816]{1,0:T(8,128)} %get-tuple-element.58.refs_0_.refs_1_, bf16[2048,2048]{1,0:T(8,128)(2,1)} %get-tuple-element.55.refs_2_.refs_4_, ...), custom_call_target="tpu_custom_call" | custom-call | flops 47244640256 | bytes 57671680 | tf_op jit(solution)/shard_map/pallas_call | solution.py:287
  434.7 3.4 collective-permute-done.refs_2_.refs_3_
  438.1 25.3 %shard_map.48 = (f32[2048,3584]{1,0:T(8,128)}, bf16[2048,3584]{1,0:T(8,128)(2,1)}, f32[32,2048]{1,0:T(8,128)}) custom-call(f32[1024,768]{1,0:T(8,128)} %get-tuple-element.49.refs_0_.refs_1_, f32[1024,768]{1,0:T(8,128)} %get-tuple-element.49.refs_0_.refs_1_, ...), custom_call_target="tpu_custom_call", output_to_operand_aliasing={{1}: (11, {}), {0}: (12, {})} | custom-call | flops 12884901888 | bytes 15728640 | tf_op jit(solution)/shard_map/pallas_call | solution.py:287
  463.4 81.0 %shard_map.49 = (bf16[2048,2048]{1,0:T(8,128)(2,1)}, bf16[2048,32]{1,0:T(8,128)(2,1)}, f32[2048,1]{1,0:T(8,128)}) custom-call(bf16[2048,3584]{1,0:T(8,128)(2,1)} %get-tuple-element.63.src_ref, f32[32,2048]{1,0:T(8,128)} %get-tuple-element.64.proj_ref), custom_call_target="tpu_custom_call" | custom-call | tf_op jit(solution)/shard_map/pallas_call | solution.py:671
  544.4 18.8 %shard_map.50 = (f32[2048,512]{1,0:T(8,128)}, bf16[2048,3584]{1,0:T(8,128)(2,1)}, f32[32,2048]{1,0:T(8,128)}) custom-call(f32[2048,3584]{1,0:T(8,128)} %get-tuple-element.62.refs_0_.refs_1_, f32[2048,3584]{1,0:T(8,128)} %get-tuple-element.62.refs_0_.refs_1_, bf16[2048,2048]{1,0:T(8,128)(2,1)} %get-tuple-element.65.refs_2_, ...), custom_call_target="tpu_custom_call" | custom-call | flops 8589934592 | bytes 10485760 | tf_op jit(solution)/shard_map/pallas_call | solution.py:287
  563.2 72.4 %shard_map.51 = (f32[2048,3584]{1,0:T(8,128)}, bf16[2048,3584]{1,0:T(8,128)(2,1)}, f32[32,2048]{1,0:T(8,128)}) custom-call(f32[2048,3584]{1,0:T(8,128)} %get-tuple-element.62.refs_0_.refs_1_, f32[2048,3584]{1,0:T(8,128)} %get-tuple-element.62.refs_0_.refs_1_, bf16[2048,2048]{1,0:T(8,128)(2,1)} %get-tuple-element.65.refs_2_, ...), custom_call_target="tpu_custom_call", output_to_operand_aliasing={{1}: (9, {})} | custom-call | flops 51539607552 | bytes 62914560 | tf_op jit(solution)/shard_map/pallas_call | solution.py:287
  635.6 82.6 %shard_map.52 = (bf16[2048,2048]{1,0:T(8,128)(2,1)}, bf16[2048,32]{1,0:T(8,128)(2,1)}, f32[2048,1]{1,0:T(8,128)}) custom-call(bf16[2048,3584]{1,0:T(8,128)(2,1)} %get-tuple-element.71.src_ref, f32[32,2048]{1,0:T(8,128)} %get-tuple-element.72.proj_ref), custom_call_target="tpu_custom_call" | custom-call | tf_op jit(solution)/shard_map/pallas_call | solution.py:671
  718.2 9.6 shard_map.53
  727.8 17.9 %shard_map.54 = (f32[1024,7168]{1,0:T(8,128)}, f32[1024,512]{1,0:T(8,128)}) custom-call(s32[1]{0:T(128)} %bitcast.pos_ref, f32[2048,3584]{1,0:T(8,128)} %get-tuple-element.70.theta_ref, bf16[2048,2048]{1,0:T(8,128)(2,1)} %get-tuple-element.73.kern_hbm.kern_ref, f32[2048,1]{1,0:T(8,128)} %get-tuple-element.74.mass_ref, ...), custom_call_target="tpu_custom_call", output_to_operand_aliasing={{0}: (8, {})} | custom-call | flops 8589934592 | bytes 10485760 | tf_op jit(solution)/shard_map/pallas_call | solution.py:337
  745.7 0.7 collective-permute-start.9
  746.4 17.9 %shard_map.55 = (f32[1024,7168]{1,0:T(8,128)}, f32[1024,512]{1,0:T(8,128)}) custom-call(s32[1]{0:T(128)} %bitcast.pos_ref, f32[2048,3584]{1,0:T(8,128)} %get-tuple-element.70.theta_ref, bf16[2048,2048]{1,0:T(8,128)(2,1)} %get-tuple-element.73.kern_hbm.kern_ref, f32[2048,1]{1,0:T(8,128)} %get-tuple-element.74.mass_ref, ...), custom_call_target="tpu_custom_call", output_to_operand_aliasing={{0}: (8, {})} | custom-call | flops 8589934592 | bytes 10485760 | tf_op jit(solution)/shard_map/pallas_call | solution.py:337
  764.3 1.4 collective-permute-start.8
  765.7 0.7 collective-permute-start.7
  766.4 1.4 collective-permute-start.6
  767.7 17.9 %shard_map.56 = (f32[1024,7168]{1,0:T(8,128)}, f32[1024,512]{1,0:T(8,128)}) custom-call(s32[1]{0:T(128)} %bitcast.pos_ref, f32[2048,3584]{1,0:T(8,128)} %get-tuple-element.70.theta_ref, bf16[2048,2048]{1,0:T(8,128)(2,1)} %get-tuple-element.73.kern_hbm.kern_ref, f32[2048,1]{1,0:T(8,128)} %get-tuple-element.74.mass_ref, ...), custom_call_target="tpu_custom_call", output_to_operand_aliasing={{0}: (8, {})} | custom-call | flops 8589934592 | bytes 10485760 | tf_op jit(solution)/shard_map/pallas_call | solution.py:337
  785.6 17.9 %shard_map.57 = (f32[1024,7168]{1,0:T(8,128)}, f32[1024,512]{1,0:T(8,128)}) custom-call(s32[1]{0:T(128)} %bitcast.pos_ref, f32[2048,3584]{1,0:T(8,128)} %get-tuple-element.70.theta_ref, bf16[2048,2048]{1,0:T(8,128)(2,1)} %get-tuple-element.73.kern_hbm.kern_ref, f32[2048,1]{1,0:T(8,128)} %get-tuple-element.74.mass_ref, ...), custom_call_target="tpu_custom_call", output_to_operand_aliasing={{0}: (8, {})} | custom-call | flops 8589934592 | bytes 10485760 | tf_op jit(solution)/shard_map/pallas_call | solution.py:337
  803.5 0.7 collective-permute-start.5
  804.2 46.5 %collective-permute-done.8.recv_ref = f32[1024,128]{1,0:T(8,128)S(1)} collective-permute-done((f32[1024,128]{1,0:T(8,128)}, f32[1024,128]{1,0:T(8,128)S(1)}, u32[]{:S(2)}, u32[]{:S(2)}) %collective-permute-start.8) | collective-permute-done | bytes 524320 | tf_op jit(solution)/shard_map/ppermute | solution.py:716
  850.6 0.7 collective-permute-start.4
  851.3 17.9 %shard_map.58 = (f32[1024,7168]{1,0:T(8,128)}, f32[1024,512]{1,0:T(8,128)}) custom-call(s32[1]{0:T(128)} %bitcast.pos_ref, f32[2048,3584]{1,0:T(8,128)} %get-tuple-element.70.theta_ref, bf16[2048,2048]{1,0:T(8,128)(2,1)} %get-tuple-element.73.kern_hbm.kern_ref, f32[2048,1]{1,0:T(8,128)} %get-tuple-element.74.mass_ref, ...), custom_call_target="tpu_custom_call", output_to_operand_aliasing={{0}: (8, {})} | custom-call | flops 8589934592 | bytes 10485760 | tf_op jit(solution)/shard_map/pallas_call | solution.py:337
  869.2 0.0 copy-done
  869.2 26.5 %collective-permute-done.7.recv_ref = f32[1024,512]{1,0:T(8,128)} collective-permute-done((f32[1024,512]{1,0:T(8,128)}, f32[1024,512]{1,0:T(8,128)}, u32[]{:S(2)}, u32[]{:S(2)}) %collective-permute-start.7) | collective-permute-done | bytes 2097184 | tf_op jit(solution)/shard_map/ppermute | solution.py:716
  895.7 0.7 collective-permute-start.3
  896.4 12.2 %shard_map.59 = (f32[1024,7168]{1,0:T(8,128)}, f32[1024,256]{1,0:T(8,128)}) custom-call(s32[1]{0:T(128)} %bitcast.pos_ref, f32[2048,3584]{1,0:T(8,128)} %get-tuple-element.70.theta_ref, bf16[2048,2048]{1,0:T(8,128)(2,1)} %get-tuple-element.73.kern_hbm.kern_ref, f32[2048,1]{1,0:T(8,128)} %get-tuple-element.74.mass_ref, ...), custom_call_target="tpu_custom_call", output_to_operand_aliasing={{0}: (8, {})} | custom-call | flops 4294967296 | bytes 5242880 | tf_op jit(solution)/shard_map/pallas_call | solution.py:337
  908.6 9.6 shard_map.60
  918.2 22.4 %collective-permute-done.6.recv_ref = f32[1024,512]{1,0:T(8,128)} collective-permute-done((f32[1024,512]{1,0:T(8,128)}, f32[1024,512]{1,0:T(8,128)}, u32[]{:S(2)}, u32[]{:S(2)}) %collective-permute-start.6) | collective-permute-done | bytes 2097184 | tf_op jit(solution)/shard_map/ppermute | solution.py:716
  940.6 0.7 collective-permute-start.2
  941.3 13.9 %own_shared.1.base_ref = f32[1024,7168]{1,0:T(8,128)} custom-call(s32[1]{0:T(128)} %bitcast.pos_ref, f32[2048,512]{1,0:T(8,128)} %get-tuple-element.91.theta_ref, bf16[2048,2048]{1,0:T(8,128)(2,1)} %get-tuple-element.73.kern_hbm.kern_ref, f32[2048,1]{1,0:T(8,128)} %get-tuple-element.74.mass_ref, ...), custom_call_target="tpu_custom_call", output_to_operand_aliasing={{}: (8, {})} | custom-call | flops 4294967296 | bytes 10485760 | tf_op jit(solution)/shard_map/own_shared/pallas_call | solution.py:374
  955.2 0.0 collective-permute-done.9.theta_ref
  955.3 1.3 collective-permute-start.1
  956.6 14.0 %own_foreign.1.base_ref = f32[1024,7168]{1,0:T(8,128)} custom-call(s32[1]{0:T(128)} %bitcast.pos_ref, f32[2048,512]{1,0:T(8,128)} %collective-permute-done.9.theta_ref, bf16[2048,2048]{1,0:T(8,128)(2,1)} %get-tuple-element.73.kern_hbm.kern_ref, f32[2048,1]{1,0:T(8,128)} %get-tuple-element.74.mass_ref, ...), custom_call_target="tpu_custom_call", output_to_operand_aliasing={{}: (8, {})} | custom-call | flops 4294967296 | bytes 10485760 | tf_op jit(solution)/shard_map/own_foreign/pallas_call | solution.py:374
  970.6 1.9 shard_map.61.base_ref
  972.5 3.8 shard_map.62.base_ref
  976.2 3.8 shard_map.63.base_ref
  980.0 5.6 collective-permute-done.5.recv_ref
  985.6 3.8 shard_map.64.base_ref
  989.3 41.2 %collective-permute-done.4.recv_ref = f32[1024,512]{1,0:T(8,128)} collective-permute-done((f32[1024,512]{1,0:T(8,128)}, f32[1024,512]{1,0:T(8,128)}, u32[]{:S(2)}, u32[]{:S(2)}) %collective-permute-start.4) | collective-permute-done | bytes 2097184 | tf_op jit(solution)/shard_map/ppermute | solution.py:716
  1030.5 3.8 shard_map.65.base_ref
  1034.3 41.2 %collective-permute-done.3.recv_ref = f32[1024,512]{1,0:T(8,128)} collective-permute-done((f32[1024,512]{1,0:T(8,128)}, f32[1024,512]{1,0:T(8,128)}, u32[]{:S(2)}, u32[]{:S(2)}) %collective-permute-start.3) | collective-permute-done | bytes 2097184 | tf_op jit(solution)/shard_map/ppermute | solution.py:716
  1075.5 3.8 shard_map.66.base_ref
  1079.2 18.7 %collective-permute-done.2.recv_ref = f32[1024,256]{1,0:T(8,128)} collective-permute-done((f32[1024,256]{1,0:T(8,128)}, f32[1024,256]{1,0:T(8,128)}, u32[]{:S(2)}, u32[]{:S(2)}) %collective-permute-start.2) | collective-permute-done | bytes 1048608 | tf_op jit(solution)/shard_map/ppermute | solution.py:716
  1097.9 2.0 shard_map.67.base_ref
  1100.0 9.0 collective-permute-done.1.recv_ref
  1108.9 0.8 copy-done.1
  1109.7 1.9 shard_map.68
  (2 shorter events, 0.0 us)
Async XLA Ops:
  366.9 71.2 %collective-permute-start = (f32[1024,768]{1,0:T(8,128)}, f32[1024,768]{1,0:T(8,128)}, u32[]{:S(2)}, u32[]{:S(2)}) collective-permute-start(f32[1024,768]{1,0:T(8,128)} %get-tuple-element.54), channel_id=1, source_target_pairs={{0,4},{4,0},{1,5},{5,1},{2,6},{6,2},{3,7},{7,3}} | collective-permute-start | bytes 9437192 | tf_op jit(solution)/shard_map/ppermute | solution.py:704
  745.7 209.5 %collective-permute-start.9 = (f32[2048,512]{1,0:T(8,128)}, f32[2048,512]{1,0:T(8,128)}, u32[]{:S(2)}, u32[]{:S(2)}) collective-permute-start(f32[2048,512]{1,0:T(8,128)} %get-tuple-element.91.theta_ref), channel_id=1, source_target_pairs={{0,4},{4,0},{1,5},{5,1},{2,6},{6,2},{3,7},{7,3}} | collective-permute-start | bytes 12582920 | tf_op jit(solution)/shard_map/ppermute | solution.py:709
  764.3 86.3 %collective-permute-start.8 = (f32[1024,128]{1,0:T(8,128)}, f32[1024,128]{1,0:T(8,128)S(1)}, u32[]{:S(2)}, u32[]{:S(2)}) collective-permute-start(f32[1024,128]{1,0:T(8,128)} %get-tuple-element.90), channel_id=1, source_target_pairs={{0,4},{4,0},{1,5},{5,1},{2,6},{6,2},{3,7},{7,3}} | collective-permute-start | bytes 1572872 | tf_op jit(solution)/shard_map/ppermute | solution.py:716
  765.7 130.0 %collective-permute-start.7 = (f32[1024,512]{1,0:T(8,128)}, f32[1024,512]{1,0:T(8,128)}, u32[]{:S(2)}, u32[]{:S(2)}) collective-permute-start(f32[1024,512]{1,0:T(8,128)} %get-tuple-element.89), channel_id=1, source_target_pairs={{0,4},{4,0},{1,5},{5,1},{2,6},{6,2},{3,7},{7,3}} | collective-permute-start | bytes 6291464 | tf_op jit(solution)/shard_map/ppermute | solution.py:716
  766.4 174.3 %collective-permute-start.6 = (f32[1024,512]{1,0:T(8,128)}, f32[1024,512]{1,0:T(8,128)}, u32[]{:S(2)}, u32[]{:S(2)}) collective-permute-start(f32[1024,512]{1,0:T(8,128)} %get-tuple-element.88), channel_id=1, source_target_pairs={{0,4},{4,0},{1,5},{5,1},{2,6},{6,2},{3,7},{7,3}} | collective-permute-start | bytes 6291464 | tf_op jit(solution)/shard_map/ppermute | solution.py:716
  803.5 182.1 %collective-permute-start.5 = (f32[1024,512]{1,0:T(8,128)}, f32[1024,512]{1,0:T(8,128)}, u32[]{:S(2)}, u32[]{:S(2)}) collective-permute-start(f32[1024,512]{1,0:T(8,128)} %get-tuple-element.87), channel_id=1, source_target_pairs={{0,4},{4,0},{1,5},{5,1},{2,6},{6,2},{3,7},{7,3}} | collective-permute-start | bytes 6291464 | tf_op jit(solution)/shard_map/ppermute | solution.py:716
  850.6 18.6 %copy-start = (f32[1024,128]{1,0:T(8,128)}, f32[1024,128]{1,0:T(8,128)S(1)}, u32[]{:S(2)}) copy-start(f32[1024,128]{1,0:T(8,128)S(1)} %collective-permute-done.8.recv_ref) | copy-start | bytes 1572868
  850.6 179.9 %collective-permute-start.4 = (f32[1024,512]{1,0:T(8,128)}, f32[1024,512]{1,0:T(8,128)}, u32[]{:S(2)}, u32[]{:S(2)}) collective-permute-start(f32[1024,512]{1,0:T(8,128)} %get-tuple-element.86), channel_id=1, source_target_pairs={{0,4},{4,0},{1,5},{5,1},{2,6},{6,2},{3,7},{7,3}} | collective-permute-start | bytes 6291464 | tf_op jit(solution)/shard_map/ppermute | solution.py:716
  895.7 179.8 %collective-permute-start.3 = (f32[1024,512]{1,0:T(8,128)}, f32[1024,512]{1,0:T(8,128)}, u32[]{:S(2)}, u32[]{:S(2)}) collective-permute-start(f32[1024,512]{1,0:T(8,128)} %get-tuple-element.85), channel_id=1, source_target_pairs={{0,4},{4,0},{1,5},{5,1},{2,6},{6,2},{3,7},{7,3}} | collective-permute-start | bytes 6291464 | tf_op jit(solution)/shard_map/ppermute | solution.py:716
  940.6 157.3 %collective-permute-start.2 = (f32[1024,256]{1,0:T(8,128)}, f32[1024,256]{1,0:T(8,128)}, u32[]{:S(2)}, u32[]{:S(2)}) collective-permute-start(f32[1024,256]{1,0:T(8,128)} %get-tuple-element.84), channel_id=1, source_target_pairs={{0,4},{4,0},{1,5},{5,1},{2,6},{6,2},{3,7},{7,3}} | collective-permute-start | bytes 3145736 | tf_op jit(solution)/shard_map/ppermute | solution.py:716
  955.3 153.7 %collective-permute-start.1 = (f32[1024,128]{1,0:T(8,128)}, f32[1024,128]{1,0:T(8,128)S(1)}, u32[]{:S(2)}, u32[]{:S(2)}) collective-permute-start(f32[1024,128]{1,0:T(8,128)} %get-tuple-element.83), channel_id=1, source_target_pairs={{0,4},{4,0},{1,5},{5,1},{2,6},{6,2},{3,7},{7,3}} | collective-permute-start | bytes 1572872 | tf_op jit(solution)/shard_map/ppermute | solution.py:716
  1108.9 0.8 copy-start.1

commit v4 on v3

--- a/solution.py
+++ b/solution.py
@@ -9,8 +9,8 @@
 
 BLK = 256
 HALF = BLK // 2
-REACH = 5
-WIDE = 9 * HALF
+WIDE = 8 * HALF
+TALL = HALF + 8
 MESH = pl.DeviceIdType.MESH
 F32 = jnp.float32
 BF16 = jnp.bfloat16
@@ -20,13 +20,34 @@
 NT = (((1,), (1,)), ((), ()))
 
 
-def band_parts(k, val):
-    top, low = val[:HALF], val[HALF:]
-    if k == 0:
-        return (0, 0, top), (1, 0, low[:, HALF:])
-    if k == REACH - 1:
-        top = top[:, :HALF]
-    return (0, k * BLK, top), (1, k * BLK - HALF, low)
+def fold(tile):
+    return jnp.concatenate([tile[8 * g:8 * g + 8] for g in range(8)], axis=1)
+
+
+def unfold(rows):
+    return jnp.concatenate([rows[:, HALF * g:HALF * (g + 1)] for g in range(8)], axis=0)
+
+
+def band_pieces(rows_at, b, n_blk):
+    def dot(left, right):
+        return lax.dot_general(left, right, NT, preferred_element_type=F32)
+
+    def wrap(j):
+        return j % n_blk if isinstance(j, int) else lax.rem(j, n_blk)
+
+    main = slice(0, HALF)
+    both = rows_at(b * BLK, BLK)
+    for k in range(4):
+        val = dot(both, rows_at(wrap(b + k) * BLK, BLK))
+        yield 0, main, slice(k * BLK, (k + 1) * BLK), val[:HALF]
+        if k == 0:
+            yield 1, main, slice(0, HALF), val[HALF:, HALF:]
+        else:
+            yield 1, main, slice(k * BLK - HALF, k * BLK + HALF), val[HALF:]
+    yield 1, main, slice(WIDE - HALF, WIDE), dot(rows_at(b * BLK + HALF, HALF), rows_at(wrap(b + 4) * BLK, HALF))
+    far = dot(rows_at(b * HALF, HALF), rows_at((b + n_blk) * HALF, HALF))
+    for h in range(2):
+        yield h, slice(HALF, TALL), slice(0, WIDE), fold(far[h * (HALF // 2):(h + 1) * (HALF // 2)])
 
 
 def exchange_kernel(n_early, n_late, theta_ref, mean_ref, fact_ref, col_ref, late_own_ref, late_away_ref, gram_ref, proj_ref,
@@ -76,12 +97,8 @@
 
     def add_gram():
         for b in range(n_blk):
-            rows_b = tb[b * BLK:(b + 1) * BLK, :]
-            for k in range(REACH):
-                j = (b + k) % n_blk
-                val = lax.dot_general(rows_b, tb[j * BLK:(j + 1) * BLK, :], NT, preferred_element_type=F32)
-                for h, col, piece in band_parts(k, val):
-                    gram_ref[b, h, :, col:col + piece.shape[1]] += piece
+            for h, rows_, cols_, piece in band_pieces(lambda at, n: tb[at:at + n, :], b, n_blk):
+                gram_ref[b, h, rows_, cols_] += piece
 
     @pl.loop(0, n_early)
     def _(c):
@@ -178,7 +195,7 @@
         out_shape=(jax.ShapeDtypeStruct((n_rows, n_early * cw), F32),
                    jax.ShapeDtypeStruct((rows, n_late * cw), F32),
                    jax.ShapeDtypeStruct((rows, n_late * cw), F32),
-                   jax.ShapeDtypeStruct((n_rows // BLK, 2, HALF, WIDE), F32),
+                   jax.ShapeDtypeStruct((n_rows // BLK, 2, TALL, WIDE), F32),
                    jax.ShapeDtypeStruct((fact_t.shape[0], n_rows), F32)),
         in_specs=[ANY, VMEM, VMEM], out_specs=(ANY, ANY, ANY, VMEM, VMEM),
         scratch_shapes=[
@@ -223,10 +240,16 @@
     def span(at, size):
         return pl.ds(pl.multiple_of(at, BLK), size)
 
+    def order(h):
+        return lax.rem(part + h, 2) if split else h
+
+    def fetch(half):
+        return pltpu.make_async_copy(kern_hbm.at[span(half * big, big), :], kern_ref.at[span(half * big, big), :], kern_sem.at[half])
+
     @pl.when(i == 0)
     def _():
-        kern_copy = pltpu.make_async_copy(kern_hbm, kern_ref, kern_sem)
-        kern_copy.start()
+        for h in range(2):
+            fetch(order(h)).start()
         proj_ref[...] = refs[n_in + 6][...] if has_before else jnp.zeros_like(proj_ref)
         now = columns(part, first * tile, tile, params)
         if split:
@@ -237,12 +260,17 @@
             def _(b):
                 rs = span(b * big, big)
                 build_rhs(refs[0][rs, :], *now, zb_ref, rhs.at[0], rs)
-        kern_copy.wait()
 
     mean, _, fact = columns(part, (first + i) * tile, tile, params)
     after = columns(part, (first + jnp.minimum(i + 1, pl.num_programs(0) - 1)) * tile, tile, params)
 
-    def half_step(ref, next_ref, src, rs):
+    def half_step(ref, next_ref, src, half):
+        rs = span(half * big, big)
+
+        @pl.when(i == 0)
+        def _():
+            fetch(half).wait()
+
         acc = jnp.dot(kern_ref[rs, :], rhs[slot], preferred_element_type=F32)
         build_rhs(next_ref[src, :], *after, zb_ref, rhs.at[1 - slot], rs)
         new = stepped(ref[src, :], acc, mass_ref, rs, *consts)
@@ -252,12 +280,11 @@
 
     if split:
         for at, half in ((0, part), (2, 1 - part)):
-            half_step(refs[at], refs[at + 1], slice(None), span(half * big, big))
+            half_step(refs[at], refs[at + 1], slice(None), half)
     else:
         @pl.loop(0, 2)
         def _(b):
-            rs = span(b * big, big)
-            half_step(refs[0], refs[1], rs, rs)
+            half_step(refs[0], refs[1], span(b * big, big), b)
 
 
 def update(consts, theta, kern, mass, zb, params, width, start, stop, own_out, before=None):
@@ -292,7 +319,7 @@
                    jax.ShapeDtypeStruct((rank, n_rows), F32)),
         in_specs=in_specs,
         out_specs=(pl.BlockSpec((n_rows, BLK), lambda i: (0, i)) if own_out else col, col, VMEM),
-        scratch_shapes=[pltpu.VMEM((2, n_rows, 2 * BLK), BF16), pltpu.VMEM(kern.shape, BF16), pltpu.SemaphoreType.DMA],
+        scratch_shapes=[pltpu.VMEM((2, n_rows, 2 * BLK), BF16), pltpu.VMEM(kern.shape, BF16), pltpu.SemaphoreType.DMA((2,))],
         input_output_aliases=alias,
         compiler_params=pltpu.CompilerParams(vmem_limit_bytes=VMEM_LIMIT),
         cost_estimate=pl.CostEstimate(flops=4 * n_rows * n_rows * (stop - start), bytes_accessed=10 * n_rows * (stop - start), transcendentals=0),
@@ -313,12 +340,24 @@
         build_rhs(theta_ref[rs, :], *now, zb_ref, rhs, rs)
 
     kern_copy.wait()
-    for dst, which in ((send_ref, 1 - part), (out_ref, part)):
-        @pl.loop(0, rows // BLK)
-        def _(b):
-            rs = pl.ds(pl.multiple_of(which * rows + b * BLK, BLK), BLK)
-            acc = jnp.dot(kern_ref[rs, :], rhs[...], preferred_element_type=F32)
-            dst[pl.ds(pl.multiple_of(b * BLK, BLK), BLK), :] = stepped(theta_ref[rs, :], acc, mass_ref, rs, *consts)
+    size = BLK if theta_ref.shape[1] < BLK else HALF
+    each = rows // size
+
+    @pl.loop(0, 2 * each)
+    def _(b):
+        mine = b // each
+        at = pl.multiple_of(lax.rem(b, each) * size, size)
+        rs = pl.ds(pl.multiple_of(lax.rem(1 - part + mine, 2) * rows + at, size), size)
+        acc = jnp.dot(kern_ref[rs, :], rhs[...], preferred_element_type=F32)
+        new = stepped(theta_ref[rs, :], acc, mass_ref, rs, *consts)
+
+        @pl.when(mine == 0)
+        def _():
+            send_ref[pl.ds(at, size), :] = new
+
+        @pl.when(mine == 1)
+        def _():
+            out_ref[pl.ds(at, size), :] = new
 
 
 def last_update(consts, pos, theta, kern, mass, zb, mean, prec, fact_t, out, start, tile):
@@ -406,14 +445,12 @@
     )(pos, recv, out)
 
 
-def kmat_kernel(from_gram, two_over_h, src_ref, proj_ref, kern_ref, zb_ref, mass_ref, *scratch):
-    if from_gram:
-        tb, sib_out = None, None
-    else:
-        tb, sib_out, load_sem = scratch[-3:]
+def kmat_kernel(from_gram, two_over_h, src_ref, proj_ref, kern_out, zb_ref, mass_ref, *scratch):
+    if not from_gram:
+        tb, load_sem = scratch[-2:]
     (gbuf, sib_in, r_x1, r_y1, r_x2, r_y2, sq_parts, sq, z_in, z_all, kbuf,
      sib_send, sib_recv, rs_send, rs_recv, sq_send, sq_recv, z_send, z_recv, zb_send, zb_recv,
-     k_send, k_recv, loc_sem) = scratch[:24]
+     k_send, k_recv, loc_sem, kern_ref, kern_sem) = scratch[:26]
     n_rows = kern_ref.shape[0]
     n_blk = n_rows // BLK
     ens, part, feat = lax.axis_index("ens"), lax.axis_index("part"), lax.axis_index("feat")
@@ -470,7 +507,7 @@
     z_own.start()
 
     def sib_copy(rel):
-        src = src_ref.at[block(rel, 1)] if from_gram else sib_out.at[rel]
+        src = src_ref.at[block(rel, 1)] if from_gram else gbuf.at[4 + rel]
         return rcopy(src, sib_in.at[rel], sib_send.at[rel], sib_recv.at[rel], sibling)
 
     lo, hi = 0, 1
@@ -500,37 +537,39 @@
             merge(rel)
             first_sends(rel)
     else:
-        def bands_of(b, dst):
-            rows = tb[pl.ds(pl.multiple_of(b * BLK, BLK), BLK), :]
-            for k in range(REACH):
-                j = lax.rem(b + k, n_blk)
-                val = lax.dot_general(
-                    rows, tb[pl.ds(pl.multiple_of(j * BLK, BLK), BLK), :], NT, preferred_element_type=F32)
-                for h, col, piece in band_parts(k, val):
-                    dst[h, :, col:col + piece.shape[1]] = piece
+        def rows_at(at, n):
+            return tb[pl.ds(pl.multiple_of(at, HALF), n), :]
 
         for b in range(n_blk):
             load(b).wait()
 
-        @pl.loop(0, 4)
+        @pl.loop(0, 8)
         def _(i):
-            rel = 3 - i
+            rel, own = 3 - i // 2, lax.rem(i, 2)
             cy, cx = lax.rem(part + rel // 2, 2), lax.rem(x + lax.rem(rel, 2), 2)
-            base = cy * 4 + cx * 2
-            bands_of(base + 1 - core, sib_out.at[rel])
-            rcopy(sib_out.at[rel], sib_in.at[rel], sib_send.at[rel], sib_recv.at[rel], sibling).start()
-            bands_of(base + core, gbuf.at[rel])
-            rcopy(sib_out.at[rel], sib_in.at[rel], sib_send.at[rel], sib_recv.at[rel], sibling).wait_recv()
-            gbuf[rel] += sib_in[rel]
-            for r in (3, 2, 1):
-                @pl.when(rel == r)
-                def _():
-                    first_sends(r)
+            b = cy * 4 + cx * 2 + lax.rem(core + 1 - own, 2)
+            dst = rel + 4 * (1 - own)
+            for h, rows_, cols_, piece in band_pieces(rows_at, b, n_blk):
+                gbuf[dst, h, rows_, cols_] = piece
+            across = rcopy(gbuf.at[4 + rel], sib_in.at[rel], sib_send.at[rel], sib_recv.at[rel], sibling)
+
+            @pl.when(own == 0)
+            def _():
+                across.start()
+
+            @pl.when(own == 1)
+            def _():
+                across.wait_recv()
+                gbuf[rel] += sib_in[rel]
+                for r in (3, 2, 1):
+                    @pl.when(rel == r)
+                    def _():
+                        first_sends(r)
 
     for rel in range(4):
         cy, cx = chip(rel)
         for h in range(2):
-            sq_parts[me, cy * 2 + cx, :, h * HALF:(h + 1) * HALF] = jnp.sum(gbuf[rel, h, :, :HALF] * eye, axis=0, keepdims=True)
+            sq_parts[me, cy * 2 + cx, :, h * HALF:(h + 1) * HALF] = jnp.sum(gbuf[rel, h, :HALF, :HALF] * eye, axis=0, keepdims=True)
 
     def sq_copy(i):
         rel, flip = others[i]
@@ -571,13 +610,24 @@
             s = sq_parts[c, q] + sq_parts[2 + c, q] + sq_parts[4 + c, q] + sq_parts[6 + c, q]
             b = 2 * q + c
             sq[:, b * BLK:(b + 1) * BLK] = s
-            if b < REACH - 1:
+            if b < WIDE // BLK:
                 sq[:, n_rows + b * BLK:n_rows + (b + 1) * BLK] = s
 
-    def kernel_of(h, gram):
-        row = sq[:, pl.ds(pl.multiple_of((2 * me + h) * HALF, HALF), WIDE)]
-        col = jnp.sum(eye * row[:, :HALF], axis=1, keepdims=True)
-        return jnp.exp(-jnp.maximum(col + row - 2.0 * gram, 0.0) * (0.5 * two_over_h)).astype(BF16)
+    def sq_at(at, n):
+        return sq[:, pl.ds(pl.multiple_of(at * HALF, HALF), n)]
+
+    def upright(row):
+        return jnp.sum(eye * row, axis=1, keepdims=True)
+
+    def kernel_of(gram, col, row):
+        return jnp.exp(-jnp.maximum(col + row - 2.0 * gram, 0.0) * (0.5 * two_over_h))
+
+    def make_band(h, gram):
+        idx = 2 * me + h
+        row = sq_at(idx, WIDE)
+        kbuf[idx, :HALF, :] = kernel_of(gram[:HALF], upright(row[:, :HALF]), row).astype(BF16)
+        col = upright(sq_at(me, HALF))[h * (HALF // 2):(h + 1) * (HALF // 2)]
+        kbuf[idx, HALF:, :] = fold(kernel_of(unfold(gram[HALF:]), col, sq_at(me + n_blk, HALF))).astype(BF16)
 
     slots = iter(range(14))
     sent = []
@@ -594,21 +644,21 @@
     def spread(b, h):
         idx = 2 * b + h
         row0 = pl.multiple_of(idx * HALF, HALF)
-        for k in range(REACH * 2 - 1):
+        for k in range(WIDE // HALF):
             col0 = pl.multiple_of(lax.rem(idx + k, 2 * n_blk) * HALF, HALF)
-            tile = kbuf[idx, :, k * HALF:(k + 1) * HALF]
+            tile = kbuf[idx, :HALF, k * HALF:(k + 1) * HALF]
             kern_ref[pl.ds(row0, HALF), pl.ds(col0, HALF)] = tile
-            if 0 < k < REACH * 2 - 2:
+            if k > 0:
                 kern_ref[pl.ds(col0, HALF), pl.ds(row0, HALF)] = tile.T
 
     rs_copies["x_lo"].wait_recv()
     rs_copies["y_lo"].wait_recv()
-    kbuf[2 * me] = kernel_of(0, gbuf[0, 0] + (r_x1[1] + r_y2[...]))
+    make_band(0, gbuf[0, 0] + (r_x1[1] + r_y2[...]))
     for dev in (dev_y, sibling):
         send_band(2 * me, dev)
     rs_copies["y_hi"].wait_recv()
     rs_copies["x_hi"].wait_recv()
-    kbuf[2 * me + 1] = kernel_of(1, gbuf[0, 1] + (r_y1[1] + r_x2[...]))
+    make_band(1, gbuf[0, 1] + (r_y1[1] + r_x2[...]))
     for dev in (dev_x, sibling):
         send_band(2 * me + 1, dev)
     send_band(2 * me, dev_x)
@@ -639,9 +689,22 @@
     for rel, flip in others:
         recv_from(z_all, zb_recv, rel, flip).wait_recv()
     for b in range(n_blk):
+        tile = jnp.concatenate([unfold(kbuf[2 * b + h, HALF:, :].astype(F32)) for h in range(2)], axis=0)
+        near, away = slice(b * HALF, (b + 1) * HALF), slice((b + n_blk) * HALF, (b + n_blk + 1) * HALF)
+        kern_ref[near, away] = tile.astype(BF16)
+        kern_ref[away, near] = tile.T.astype(BF16)
+
+    def put(b):
+        rs = pl.ds(b * BLK, BLK)
+        return pltpu.make_async_copy(kern_ref.at[rs, :], kern_out.at[rs, :], kern_sem.at[b])
+
+    for b in range(n_blk):
         rs = slice(b * BLK, (b + 1) * BLK)
         zb_ref[rs, :] = z_all[b].astype(F32).T.astype(BF16)
         mass_ref[rs, :] = jnp.sum(kern_ref[rs, :].astype(F32), axis=1, keepdims=True)
+        put(b).start()
+    for b in range(n_blk):
+        put(b).wait()
     for rel in range(4):
         sib_copy(rel).wait_send()
     for cp in rs_copies.values():
@@ -659,20 +722,21 @@
     n_blk = n_rows // BLK
     dma = lambda *n: pltpu.SemaphoreType.DMA(n)
     scratch = [
-        pltpu.VMEM((4, 2, HALF, WIDE), F32), pltpu.VMEM((4, 2, HALF, WIDE), F32),
-        pltpu.VMEM((2, HALF, WIDE), F32), pltpu.VMEM((2, HALF, WIDE), F32),
-        pltpu.VMEM((HALF, WIDE), F32), pltpu.VMEM((HALF, WIDE), F32),
-        pltpu.VMEM((8, 4, 1, BLK), F32), pltpu.VMEM((1, n_rows + (REACH - 1) * BLK), F32),
+        pltpu.VMEM((4 if from_gram else 8, 2, TALL, WIDE), F32), pltpu.VMEM((4, 2, TALL, WIDE), F32),
+        pltpu.VMEM((2, TALL, WIDE), F32), pltpu.VMEM((2, TALL, WIDE), F32),
+        pltpu.VMEM((TALL, WIDE), F32), pltpu.VMEM((TALL, WIDE), F32),
+        pltpu.VMEM((8, 4, 1, BLK), F32), pltpu.VMEM((1, n_rows + WIDE), F32),
         pltpu.VMEM((n_blk, rank, BLK), F32), pltpu.VMEM((n_blk, rank, BLK), BF16),
-        pltpu.VMEM((2 * n_blk, HALF, WIDE), BF16),
-        dma(4), dma(4), dma(6), dma(6), dma(7), dma(8), dma(7), dma(8), dma(7), dma(8), dma(14), dma(16), dma(4)]
+        pltpu.VMEM((2 * n_blk, TALL, WIDE), BF16),
+        dma(4), dma(4), dma(6), dma(6), dma(7), dma(8), dma(7), dma(8), dma(7), dma(8), dma(14), dma(16), dma(4),
+        pltpu.VMEM((n_rows, n_rows), BF16), dma(n_blk)]
     if not from_gram:
-        scratch += [pltpu.VMEM(src.shape, BF16), pltpu.VMEM((4, 2, HALF, WIDE), F32), dma(n_blk)]
+        scratch += [pltpu.VMEM(src.shape, BF16), dma(n_blk)]
     return pl.pallas_call(
         functools.partial(kmat_kernel, from_gram, two_over_h),
         out_shape=(jax.ShapeDtypeStruct((n_rows, n_rows), BF16), jax.ShapeDtypeStruct((n_rows, rank), BF16),
                    jax.ShapeDtypeStruct((n_rows, 1), F32)),
-        in_specs=[ANY, VMEM], out_specs=(VMEM, VMEM, VMEM), scratch_shapes=scratch,
+        in_specs=[ANY, VMEM], out_specs=(ANY, VMEM, VMEM), scratch_shapes=scratch,
         compiler_params=pltpu.CompilerParams(collective_id=collective_id, has_side_effects=True, vmem_limit_bytes=VMEM_LIMIT),
     )(src, proj)
 

time: 1120 us -> 1110 us (level)
  waiting for transfers between devices: 214 us -> 202 us
    pallas_call x8, Pallas kernels: 121 us -> 137 us  [last_update(): pl.pallas_call(functools.partial(last_kernel, consts, start), grid_spec=p...]
    pallas_call x3, Pallas kernels: 239 us -> 225 us  [kernel_matrix(): pl.pallas_call(functools.partial(kmat_kernel, from_gram, two_over_h), out...]
    ppermute x8, waiting for transfers between devices: 211 us -> 198 us  [local_steps(): received.append(lax.ppermute(send, 'part', swap))]
  transfers between devices with their start and end apart: 10 -> 10, of which waited for: 9 -> 9; matrix products, arithmetic and copies ran while one was open for 0% -> 0% of each run, Pallas kernels for 19% -> 20%
where the time goes in v4:
time: 1110 us; the launch traced here: 1100 us
  Pallas kernels  886 us (80%)
  waiting for transfers between devices  202 us (18%)
    pallas_call x1, Pallas kernels, exchange(): pl.pallas_call(functools.partial(exchange_kernel, n_early, n_late), out_s...  292 us
    pallas_call x3, Pallas kernels, kernel_matrix(): pl.pallas_call(functools.partial(kmat_kernel, from_gram, two_over_h), out...  225 us
    ppermute x8, waiting for transfers between devices, local_steps(): received.append(lax.ppermute(send, 'part', swap))  198 us
    pallas_call x4, Pallas kernels, update(): pl.pallas_call(functools.partial(update_kernel, consts, first, split, bef...  179 us
    pallas_call x8, Pallas kernels, last_update(): pl.pallas_call(functools.partial(last_kernel, consts, start), grid_spec=p...  137 us
    pallas_call x2, Pallas kernels, own_update(): pl.pallas_call(functools.partial(own_kernel, consts, foreign), grid_spec=...  27.9 us
    pallas_call x8, Pallas kernels, place(): pl.pallas_call(place_kernel, grid_spec=pltpu.PrefetchScalarGridSpec(num_s...  24.7 us
  transfers between devices with their start and end apart: 10, of which 9 were waited for; matrix products, arithmetic and copies ran while one was open for 0% of the time, Pallas kernels for 20%

profile of v4, /device:TPU:0, one launch (start us, length us, event | category | flops | bytes accessed | tf_op | source)
XLA Modules:
  0.0 1098.8 jit_solution(10552688600006932775)
XLA Ops:
  0.0 292.1 %exchange.1 = (f32[2048,2816]{1,0:T(8,128)}, f32[1024,768]{1,0:T(8,128)}, f32[1024,768]{1,0:T(8,128)}, f32[8,2,136,1024]{3,2,1,0:T(8,128)}, f32[32,2048]{1,0:T(8,128)}) custom-call(f32[1024,7168]{1,0:T(8,128)} %theta_ref.1, f32[1,7168]{1,0:T(1,128)} %bitcast.19, bf16[32,7168]{1,0:T(8,128)(2,1)} %bitcast.4), custom_call_target="tpu_custom_call" | custom-call | tf_op jit(solution)/shard_map/exchange/pallas_call | solution.py:193
  292.1 71.3 %shard_map.46 = (bf16[2048,2048]{1,0:T(8,128)(2,1)}, bf16[2048,32]{1,0:T(8,128)(2,1)}, f32[2048,1]{1,0:T(8,128)}) custom-call(f32[8,2,136,1024]{3,2,1,0:T(8,128)} %get-tuple-element.51.src_ref, f32[32,2048]{1,0:T(8,128)} %get-tuple-element.52.proj_ref), custom_call_target="tpu_custom_call" | custom-call | tf_op jit(solution)/shard_map/pallas_call | solution.py:735
  363.4 0.9 collective-permute-start
  364.3 65.8 %shard_map.47 = (f32[2048,3584]{1,0:T(8,128)}, bf16[2048,3584]{1,0:T(8,128)(2,1)}, f32[32,2048]{1,0:T(8,128)}) custom-call(f32[2048,2816]{1,0:T(8,128)} %get-tuple-element.58.refs_0_.refs_1_, f32[2048,2816]{1,0:T(8,128)} %get-tuple-element.58.refs_0_.refs_1_, bf16[2048,2048]{1,0:T(8,128)(2,1)} %get-tuple-element.55.refs_2_.refs_4_, ...), custom_call_target="tpu_custom_call" | custom-call | flops 47244640256 | bytes 57671680 | tf_op jit(solution)/shard_map/pallas_call | solution.py:314
  430.1 4.6 collective-permute-done.refs_2_.refs_3_
  434.6 24.4 %shard_map.48 = (f32[2048,3584]{1,0:T(8,128)}, bf16[2048,3584]{1,0:T(8,128)(2,1)}, f32[32,2048]{1,0:T(8,128)}) custom-call(f32[1024,768]{1,0:T(8,128)} %get-tuple-element.49.refs_0_.refs_1_, f32[1024,768]{1,0:T(8,128)} %get-tuple-element.49.refs_0_.refs_1_, ...), custom_call_target="tpu_custom_call", output_to_operand_aliasing={{1}: (11, {}), {0}: (12, {})} | custom-call | flops 12884901888 | bytes 15728640 | tf_op jit(solution)/shard_map/pallas_call | solution.py:314
  459.1 76.8 %shard_map.49 = (bf16[2048,2048]{1,0:T(8,128)(2,1)}, bf16[2048,32]{1,0:T(8,128)(2,1)}, f32[2048,1]{1,0:T(8,128)}) custom-call(bf16[2048,3584]{1,0:T(8,128)(2,1)} %get-tuple-element.63.src_ref, f32[32,2048]{1,0:T(8,128)} %get-tuple-element.64.proj_ref), custom_call_target="tpu_custom_call" | custom-call | tf_op jit(solution)/shard_map/pallas_call | solution.py:735
  535.8 17.8 %shard_map.50 = (f32[2048,512]{1,0:T(8,128)}, bf16[2048,3584]{1,0:T(8,128)(2,1)}, f32[32,2048]{1,0:T(8,128)}) custom-call(f32[2048,3584]{1,0:T(8,128)} %get-tuple-element.62.refs_0_.refs_1_, f32[2048,3584]{1,0:T(8,128)} %get-tuple-element.62.refs_0_.refs_1_, bf16[2048,2048]{1,0:T(8,128)(2,1)} %get-tuple-element.65.refs_2_, ...), custom_call_target="tpu_custom_call" | custom-call | flops 8589934592 | bytes 10485760 | tf_op jit(solution)/shard_map/pallas_call | solution.py:314
  553.6 71.3 %shard_map.51 = (f32[2048,3584]{1,0:T(8,128)}, bf16[2048,3584]{1,0:T(8,128)(2,1)}, f32[32,2048]{1,0:T(8,128)}) custom-call(f32[2048,3584]{1,0:T(8,128)} %get-tuple-element.62.refs_0_.refs_1_, f32[2048,3584]{1,0:T(8,128)} %get-tuple-element.62.refs_0_.refs_1_, bf16[2048,2048]{1,0:T(8,128)(2,1)} %get-tuple-element.65.refs_2_, ...), custom_call_target="tpu_custom_call", output_to_operand_aliasing={{1}: (9, {})} | custom-call | flops 51539607552 | bytes 62914560 | tf_op jit(solution)/shard_map/pallas_call | solution.py:314
  624.9 77.1 %shard_map.52 = (bf16[2048,2048]{1,0:T(8,128)(2,1)}, bf16[2048,32]{1,0:T(8,128)(2,1)}, f32[2048,1]{1,0:T(8,128)}) custom-call(bf16[2048,3584]{1,0:T(8,128)(2,1)} %get-tuple-element.71.src_ref, f32[32,2048]{1,0:T(8,128)} %get-tuple-element.72.proj_ref), custom_call_target="tpu_custom_call" | custom-call | tf_op jit(solution)/shard_map/pallas_call | solution.py:735
  702.1 9.9 shard_map.53
  711.9 20.7 %shard_map.54 = (f32[1024,7168]{1,0:T(8,128)}, f32[1024,512]{1,0:T(8,128)}) custom-call(s32[1]{0:T(128)} %bitcast.pos_ref, f32[2048,3584]{1,0:T(8,128)} %get-tuple-element.70.theta_ref, bf16[2048,2048]{1,0:T(8,128)(2,1)} %get-tuple-element.73.kern_hbm.kern_ref, f32[2048,1]{1,0:T(8,128)} %get-tuple-element.74.mass_ref, ...), custom_call_target="tpu_custom_call", output_to_operand_aliasing={{0}: (8, {})} | custom-call | flops 8589934592 | bytes 10485760 | tf_op jit(solution)/shard_map/pallas_call | solution.py:376
  732.7 0.8 collective-permute-start.9
  733.5 20.5 %shard_map.55 = (f32[1024,7168]{1,0:T(8,128)}, f32[1024,512]{1,0:T(8,128)}) custom-call(s32[1]{0:T(128)} %bitcast.pos_ref, f32[2048,3584]{1,0:T(8,128)} %get-tuple-element.70.theta_ref, bf16[2048,2048]{1,0:T(8,128)(2,1)} %get-tuple-element.73.kern_hbm.kern_ref, f32[2048,1]{1,0:T(8,128)} %get-tuple-element.74.mass_ref, ...), custom_call_target="tpu_custom_call", output_to_operand_aliasing={{0}: (8, {})} | custom-call | flops 8589934592 | bytes 10485760 | tf_op jit(solution)/shard_map/pallas_call | solution.py:376
  754.0 1.2 collective-permute-start.8
  755.3 0.8 collective-permute-start.7
  756.1 1.2 collective-permute-start.6
  757.3 20.5 %shard_map.56 = (f32[1024,7168]{1,0:T(8,128)}, f32[1024,512]{1,0:T(8,128)}) custom-call(s32[1]{0:T(128)} %bitcast.pos_ref, f32[2048,3584]{1,0:T(8,128)} %get-tuple-element.70.theta_ref, bf16[2048,2048]{1,0:T(8,128)(2,1)} %get-tuple-element.73.kern_hbm.kern_ref, f32[2048,1]{1,0:T(8,128)} %get-tuple-element.74.mass_ref, ...), custom_call_target="tpu_custom_call", output_to_operand_aliasing={{0}: (8, {})} | custom-call | flops 8589934592 | bytes 10485760 | tf_op jit(solution)/shard_map/pallas_call | solution.py:376
  777.8 20.5 %shard_map.57 = (f32[1024,7168]{1,0:T(8,128)}, f32[1024,512]{1,0:T(8,128)}) custom-call(s32[1]{0:T(128)} %bitcast.pos_ref, f32[2048,3584]{1,0:T(8,128)} %get-tuple-element.70.theta_ref, bf16[2048,2048]{1,0:T(8,128)(2,1)} %get-tuple-element.73.kern_hbm.kern_ref, f32[2048,1]{1,0:T(8,128)} %get-tuple-element.74.mass_ref, ...), custom_call_target="tpu_custom_call", output_to_operand_aliasing={{0}: (8, {})} | custom-call | flops 8589934592 | bytes 10485760 | tf_op jit(solution)/shard_map/pallas_call | solution.py:376
  798.3 0.9 collective-permute-start.5
  799.2 38.4 %collective-permute-done.8.recv_ref = f32[1024,128]{1,0:T(8,128)S(1)} collective-permute-done((f32[1024,128]{1,0:T(8,128)}, f32[1024,128]{1,0:T(8,128)S(1)}, u32[]{:S(2)}, u32[]{:S(2)}) %collective-permute-start.8) | collective-permute-done | bytes 524320 | tf_op jit(solution)/shard_map/ppermute | solution.py:780
  837.6 0.8 collective-permute-start.4
  838.4 20.5 %shard_map.58 = (f32[1024,7168]{1,0:T(8,128)}, f32[1024,512]{1,0:T(8,128)}) custom-call(s32[1]{0:T(128)} %bitcast.pos_ref, f32[2048,3584]{1,0:T(8,128)} %get-tuple-element.70.theta_ref, bf16[2048,2048]{1,0:T(8,128)(2,1)} %get-tuple-element.73.kern_hbm.kern_ref, f32[2048,1]{1,0:T(8,128)} %get-tuple-element.74.mass_ref, ...), custom_call_target="tpu_custom_call", output_to_operand_aliasing={{0}: (8, {})} | custom-call | flops 8589934592 | bytes 10485760 | tf_op jit(solution)/shard_map/pallas_call | solution.py:376
  858.9 0.0 copy-done
  858.9 23.7 %collective-permute-done.7.recv_ref = f32[1024,512]{1,0:T(8,128)} collective-permute-done((f32[1024,512]{1,0:T(8,128)}, f32[1024,512]{1,0:T(8,128)}, u32[]{:S(2)}, u32[]{:S(2)}) %collective-permute-start.7) | collective-permute-done | bytes 2097184 | tf_op jit(solution)/shard_map/ppermute | solution.py:780
  882.6 0.8 collective-permute-start.3
  883.5 14.3 %shard_map.59 = (f32[1024,7168]{1,0:T(8,128)}, f32[1024,256]{1,0:T(8,128)}) custom-call(s32[1]{0:T(128)} %bitcast.pos_ref, f32[2048,3584]{1,0:T(8,128)} %get-tuple-element.70.theta_ref, bf16[2048,2048]{1,0:T(8,128)(2,1)} %get-tuple-element.73.kern_hbm.kern_ref, f32[2048,1]{1,0:T(8,128)} %get-tuple-element.74.mass_ref, ...), custom_call_target="tpu_custom_call", output_to_operand_aliasing={{0}: (8, {})} | custom-call | flops 4294967296 | bytes 5242880 | tf_op jit(solution)/shard_map/pallas_call | solution.py:376
  897.8 9.9 shard_map.60
  907.7 19.9 %collective-permute-done.6.recv_ref = f32[1024,512]{1,0:T(8,128)} collective-permute-done((f32[1024,512]{1,0:T(8,128)}, f32[1024,512]{1,0:T(8,128)}, u32[]{:S(2)}, u32[]{:S(2)}) %collective-permute-start.6) | collective-permute-done | bytes 2097184 | tf_op jit(solution)/shard_map/ppermute | solution.py:780
  927.6 0.8 collective-permute-start.2
  928.4 13.9 %own_shared.1.base_ref = f32[1024,7168]{1,0:T(8,128)} custom-call(s32[1]{0:T(128)} %bitcast.pos_ref, f32[2048,512]{1,0:T(8,128)} %get-tuple-element.91.theta_ref, bf16[2048,2048]{1,0:T(8,128)(2,1)} %get-tuple-element.73.kern_hbm.kern_ref, f32[2048,1]{1,0:T(8,128)} %get-tuple-element.74.mass_ref, ...), custom_call_target="tpu_custom_call", output_to_operand_aliasing={{}: (8, {})} | custom-call | flops 4294967296 | bytes 10485760 | tf_op jit(solution)/shard_map/own_shared/pallas_call | solution.py:413
  942.3 0.0 collective-permute-done.9.theta_ref
  942.3 1.2 collective-permute-start.1
  943.6 14.0 %own_foreign.1.base_ref = f32[1024,7168]{1,0:T(8,128)} custom-call(s32[1]{0:T(128)} %bitcast.pos_ref, f32[2048,512]{1,0:T(8,128)} %collective-permute-done.9.theta_ref, bf16[2048,2048]{1,0:T(8,128)(2,1)} %get-tuple-element.73.kern_hbm.kern_ref, f32[2048,1]{1,0:T(8,128)} %get-tuple-element.74.mass_ref, ...), custom_call_target="tpu_custom_call", output_to_operand_aliasing={{}: (8, {})} | custom-call | flops 4294967296 | bytes 10485760 | tf_op jit(solution)/shard_map/own_foreign/pallas_call | solution.py:413
  957.6 1.9 shard_map.61.base_ref
  959.4 3.8 shard_map.62.base_ref
  963.2 3.8 shard_map.63.base_ref
  967.0 5.6 collective-permute-done.5.recv_ref
  972.5 3.8 shard_map.64.base_ref
  976.3 41.2 %collective-permute-done.4.recv_ref = f32[1024,512]{1,0:T(8,128)} collective-permute-done((f32[1024,512]{1,0:T(8,128)}, f32[1024,512]{1,0:T(8,128)}, u32[]{:S(2)}, u32[]{:S(2)}) %collective-permute-start.4) | collective-permute-done | bytes 2097184 | tf_op jit(solution)/shard_map/ppermute | solution.py:780
  1017.5 3.8 shard_map.65.base_ref
  1021.2 41.2 %collective-permute-done.3.recv_ref = f32[1024,512]{1,0:T(8,128)} collective-permute-done((f32[1024,512]{1,0:T(8,128)}, f32[1024,512]{1,0:T(8,128)}, u32[]{:S(2)}, u32[]{:S(2)}) %collective-permute-start.3) | collective-permute-done | bytes 2097184 | tf_op jit(solution)/shard_map/ppermute | solution.py:780
  1062.4 3.8 shard_map.66.base_ref
  1066.2 18.7 %collective-permute-done.2.recv_ref = f32[1024,256]{1,0:T(8,128)} collective-permute-done((f32[1024,256]{1,0:T(8,128)}, f32[1024,256]{1,0:T(8,128)}, u32[]{:S(2)}, u32[]{:S(2)}) %collective-permute-start.2) | collective-permute-done | bytes 1048608 | tf_op jit(solution)/shard_map/ppermute | solution.py:780
  1084.9 2.0 shard_map.67.base_ref
  1086.9 9.0 collective-permute-done.1.recv_ref
  1095.9 0.8 copy-done.1
  1096.7 1.9 shard_map.68
  (2 shorter events, 0.0 us)
Async XLA Ops:
  363.4 71.2 %collective-permute-start = (f32[1024,768]{1,0:T(8,128)}, f32[1024,768]{1,0:T(8,128)}, u32[]{:S(2)}, u32[]{:S(2)}) collective-permute-start(f32[1024,768]{1,0:T(8,128)} %get-tuple-element.54), channel_id=1, source_target_pairs={{0,4},{4,0},{1,5},{5,1},{2,6},{6,2},{3,7},{7,3}} | collective-permute-start | bytes 9437192 | tf_op jit(solution)/shard_map/ppermute | solution.py:768
  732.7 209.7 %collective-permute-start.9 = (f32[2048,512]{1,0:T(8,128)}, f32[2048,512]{1,0:T(8,128)}, u32[]{:S(2)}, u32[]{:S(2)}) collective-permute-start(f32[2048,512]{1,0:T(8,128)} %get-tuple-element.91.theta_ref), channel_id=1, source_target_pairs={{0,4},{4,0},{1,5},{5,1},{2,6},{6,2},{3,7},{7,3}} | collective-permute-start | bytes 12582920 | tf_op jit(solution)/shard_map/ppermute | solution.py:773
  754.0 83.6 %collective-permute-start.8 = (f32[1024,128]{1,0:T(8,128)}, f32[1024,128]{1,0:T(8,128)S(1)}, u32[]{:S(2)}, u32[]{:S(2)}) collective-permute-start(f32[1024,128]{1,0:T(8,128)} %get-tuple-element.90), channel_id=1, source_target_pairs={{0,4},{4,0},{1,5},{5,1},{2,6},{6,2},{3,7},{7,3}} | collective-permute-start | bytes 1572872 | tf_op jit(solution)/shard_map/ppermute | solution.py:780
  755.3 127.4 %collective-permute-start.7 = (f32[1024,512]{1,0:T(8,128)}, f32[1024,512]{1,0:T(8,128)}, u32[]{:S(2)}, u32[]{:S(2)}) collective-permute-start(f32[1024,512]{1,0:T(8,128)} %get-tuple-element.89), channel_id=1, source_target_pairs={{0,4},{4,0},{1,5},{5,1},{2,6},{6,2},{3,7},{7,3}} | collective-permute-start | bytes 6291464 | tf_op jit(solution)/shard_map/ppermute | solution.py:780
  756.1 171.5 %collective-permute-start.6 = (f32[1024,512]{1,0:T(8,128)}, f32[1024,512]{1,0:T(8,128)}, u32[]{:S(2)}, u32[]{:S(2)}) collective-permute-start(f32[1024,512]{1,0:T(8,128)} %get-tuple-element.88), channel_id=1, source_target_pairs={{0,4},{4,0},{1,5},{5,1},{2,6},{6,2},{3,7},{7,3}} | collective-permute-start | bytes 6291464 | tf_op jit(solution)/shard_map/ppermute | solution.py:780
  798.3 174.2 %collective-permute-start.5 = (f32[1024,512]{1,0:T(8,128)}, f32[1024,512]{1,0:T(8,128)}, u32[]{:S(2)}, u32[]{:S(2)}) collective-permute-start(f32[1024,512]{1,0:T(8,128)} %get-tuple-element.87), channel_id=1, source_target_pairs={{0,4},{4,0},{1,5},{5,1},{2,6},{6,2},{3,7},{7,3}} | collective-permute-start | bytes 6291464 | tf_op jit(solution)/shard_map/ppermute | solution.py:780
  837.6 21.3 %copy-start = (f32[1024,128]{1,0:T(8,128)}, f32[1024,128]{1,0:T(8,128)S(1)}, u32[]{:S(2)}) copy-start(f32[1024,128]{1,0:T(8,128)S(1)} %collective-permute-done.8.recv_ref) | copy-start | bytes 1572868
  837.6 179.9 %collective-permute-start.4 = (f32[1024,512]{1,0:T(8,128)}, f32[1024,512]{1,0:T(8,128)}, u32[]{:S(2)}, u32[]{:S(2)}) collective-permute-start(f32[1024,512]{1,0:T(8,128)} %get-tuple-element.86), channel_id=1, source_target_pairs={{0,4},{4,0},{1,5},{5,1},{2,6},{6,2},{3,7},{7,3}} | collective-permute-start | bytes 6291464 | tf_op jit(solution)/shard_map/ppermute | solution.py:780
  882.6 179.8 %collective-permute-start.3 = (f32[1024,512]{1,0:T(8,128)}, f32[1024,512]{1,0:T(8,128)}, u32[]{:S(2)}, u32[]{:S(2)}) collective-permute-start(f32[1024,512]{1,0:T(8,128)} %get-tuple-element.85), channel_id=1, source_target_pairs={{0,4},{4,0},{1,5},{5,1},{2,6},{6,2},{3,7},{7,3}} | collective-permute-start | bytes 6291464 | tf_op jit(solution)/shard_map/ppermute | solution.py:780
  927.6 157.3 %collective-permute-start.2 = (f32[1024,256]{1,0:T(8,128)}, f32[1024,256]{1,0:T(8,128)}, u32[]{:S(2)}, u32[]{:S(2)}) collective-permute-start(f32[1024,256]{1,0:T(8,128)} %get-tuple-element.84), channel_id=1, source_target_pairs={{0,4},{4,0},{1,5},{5,1},{2,6},{6,2},{3,7},{7,3}} | collective-permute-start | bytes 3145736 | tf_op jit(solution)/shard_map/ppermute | solution.py:780
  942.3 153.6 %collective-permute-start.1 = (f32[1024,128]{1,0:T(8,128)}, f32[1024,128]{1,0:T(8,128)S(1)}, u32[]{:S(2)}, u32[]{:S(2)}) collective-permute-start(f32[1024,128]{1,0:T(8,128)} %get-tuple-element.83), channel_id=1, source_target_pairs={{0,4},{4,0},{1,5},{5,1},{2,6},{6,2},{3,7},{7,3}} | collective-permute-start | bytes 1572872 | tf_op jit(solution)/shard_map/ppermute | solution.py:780
  1095.9 0.8 copy-start.1

commit v5 on v4

--- a/solution.py
+++ b/solution.py
@@ -50,8 +50,8 @@
         yield h, slice(HALF, TALL), slice(0, WIDE), fold(far[h * (HALF // 2):(h + 1) * (HALF // 2)])
 
 
-def exchange_kernel(n_early, n_late, theta_ref, mean_ref, fact_ref, col_ref, late_own_ref, late_away_ref, gram_ref, proj_ref,
-                    buf, tb, away, away_b, late_b, send_sem, recv_sem, lsend_sem, lrecv_sem, own_sem, put_sem, other_sem):
+def exchange_body(n_early, n_late, theta_ref, mean_ref, fact_ref, col_ref, late_own_ref, late_away_ref, gram_ref, proj_ref,
+                  buf, tb, away, away_b, late_b, send_sem, recv_sem, lsend_sem, lrecv_sem, own_sem, put_sem, other_sem):
     part = lax.axis_index("part")
     other = 1 - part
     peer = (lax.axis_index("ens"), other, lax.axis_index("feat"))
@@ -59,9 +59,6 @@
     n_rows = col_ref.shape[0]
     cw = width // (n_early + n_late)
     n_blk = n_rows // BLK
-    barrier = pltpu.get_barrier_semaphore()
-    pl.semaphore_signal(barrier, inc=1, device_id=peer, device_id_type=MESH)
-    pl.semaphore_wait(barrier, 1)
     own_rows = pl.ds(pl.multiple_of(part * rows, BLK), rows)
     other_rows = pl.ds(pl.multiple_of(other * rows, BLK), rows)
 
@@ -182,30 +179,6 @@
     @pl.loop(0, n_late)
     def _(c):
         remote_late(c).wait_send()
-
-
-def exchange(theta, mean, fact_t, n_early, n_late):
-    rows, feat = theta.shape
-    width = feat // 2
-    n_rows = rows * 2
-    cw = width // (n_early + n_late)
-    dma = lambda *n: pltpu.SemaphoreType.DMA(n)
-    return pl.pallas_call(
-        functools.partial(exchange_kernel, n_early, n_late),
-        out_shape=(jax.ShapeDtypeStruct((n_rows, n_early * cw), F32),
-                   jax.ShapeDtypeStruct((rows, n_late * cw), F32),
-                   jax.ShapeDtypeStruct((rows, n_late * cw), F32),
-                   jax.ShapeDtypeStruct((n_rows // BLK, 2, TALL, WIDE), F32),
-                   jax.ShapeDtypeStruct((fact_t.shape[0], n_rows), F32)),
-        in_specs=[ANY, VMEM, VMEM], out_specs=(ANY, ANY, ANY, VMEM, VMEM),
-        scratch_shapes=[
-            pltpu.VMEM((n_rows, cw), F32), pltpu.VMEM((n_rows, cw), BF16), pltpu.VMEM((rows, cw), F32),
-            pltpu.VMEM((n_late, rows, cw), BF16), pltpu.VMEM((n_late, rows, cw), BF16),
-            dma(n_early), dma(n_early), dma(n_late), dma(n_late),
-            pltpu.SemaphoreType.DMA, pltpu.SemaphoreType.DMA, pltpu.SemaphoreType.DMA],
-        compiler_params=pltpu.CompilerParams(collective_id=0, has_side_effects=True, vmem_limit_bytes=VMEM_LIMIT),
-        name="exchange",
-    )(theta, mean, fact_t)
 
 
 def columns(half, start, tile, refs):
@@ -328,8 +301,13 @@
 
 def last_kernel(consts, start, pos_ref, theta_ref, kern_hbm, mass_ref, zb_ref, mean_ref, prec_ref, fact_ref, *rest):
     out_ref, send_ref, rhs, kern_ref, kern_sem = rest[-5:]
-    kern_copy = pltpu.make_async_copy(kern_hbm, kern_ref, kern_sem)
-    kern_copy.start()
+
+    def fetch(mine):
+        rs = pl.ds(pl.multiple_of(lax.rem(1 - pos_ref[0] + mine, 2) * out_ref.shape[0], BLK), out_ref.shape[0])
+        return pltpu.make_async_copy(kern_hbm.at[rs, :], kern_ref.at[rs, :], kern_sem.at[mine])
+
+    fetch(0).start()
+    fetch(1).start()
     rows = out_ref.shape[0]
     part = pos_ref[0]
     now = columns(part, start, theta_ref.shape[1], (mean_ref, prec_ref, fact_ref))
@@ -339,13 +317,17 @@
         rs = pl.ds(pl.multiple_of(b * rows, BLK), rows)
         build_rhs(theta_ref[rs, :], *now, zb_ref, rhs, rs)
 
-    kern_copy.wait()
     size = BLK if theta_ref.shape[1] < BLK else HALF
     each = rows // size
 
     @pl.loop(0, 2 * each)
     def _(b):
         mine = b // each
+
+        @pl.when(lax.rem(b, each) == 0)
+        def _():
+            fetch(mine).wait()
+
         at = pl.multiple_of(lax.rem(b, each) * size, size)
         rs = pl.ds(pl.multiple_of(lax.rem(1 - part + mine, 2) * rows + at, size), size)
         acc = jnp.dot(kern_ref[rs, :], rhs[...], preferred_element_type=F32)
@@ -379,7 +361,7 @@
             num_scalar_prefetch=1, grid=(1,), in_specs=in_specs,
             out_specs=(pl.BlockSpec((rows, tile), lambda i, pos: (0, pos[0] * per + chunk)),
                        pl.BlockSpec((rows, tile), lambda i, pos: (0, 0))),
-            scratch_shapes=[pltpu.VMEM((n_rows, 2 * tile), BF16), pltpu.VMEM(kern.shape, BF16), pltpu.SemaphoreType.DMA]),
+            scratch_shapes=[pltpu.VMEM((n_rows, 2 * tile), BF16), pltpu.VMEM(kern.shape, BF16), pltpu.SemaphoreType.DMA((2,))]),
         out_shape=(jax.ShapeDtypeStruct((rows, feat), F32), jax.ShapeDtypeStruct((rows, tile), F32)),
         input_output_aliases=alias,
         compiler_params=pltpu.CompilerParams(vmem_limit_bytes=VMEM_LIMIT),
@@ -445,12 +427,21 @@
     )(pos, recv, out)
 
 
-def kmat_kernel(from_gram, two_over_h, src_ref, proj_ref, kern_out, zb_ref, mass_ref, *scratch):
+def greet():
+    ens, part, feat = lax.axis_index("ens"), lax.axis_index("part"), lax.axis_index("feat")
+    barrier = pltpu.get_barrier_semaphore()
+    for i in range(1, 8):
+        there = (ens, lax.rem(part + i // 4, 2), lax.rem(feat + i % 4, 4))
+        pl.semaphore_signal(barrier, inc=1, device_id=there, device_id_type=MESH)
+    pl.semaphore_wait(barrier, 7)
+
+
+def kmat_body(from_gram, two_over_h, src_ref, proj_ref, kern_out, zb_ref, mass_ref, *scratch):
     if not from_gram:
         tb, load_sem = scratch[-2:]
     (gbuf, sib_in, r_x1, r_y1, r_x2, r_y2, sq_parts, sq, z_in, z_all, kbuf,
      sib_send, sib_recv, rs_send, rs_recv, sq_send, sq_recv, z_send, z_recv, zb_send, zb_recv,
-     k_send, k_recv, loc_sem, kern_ref, kern_sem) = scratch[:26]
+     k_send, k_recv, _, kern_ref, kern_sem) = scratch[:26]
     n_rows = kern_ref.shape[0]
     n_blk = n_rows // BLK
     ens, part, feat = lax.axis_index("ens"), lax.axis_index("part"), lax.axis_index("feat")
@@ -475,24 +466,14 @@
         return pltpu.make_async_remote_copy(src_ref=src, dst_ref=dst, send_sem=ssem, recv_sem=rsem,
                                             device_id=dev, device_id_type=MESH)
 
-    barrier = pltpu.get_barrier_semaphore()
-    for rel, flip in others:
-        pl.semaphore_signal(barrier, inc=1, device_id=device(rel, flip), device_id_type=MESH)
-
     def load(b):
         rs = pl.ds(b * BLK, BLK)
         return pltpu.make_async_copy(src_ref.at[rs, :], tb.at[rs, :], load_sem.at[b])
 
-    def own_gram(rel):
-        return pltpu.make_async_copy(src_ref.at[block(rel, 0)], gbuf.at[rel], loc_sem.at[rel])
-
-    if from_gram:
-        for rel in (3, 2, 1, 0):
-            own_gram(rel).start()
-    else:
+    if not from_gram:
         for b in range(n_blk):
             load(b).start()
-    pl.semaphore_wait(barrier, len(others))
+        greet()
 
     def z_cols(b):
         return proj_ref.at[:, pl.ds(pl.multiple_of(b * BLK, BLK), BLK)]
@@ -523,7 +504,7 @@
 
     def merge(rel):
         sib_copy(rel).wait_recv()
-        gbuf[rel] += sib_in[rel]
+        gbuf[rel] = src_ref[block(rel, 0)] + sib_in[rel]
 
     def first_sends(rel):
         for name in {3: ("d_lo", "d_hi"), 2: ("y_hi",), 1: ("x_lo",), 0: ()}[rel]:
@@ -533,7 +514,6 @@
         for rel in (3, 2, 1, 0):
             sib_copy(rel).start()
         for rel in (3, 2, 1, 0):
-            own_gram(rel).wait()
             merge(rel)
             first_sends(rel)
     else:
@@ -644,12 +624,14 @@
     def spread(b, h):
         idx = 2 * b + h
         row0 = pl.multiple_of(idx * HALF, HALF)
-        for k in range(WIDE // HALF):
+        kern_ref[pl.ds(row0, HALF), pl.ds(row0, HALF)] = kbuf[idx, :HALF, :HALF]
+
+        @pl.loop(1, WIDE // HALF)
+        def _(k):
             col0 = pl.multiple_of(lax.rem(idx + k, 2 * n_blk) * HALF, HALF)
-            tile = kbuf[idx, :HALF, k * HALF:(k + 1) * HALF]
+            tile = kbuf[idx, :HALF, pl.ds(pl.multiple_of(k * HALF, HALF), HALF)]
             kern_ref[pl.ds(row0, HALF), pl.ds(col0, HALF)] = tile
-            if k > 0:
-                kern_ref[pl.ds(col0, HALF), pl.ds(row0, HALF)] = tile.T
+            kern_ref[pl.ds(col0, HALF), pl.ds(row0, HALF)] = tile.T
 
     rs_copies["x_lo"].wait_recv()
     rs_copies["y_lo"].wait_recv()
@@ -688,23 +670,30 @@
         spread(b, h)
     for rel, flip in others:
         recv_from(z_all, zb_recv, rel, flip).wait_recv()
-    for b in range(n_blk):
+
+    @pl.loop(0, n_blk)
+    def _(b):
         tile = jnp.concatenate([unfold(kbuf[2 * b + h, HALF:, :].astype(F32)) for h in range(2)], axis=0)
-        near, away = slice(b * HALF, (b + 1) * HALF), slice((b + n_blk) * HALF, (b + n_blk + 1) * HALF)
+        near = pl.ds(pl.multiple_of(b * HALF, HALF), HALF)
+        away = pl.ds(pl.multiple_of((b + n_blk) * HALF, HALF), HALF)
         kern_ref[near, away] = tile.astype(BF16)
         kern_ref[away, near] = tile.T.astype(BF16)
 
     def put(b):
-        rs = pl.ds(b * BLK, BLK)
+        rs = pl.ds(pl.multiple_of(b * BLK, BLK), BLK)
         return pltpu.make_async_copy(kern_ref.at[rs, :], kern_out.at[rs, :], kern_sem.at[b])
 
-    for b in range(n_blk):
-        rs = slice(b * BLK, (b + 1) * BLK)
+    @pl.loop(0, n_blk)
+    def _(b):
+        rs = pl.ds(pl.multiple_of(b * BLK, BLK), BLK)
         zb_ref[rs, :] = z_all[b].astype(F32).T.astype(BF16)
         mass_ref[rs, :] = jnp.sum(kern_ref[rs, :].astype(F32), axis=1, keepdims=True)
         put(b).start()
-    for b in range(n_blk):
+
+    @pl.loop(0, n_blk)
+    def _(b):
         put(b).wait()
+
     for rel in range(4):
         sib_copy(rel).wait_send()
     for cp in rs_copies.values():
@@ -717,12 +706,11 @@
         cp.wait_send()
 
 
-def kernel_matrix(src, proj, two_over_h, collective_id, from_gram):
-    rank, n_rows = proj.shape
+def kmat_scratch(n_rows, rank, n_own):
     n_blk = n_rows // BLK
     dma = lambda *n: pltpu.SemaphoreType.DMA(n)
-    scratch = [
-        pltpu.VMEM((4 if from_gram else 8, 2, TALL, WIDE), F32), pltpu.VMEM((4, 2, TALL, WIDE), F32),
+    return [
+        pltpu.VMEM((n_own, 2, TALL, WIDE), F32), pltpu.VMEM((4, 2, TALL, WIDE), F32),
         pltpu.VMEM((2, TALL, WIDE), F32), pltpu.VMEM((2, TALL, WIDE), F32),
         pltpu.VMEM((TALL, WIDE), F32), pltpu.VMEM((TALL, WIDE), F32),
         pltpu.VMEM((8, 4, 1, BLK), F32), pltpu.VMEM((1, n_rows + WIDE), F32),
@@ -730,15 +718,52 @@
         pltpu.VMEM((2 * n_blk, TALL, WIDE), BF16),
         dma(4), dma(4), dma(6), dma(6), dma(7), dma(8), dma(7), dma(8), dma(7), dma(8), dma(14), dma(16), dma(4),
         pltpu.VMEM((n_rows, n_rows), BF16), dma(n_blk)]
-    if not from_gram:
-        scratch += [pltpu.VMEM(src.shape, BF16), dma(n_blk)]
+
+
+def kmat_shapes(n_rows, rank):
+    return (jax.ShapeDtypeStruct((n_rows, n_rows), BF16), jax.ShapeDtypeStruct((n_rows, rank), BF16),
+            jax.ShapeDtypeStruct((n_rows, 1), F32))
+
+
+def kernel_matrix(tb, proj, two_over_h, collective_id):
+    rank, n_rows = proj.shape
     return pl.pallas_call(
-        functools.partial(kmat_kernel, from_gram, two_over_h),
-        out_shape=(jax.ShapeDtypeStruct((n_rows, n_rows), BF16), jax.ShapeDtypeStruct((n_rows, rank), BF16),
-                   jax.ShapeDtypeStruct((n_rows, 1), F32)),
-        in_specs=[ANY, VMEM], out_specs=(ANY, VMEM, VMEM), scratch_shapes=scratch,
+        functools.partial(kmat_body, False, two_over_h),
+        out_shape=kmat_shapes(n_rows, rank), in_specs=[ANY, VMEM], out_specs=(ANY, VMEM, VMEM),
+        scratch_shapes=kmat_scratch(n_rows, rank, 8) + [pltpu.VMEM(tb.shape, BF16), pltpu.SemaphoreType.DMA((n_rows // BLK,))],
         compiler_params=pltpu.CompilerParams(collective_id=collective_id, has_side_effects=True, vmem_limit_bytes=VMEM_LIMIT),
-    )(src, proj)
+    )(tb, proj)
+
+
+def opening_kernel(n_early, n_late, two_over_h, theta_ref, mean_ref, fact_ref, col_ref, late_own_ref, late_away_ref,
+                   kern_out, zb_ref, mass_ref, gram, proj, *scratch):
+    greet()
+    exchange_body(n_early, n_late, theta_ref, mean_ref, fact_ref, col_ref, late_own_ref, late_away_ref, gram, proj, *scratch[:12])
+    kmat_body(True, two_over_h, gram, proj, kern_out, zb_ref, mass_ref, *scratch[12:])
+
+
+def opening(theta, mean, fact_t, two_over_h, n_early, n_late):
+    rows, feat = theta.shape
+    rank = fact_t.shape[0]
+    width = feat // 2
+    n_rows = rows * 2
+    cw = width // (n_early + n_late)
+    dma = lambda *n: pltpu.SemaphoreType.DMA(n)
+    return pl.pallas_call(
+        functools.partial(opening_kernel, n_early, n_late, two_over_h),
+        out_shape=(jax.ShapeDtypeStruct((n_rows, n_early * cw), F32),
+                   jax.ShapeDtypeStruct((rows, n_late * cw), F32),
+                   jax.ShapeDtypeStruct((rows, n_late * cw), F32)) + kmat_shapes(n_rows, rank),
+        in_specs=[ANY, VMEM, VMEM], out_specs=(ANY, ANY, ANY, ANY, VMEM, VMEM),
+        scratch_shapes=[
+            pltpu.VMEM((n_rows // BLK, 2, TALL, WIDE), F32), pltpu.VMEM((rank, n_rows), F32),
+            pltpu.VMEM((n_rows, cw), F32), pltpu.VMEM((n_rows, cw), BF16), pltpu.VMEM((rows, cw), F32),
+            pltpu.VMEM((n_late, rows, cw), BF16), pltpu.VMEM((n_late, rows, cw), BF16),
+            dma(n_early), dma(n_early), dma(n_late), dma(n_late),
+            pltpu.SemaphoreType.DMA, pltpu.SemaphoreType.DMA, pltpu.SemaphoreType.DMA] + kmat_scratch(n_rows, rank, 4),
+        compiler_params=pltpu.CompilerParams(collective_id=0, has_side_effects=True, vmem_limit_bytes=VMEM_LIMIT),
+        name="opening",
+    )(theta, mean, fact_t)
 
 
 def solution(mesh):
@@ -762,17 +787,15 @@
         late = 3 * BLK
         early = width - late
 
-        cur, late_own, late_away, gram, proj = exchange(theta, params[0], params[2], early // BLK, late // BLK)
-        kern, zb, mass = kernel_matrix(gram, proj, consts[1], 1, True)
-        late_away, mass = lax.optimization_barrier((late_away, mass))
+        cur, late_own, late_away, kern, zb, mass = opening(theta, params[0], params[2], consts[1], early // BLK, late // BLK)
         recv = lax.ppermute(late_away, "part", swap)
         new, tb, proj = update(consts, cur, kern, mass, zb, params, width, 0, early, False)
         cur, tb, proj = update(consts, (late_own, recv), kern, mass, zb, params, width, early, width, False, (tb, proj, new))
-        kern, zb, mass = kernel_matrix(tb, proj, consts[1], 2, False)
+        kern, zb, mass = kernel_matrix(tb, proj, consts[1], 2)
         both, tb, proj = update(consts, cur, kern, mass, zb, params, width, 0, shared, True)
         foreign = lax.ppermute(both, "part", swap)
         cur, tb, proj = update(consts, cur, kern, mass, zb, params, width, shared, width, False, (tb, proj))
-        kern, zb, mass = kernel_matrix(tb, proj, consts[1], 3, False)
+        kern, zb, mass = kernel_matrix(tb, proj, consts[1], 3)
         out = None
         received = []
         for start, tile in chunks:

time: 1110 us -> 1100 us (level)
    pallas_call x4 -> x3, Pallas kernels: 517 us -> 522 us  [the longest x1 362 us: opening(): pl.pallas_call(functools.partial(opening_kernel, n_early, n_late, two_ove...]
where the time goes in v5:
time: 1100 us
  Pallas kernels  881 us (80%)
  waiting for transfers between devices  203 us (18%)
  starting transfers between devices  12 us (1%)
    pallas_call x1, Pallas kernels, opening(): pl.pallas_call(functools.partial(opening_kernel, n_early, n_late, two_ove...  362 us
    ppermute x8, waiting for transfers between devices, local_steps(): received.append(lax.ppermute(send, 'part', swap))  200 us
    pallas_call x4, Pallas kernels, update(): pl.pallas_call(functools.partial(update_kernel, consts, first, split, bef...  179 us
    pallas_call x2, Pallas kernels, kernel_matrix(): pl.pallas_call(functools.partial(kmat_body, False, two_over_h), out_shape...  160 us
    pallas_call x8, Pallas kernels, last_update(): pl.pallas_call(functools.partial(last_kernel, consts, start), grid_spec=p...  128 us
    pallas_call x2, Pallas kernels, own_update(): pl.pallas_call(functools.partial(own_kernel, consts, foreign), grid_spec=...  28 us
    pallas_call x8, Pallas kernels, place(): pl.pallas_call(place_kernel, grid_spec=pltpu.PrefetchScalarGridSpec(num_s...  24.7 us
  transfers between devices with their start and end apart: 10, of which 9 were waited for; matrix products, arithmetic and copies ran while one was open for 0% of the time, Pallas kernels for 20%

profile of v5, /device:TPU:0, one launch (start us, length us, event | category | flops | bytes accessed | tf_op | source)
XLA Modules:
  0.0 1097.4 jit_solution(4945055331147123913)
XLA Ops:
  0.0 361.9 %opening.1 = (f32[2048,2816]{1,0:T(8,128)}, f32[1024,768]{1,0:T(8,128)}, f32[1024,768]{1,0:T(8,128)}, bf16[2048,2048]{1,0:T(8,128)(2,1)}, bf16[2048,32]{1,0:T(8,128)(2,1)}, /*index=5*/f32[2048,1]{1,0:T(8,128)}) custom-call(f32[1024,7168]{1,0:T(8,128)} %theta_ref.1, f32[1,7168]{1,0:T(1,128)} %bitcast.19, bf16[32,7168]{1,0:T(8,128)(2,1)} %bitcast.4), custom_call_target="tpu_custom_call" | custom-call | tf_op jit(solution)/shard_map/opening/pallas_call | solution.py:752
  361.9 1.2 collective-permute-start
  363.1 65.8 %shard_map.46 = (f32[2048,3584]{1,0:T(8,128)}, bf16[2048,3584]{1,0:T(8,128)(2,1)}, f32[32,2048]{1,0:T(8,128)}) custom-call(f32[2048,2816]{1,0:T(8,128)} %get-tuple-element.50.refs_0_.refs_1_, f32[2048,2816]{1,0:T(8,128)} %get-tuple-element.50.refs_0_.refs_1_, bf16[2048,2048]{1,0:T(8,128)(2,1)} %get-tuple-element.47.refs_2_.refs_4_, ...), custom_call_target="tpu_custom_call" | custom-call | flops 47244640256 | bytes 57671680 | tf_op jit(solution)/shard_map/pallas_call | solution.py:287
  428.9 3.2 collective-permute-done.refs_2_.refs_3_
  432.2 24.0 %shard_map.47 = (f32[2048,3584]{1,0:T(8,128)}, bf16[2048,3584]{1,0:T(8,128)(2,1)}, f32[32,2048]{1,0:T(8,128)}) custom-call(f32[1024,768]{1,0:T(8,128)} %get-tuple-element.45.refs_0_.refs_1_, f32[1024,768]{1,0:T(8,128)} %get-tuple-element.45.refs_0_.refs_1_, ...), custom_call_target="tpu_custom_call", output_to_operand_aliasing={{1}: (11, {}), {0}: (12, {})} | custom-call | flops 12884901888 | bytes 15728640 | tf_op jit(solution)/shard_map/pallas_call | solution.py:287
  456.1 80.3 %shard_map.48 = (bf16[2048,2048]{1,0:T(8,128)(2,1)}, bf16[2048,32]{1,0:T(8,128)(2,1)}, f32[2048,1]{1,0:T(8,128)}) custom-call(bf16[2048,3584]{1,0:T(8,128)(2,1)} %get-tuple-element.55.src_ref, f32[32,2048]{1,0:T(8,128)} %get-tuple-element.56.proj_ref), custom_call_target="tpu_custom_call" | custom-call | tf_op jit(solution)/shard_map/pallas_call | solution.py:730
  536.4 17.7 %shard_map.49 = (f32[2048,512]{1,0:T(8,128)}, bf16[2048,3584]{1,0:T(8,128)(2,1)}, f32[32,2048]{1,0:T(8,128)}) custom-call(f32[2048,3584]{1,0:T(8,128)} %get-tuple-element.54.refs_0_.refs_1_, f32[2048,3584]{1,0:T(8,128)} %get-tuple-element.54.refs_0_.refs_1_, bf16[2048,2048]{1,0:T(8,128)(2,1)} %get-tuple-element.57.refs_2_, ...), custom_call_target="tpu_custom_call" | custom-call | flops 8589934592 | bytes 10485760 | tf_op jit(solution)/shard_map/pallas_call | solution.py:287
  554.1 71.3 %shard_map.50 = (f32[2048,3584]{1,0:T(8,128)}, bf16[2048,3584]{1,0:T(8,128)(2,1)}, f32[32,2048]{1,0:T(8,128)}) custom-call(f32[2048,3584]{1,0:T(8,128)} %get-tuple-element.54.refs_0_.refs_1_, f32[2048,3584]{1,0:T(8,128)} %get-tuple-element.54.refs_0_.refs_1_, bf16[2048,2048]{1,0:T(8,128)(2,1)} %get-tuple-element.57.refs_2_, ...), custom_call_target="tpu_custom_call", output_to_operand_aliasing={{1}: (9, {})} | custom-call | flops 51539607552 | bytes 62914560 | tf_op jit(solution)/shard_map/pallas_call | solution.py:287
  625.4 80.1 %shard_map.51 = (bf16[2048,2048]{1,0:T(8,128)(2,1)}, bf16[2048,32]{1,0:T(8,128)(2,1)}, f32[2048,1]{1,0:T(8,128)}) custom-call(bf16[2048,3584]{1,0:T(8,128)(2,1)} %get-tuple-element.63.src_ref, f32[32,2048]{1,0:T(8,128)} %get-tuple-element.64.proj_ref), custom_call_target="tpu_custom_call" | custom-call | tf_op jit(solution)/shard_map/pallas_call | solution.py:730
  705.6 8.7 shard_map.52
  714.3 19.4 %shard_map.53 = (f32[1024,7168]{1,0:T(8,128)}, f32[1024,512]{1,0:T(8,128)}) custom-call(s32[1]{0:T(128)} %bitcast.pos_ref, f32[2048,3584]{1,0:T(8,128)} %get-tuple-element.62.theta_ref, bf16[2048,2048]{1,0:T(8,128)(2,1)} %get-tuple-element.65.kern_hbm.kern_ref, f32[2048,1]{1,0:T(8,128)} %get-tuple-element.66.mass_ref, ...), custom_call_target="tpu_custom_call", output_to_operand_aliasing={{0}: (8, {})} | custom-call | flops 8589934592 | bytes 10485760 | tf_op jit(solution)/shard_map/pallas_call | solution.py:358
  733.8 1.6 collective-permute-start.9
  735.3 19.4 %shard_map.54 = (f32[1024,7168]{1,0:T(8,128)}, f32[1024,512]{1,0:T(8,128)}) custom-call(s32[1]{0:T(128)} %bitcast.pos_ref, f32[2048,3584]{1,0:T(8,128)} %get-tuple-element.62.theta_ref, bf16[2048,2048]{1,0:T(8,128)(2,1)} %get-tuple-element.65.kern_hbm.kern_ref, f32[2048,1]{1,0:T(8,128)} %get-tuple-element.66.mass_ref, ...), custom_call_target="tpu_custom_call", output_to_operand_aliasing={{0}: (8, {})} | custom-call | flops 8589934592 | bytes 10485760 | tf_op jit(solution)/shard_map/pallas_call | solution.py:358
  754.7 0.5 collective-permute-start.8
  755.2 1.5 collective-permute-start.7
  756.8 0.5 collective-permute-start.6
  757.3 19.4 %shard_map.55 = (f32[1024,7168]{1,0:T(8,128)}, f32[1024,512]{1,0:T(8,128)}) custom-call(s32[1]{0:T(128)} %bitcast.pos_ref, f32[2048,3584]{1,0:T(8,128)} %get-tuple-element.62.theta_ref, bf16[2048,2048]{1,0:T(8,128)(2,1)} %get-tuple-element.65.kern_hbm.kern_ref, f32[2048,1]{1,0:T(8,128)} %get-tuple-element.66.mass_ref, ...), custom_call_target="tpu_custom_call", output_to_operand_aliasing={{0}: (8, {})} | custom-call | flops 8589934592 | bytes 10485760 | tf_op jit(solution)/shard_map/pallas_call | solution.py:358
  776.7 19.4 %shard_map.56 = (f32[1024,7168]{1,0:T(8,128)}, f32[1024,512]{1,0:T(8,128)}) custom-call(s32[1]{0:T(128)} %bitcast.pos_ref, f32[2048,3584]{1,0:T(8,128)} %get-tuple-element.62.theta_ref, bf16[2048,2048]{1,0:T(8,128)(2,1)} %get-tuple-element.65.kern_hbm.kern_ref, f32[2048,1]{1,0:T(8,128)} %get-tuple-element.66.mass_ref, ...), custom_call_target="tpu_custom_call", output_to_operand_aliasing={{0}: (8, {})} | custom-call | flops 8589934592 | bytes 10485760 | tf_op jit(solution)/shard_map/pallas_call | solution.py:358
  796.1 1.5 collective-permute-start.5
  797.7 41.0 %collective-permute-done.8.recv_ref = f32[1024,128]{1,0:T(8,128)S(1)} collective-permute-done((f32[1024,128]{1,0:T(8,128)}, f32[1024,128]{1,0:T(8,128)S(1)}, u32[]{:S(2)}, u32[]{:S(2)}) %collective-permute-start.8) | collective-permute-done | bytes 524320 | tf_op jit(solution)/shard_map/ppermute | solution.py:803
  838.7 0.0 copy-start
  838.7 1.5 collective-permute-start.4
  840.2 19.4 %shard_map.57 = (f32[1024,7168]{1,0:T(8,128)}, f32[1024,512]{1,0:T(8,128)}) custom-call(s32[1]{0:T(128)} %bitcast.pos_ref, f32[2048,3584]{1,0:T(8,128)} %get-tuple-element.62.theta_ref, bf16[2048,2048]{1,0:T(8,128)(2,1)} %get-tuple-element.65.kern_hbm.kern_ref, f32[2048,1]{1,0:T(8,128)} %get-tuple-element.66.mass_ref, ...), custom_call_target="tpu_custom_call", output_to_operand_aliasing={{0}: (8, {})} | custom-call | flops 8589934592 | bytes 10485760 | tf_op jit(solution)/shard_map/pallas_call | solution.py:358
  859.6 0.0 copy-done
  859.6 24.1 %collective-permute-done.7.recv_ref = f32[1024,512]{1,0:T(8,128)} collective-permute-done((f32[1024,512]{1,0:T(8,128)}, f32[1024,512]{1,0:T(8,128)}, u32[]{:S(2)}, u32[]{:S(2)}) %collective-permute-start.7) | collective-permute-done | bytes 2097184 | tf_op jit(solution)/shard_map/ppermute | solution.py:803
  883.7 1.5 collective-permute-start.3
  885.2 13.3 %shard_map.58 = (f32[1024,7168]{1,0:T(8,128)}, f32[1024,256]{1,0:T(8,128)}) custom-call(s32[1]{0:T(128)} %bitcast.pos_ref, f32[2048,3584]{1,0:T(8,128)} %get-tuple-element.62.theta_ref, bf16[2048,2048]{1,0:T(8,128)(2,1)} %get-tuple-element.65.kern_hbm.kern_ref, f32[2048,1]{1,0:T(8,128)} %get-tuple-element.66.mass_ref, ...), custom_call_target="tpu_custom_call", output_to_operand_aliasing={{0}: (8, {})} | custom-call | flops 4294967296 | bytes 5242880 | tf_op jit(solution)/shard_map/pallas_call | solution.py:358
  898.5 8.7 shard_map.59
  907.2 21.4 %collective-permute-done.6.recv_ref = f32[1024,512]{1,0:T(8,128)} collective-permute-done((f32[1024,512]{1,0:T(8,128)}, f32[1024,512]{1,0:T(8,128)}, u32[]{:S(2)}, u32[]{:S(2)}) %collective-permute-start.6) | collective-permute-done | bytes 2097184 | tf_op jit(solution)/shard_map/ppermute | solution.py:803
  928.7 1.5 collective-permute-start.2
  930.2 14.0 %own_shared.1.base_ref = f32[1024,7168]{1,0:T(8,128)} custom-call(s32[1]{0:T(128)} %bitcast.pos_ref, f32[2048,512]{1,0:T(8,128)} %get-tuple-element.83.theta_ref, bf16[2048,2048]{1,0:T(8,128)(2,1)} %get-tuple-element.65.kern_hbm.kern_ref, f32[2048,1]{1,0:T(8,128)} %get-tuple-element.66.mass_ref, ...), custom_call_target="tpu_custom_call", output_to_operand_aliasing={{}: (8, {})} | custom-call | flops 4294967296 | bytes 10485760 | tf_op jit(solution)/shard_map/own_shared/pallas_call | solution.py:395
  944.1 0.0 collective-permute-done.9.theta_ref
  944.1 0.5 collective-permute-start.1
  944.6 14.0 %own_foreign.1.base_ref = f32[1024,7168]{1,0:T(8,128)} custom-call(s32[1]{0:T(128)} %bitcast.pos_ref, f32[2048,512]{1,0:T(8,128)} %collective-permute-done.9.theta_ref, bf16[2048,2048]{1,0:T(8,128)(2,1)} %get-tuple-element.65.kern_hbm.kern_ref, f32[2048,1]{1,0:T(8,128)} %get-tuple-element.66.mass_ref, ...), custom_call_target="tpu_custom_call", output_to_operand_aliasing={{}: (8, {})} | custom-call | flops 4294967296 | bytes 10485760 | tf_op jit(solution)/shard_map/own_foreign/pallas_call | solution.py:395
  958.7 1.9 shard_map.60.base_ref
  960.5 3.8 shard_map.61.base_ref
  964.3 3.8 shard_map.62.base_ref
  968.1 5.5 collective-permute-done.5.recv_ref
  973.6 3.8 shard_map.63.base_ref
  977.4 41.2 %collective-permute-done.4.recv_ref = f32[1024,512]{1,0:T(8,128)} collective-permute-done((f32[1024,512]{1,0:T(8,128)}, f32[1024,512]{1,0:T(8,128)}, u32[]{:S(2)}, u32[]{:S(2)}) %collective-permute-start.4) | collective-permute-done | bytes 2097184 | tf_op jit(solution)/shard_map/ppermute | solution.py:803
  1018.5 3.8 shard_map.64.base_ref
  1022.3 41.2 %collective-permute-done.3.recv_ref = f32[1024,512]{1,0:T(8,128)} collective-permute-done((f32[1024,512]{1,0:T(8,128)}, f32[1024,512]{1,0:T(8,128)}, u32[]{:S(2)}, u32[]{:S(2)}) %collective-permute-start.3) | collective-permute-done | bytes 2097184 | tf_op jit(solution)/shard_map/ppermute | solution.py:803
  1063.5 3.8 shard_map.65.base_ref
  1067.3 18.7 %collective-permute-done.2.recv_ref = f32[1024,256]{1,0:T(8,128)} collective-permute-done((f32[1024,256]{1,0:T(8,128)}, f32[1024,256]{1,0:T(8,128)}, u32[]{:S(2)}, u32[]{:S(2)}) %collective-permute-start.2) | collective-permute-done | bytes 1048608 | tf_op jit(solution)/shard_map/ppermute | solution.py:803
  1085.9 2.0 shard_map.66.base_ref
  1088.0 6.7 collective-permute-done.1.recv_ref
  1094.7 0.8 copy-done.1
  1095.5 1.9 shard_map.67
  (1 shorter events, 0.0 us)
Async XLA Ops:
  361.9 70.2 %collective-permute-start = (f32[1024,768]{1,0:T(8,128)}, f32[1024,768]{1,0:T(8,128)}, u32[]{:S(2)}, u32[]{:S(2)}) collective-permute-start(f32[1024,768]{1,0:T(8,128)} %get-tuple-element.46), channel_id=1, source_target_pairs={{0,4},{4,0},{1,5},{5,1},{2,6},{6,2},{3,7},{7,3}} | collective-permute-start | bytes 9437192 | tf_op jit(solution)/shard_map/ppermute | solution.py:791
  733.8 210.4 %collective-permute-start.9 = (f32[2048,512]{1,0:T(8,128)}, f32[2048,512]{1,0:T(8,128)}, u32[]{:S(2)}, u32[]{:S(2)}) collective-permute-start(f32[2048,512]{1,0:T(8,128)} %get-tuple-element.83.theta_ref), channel_id=1, source_target_pairs={{0,4},{4,0},{1,5},{5,1},{2,6},{6,2},{3,7},{7,3}} | collective-permute-start | bytes 12582920 | tf_op jit(solution)/shard_map/ppermute | solution.py:796
  754.7 83.9 %collective-permute-start.8 = (f32[1024,128]{1,0:T(8,128)}, f32[1024,128]{1,0:T(8,128)S(1)}, u32[]{:S(2)}, u32[]{:S(2)}) collective-permute-start(f32[1024,128]{1,0:T(8,128)} %get-tuple-element.82), channel_id=1, source_target_pairs={{0,4},{4,0},{1,5},{5,1},{2,6},{6,2},{3,7},{7,3}} | collective-permute-start | bytes 1572872 | tf_op jit(solution)/shard_map/ppermute | solution.py:803
  755.2 128.5 %collective-permute-start.7 = (f32[1024,512]{1,0:T(8,128)}, f32[1024,512]{1,0:T(8,128)}, u32[]{:S(2)}, u32[]{:S(2)}) collective-permute-start(f32[1024,512]{1,0:T(8,128)} %get-tuple-element.81), channel_id=1, source_target_pairs={{0,4},{4,0},{1,5},{5,1},{2,6},{6,2},{3,7},{7,3}} | collective-permute-start | bytes 6291464 | tf_op jit(solution)/shard_map/ppermute | solution.py:803
  756.8 171.9 %collective-permute-start.6 = (f32[1024,512]{1,0:T(8,128)}, f32[1024,512]{1,0:T(8,128)}, u32[]{:S(2)}, u32[]{:S(2)}) collective-permute-start(f32[1024,512]{1,0:T(8,128)} %get-tuple-element.80), channel_id=1, source_target_pairs={{0,4},{4,0},{1,5},{5,1},{2,6},{6,2},{3,7},{7,3}} | collective-permute-start | bytes 6291464 | tf_op jit(solution)/shard_map/ppermute | solution.py:803
  796.1 177.5 %collective-permute-start.5 = (f32[1024,512]{1,0:T(8,128)}, f32[1024,512]{1,0:T(8,128)}, u32[]{:S(2)}, u32[]{:S(2)}) collective-permute-start(f32[1024,512]{1,0:T(8,128)} %get-tuple-element.79), channel_id=1, source_target_pairs={{0,4},{4,0},{1,5},{5,1},{2,6},{6,2},{3,7},{7,3}} | collective-permute-start | bytes 6291464 | tf_op jit(solution)/shard_map/ppermute | solution.py:803
  838.7 21.0 %copy-start = (f32[1024,128]{1,0:T(8,128)}, f32[1024,128]{1,0:T(8,128)S(1)}, u32[]{:S(2)}) copy-start(f32[1024,128]{1,0:T(8,128)S(1)} %collective-permute-done.8.recv_ref) | copy-start | bytes 1572868
  838.7 179.9 %collective-permute-start.4 = (f32[1024,512]{1,0:T(8,128)}, f32[1024,512]{1,0:T(8,128)}, u32[]{:S(2)}, u32[]{:S(2)}) collective-permute-start(f32[1024,512]{1,0:T(8,128)} %get-tuple-element.78), channel_id=1, source_target_pairs={{0,4},{4,0},{1,5},{5,1},{2,6},{6,2},{3,7},{7,3}} | collective-permute-start | bytes 6291464 | tf_op jit(solution)/shard_map/ppermute | solution.py:803
  883.7 179.8 %collective-permute-start.3 = (f32[1024,512]{1,0:T(8,128)}, f32[1024,512]{1,0:T(8,128)}, u32[]{:S(2)}, u32[]{:S(2)}) collective-permute-start(f32[1024,512]{1,0:T(8,128)} %get-tuple-element.77), channel_id=1, source_target_pairs={{0,4},{4,0},{1,5},{5,1},{2,6},{6,2},{3,7},{7,3}} | collective-permute-start | bytes 6291464 | tf_op jit(solution)/shard_map/ppermute | solution.py:803
  928.7 157.3 %collective-permute-start.2 = (f32[1024,256]{1,0:T(8,128)}, f32[1024,256]{1,0:T(8,128)}, u32[]{:S(2)}, u32[]{:S(2)}) collective-permute-start(f32[1024,256]{1,0:T(8,128)} %get-tuple-element.76), channel_id=1, source_target_pairs={{0,4},{4,0},{1,5},{5,1},{2,6},{6,2},{3,7},{7,3}} | collective-permute-start | bytes 3145736 | tf_op jit(solution)/shard_map/ppermute | solution.py:803
  944.1 150.5 %collective-permute-start.1 = (f32[1024,128]{1,0:T(8,128)}, f32[1024,128]{1,0:T(8,128)S(1)}, u32[]{:S(2)}, u32[]{:S(2)}) collective-permute-start(f32[1024,128]{1,0:T(8,128)} %get-tuple-element.75), channel_id=1, source_target_pairs={{0,4},{4,0},{1,5},{5,1},{2,6},{6,2},{3,7},{7,3}} | collective-permute-start | bytes 1572872 | tf_op jit(solution)/shard_map/ppermute | solution.py:803
  1094.7 0.8 copy-start.1

commit v6 on v5

--- a/solution.py
+++ b/solution.py
@@ -427,12 +427,13 @@
     )(pos, recv, out)
 
 
-def greet():
+def greet(between=lambda: None):
     ens, part, feat = lax.axis_index("ens"), lax.axis_index("part"), lax.axis_index("feat")
     barrier = pltpu.get_barrier_semaphore()
     for i in range(1, 8):
         there = (ens, lax.rem(part + i // 4, 2), lax.rem(feat + i % 4, 4))
         pl.semaphore_signal(barrier, inc=1, device_id=there, device_id_type=MESH)
+    between()
     pl.semaphore_wait(barrier, 7)
 
 
@@ -471,9 +472,11 @@
         return pltpu.make_async_copy(src_ref.at[rs, :], tb.at[rs, :], load_sem.at[b])
 
     if not from_gram:
-        for b in range(n_blk):
-            load(b).start()
-        greet()
+        def load_all():
+            for b in range(n_blk):
+                load(b).start()
+
+        greet(load_all)
 
     def z_cols(b):
         return proj_ref.at[:, pl.ds(pl.multiple_of(b * BLK, BLK), BLK)]
@@ -621,17 +624,29 @@
     def wait_band(idx):
         rcopy(kbuf.at[idx], kbuf.at[idx], k_send.at[0], k_recv.at[idx], sibling).wait_recv()
 
-    def spread(b, h):
+    def spread(b, h, unroll=False):
         idx = 2 * b + h
         row0 = pl.multiple_of(idx * HALF, HALF)
         kern_ref[pl.ds(row0, HALF), pl.ds(row0, HALF)] = kbuf[idx, :HALF, :HALF]
 
-        @pl.loop(1, WIDE // HALF)
-        def _(k):
+        def move(k):
             col0 = pl.multiple_of(lax.rem(idx + k, 2 * n_blk) * HALF, HALF)
             tile = kbuf[idx, :HALF, pl.ds(pl.multiple_of(k * HALF, HALF), HALF)]
             kern_ref[pl.ds(row0, HALF), pl.ds(col0, HALF)] = tile
             kern_ref[pl.ds(col0, HALF), pl.ds(row0, HALF)] = tile.T
+
+        if unroll:
+            for k in range(1, WIDE // HALF):
+                move(k)
+        else:
+            pl.loop(1, WIDE // HALF)(move)
+
+    def spread_far(b):
+        tile = jnp.concatenate([unfold(kbuf[2 * b + h, HALF:, :].astype(F32)) for h in range(2)], axis=0)
+        near = pl.ds(pl.multiple_of(b * HALF, HALF), HALF)
+        away = pl.ds(pl.multiple_of((b + n_blk) * HALF, HALF), HALF)
+        kern_ref[near, away] = tile.astype(BF16)
+        kern_ref[away, near] = tile.T.astype(BF16)
 
     rs_copies["x_lo"].wait_recv()
     rs_copies["y_lo"].wait_recv()
@@ -660,24 +675,37 @@
     send_band(2 * bx + 1, sibling)
     spread(by, 0)
     spread(bx, 1)
-    for b, h in ((bx, 0), (by, 1), (bd, 0), (bd, 1)):
+    for b, h in ((bx, 0), (by, 1)):
         wait_band(2 * b + h)
         send_band(2 * b + h, sibling)
         spread(b, h)
-    for rel, h in ((2, 0), (1, 1), (1, 0), (2, 1), (3, 0), (3, 1)):
+    for rel, h in ((2, 0), (1, 1)):
         b = block(rel, 1)
         wait_band(2 * b + h)
         spread(b, h)
+    for h in range(2):
+        wait_band(2 * bd + h)
+        send_band(2 * bd + h, sibling)
+        spread(bd, h)
+    for rel, h in ((1, 0), (2, 1)):
+        b = block(rel, 1)
+        wait_band(2 * b + h)
+        spread(b, h)
+
+    @pl.loop(0, 6)
+    def _(i):
+        rel = i // 2
+        cy, cx = lax.rem(part + rel // 2, 2), lax.rem(x + lax.rem(rel, 2), 2)
+        spread_far(cy * 4 + cx * 2 + lax.rem(i, 2))
+
+    spread_far(bd)
+    last = block(3, 1)
+    for h in range(2):
+        wait_band(2 * last + h)
+        spread(last, h, True)
+    spread_far(last)
     for rel, flip in others:
         recv_from(z_all, zb_recv, rel, flip).wait_recv()
-
-    @pl.loop(0, n_blk)
-    def _(b):
-        tile = jnp.concatenate([unfold(kbuf[2 * b + h, HALF:, :].astype(F32)) for h in range(2)], axis=0)
-        near = pl.ds(pl.multiple_of(b * HALF, HALF), HALF)
-        away = pl.ds(pl.multiple_of((b + n_blk) * HALF, HALF), HALF)
-        kern_ref[near, away] = tile.astype(BF16)
-        kern_ref[away, near] = tile.T.astype(BF16)
 
     def put(b):
         rs = pl.ds(pl.multiple_of(b * BLK, BLK), BLK)

time: 1100 us -> 1090 us (level)
  no operation moved by 1% of the time
where the time goes in v6:
time: 1090 us
  Pallas kernels  876 us (80%)
  waiting for transfers between devices  203 us (19%)
  starting transfers between devices  11.9 us (1%)
    pallas_call x1, Pallas kernels, opening(): pl.pallas_call(functools.partial(opening_kernel, n_early, n_late, two_ove...  360 us
    ppermute x8, waiting for transfers between devices, local_steps(): received.append(lax.ppermute(send, 'part', swap))  200 us
    pallas_call x4, Pallas kernels, update(): pl.pallas_call(functools.partial(update_kernel, consts, first, split, bef...  179 us
    pallas_call x2, Pallas kernels, kernel_matrix(): pl.pallas_call(functools.partial(kmat_body, False, two_over_h), out_shape...  157 us
    pallas_call x8, Pallas kernels, last_update(): pl.pallas_call(functools.partial(last_kernel, consts, start), grid_spec=p...  128 us
    pallas_call x2, Pallas kernels, own_update(): pl.pallas_call(functools.partial(own_kernel, consts, foreign), grid_spec=...  28 us
    pallas_call x8, Pallas kernels, place(): pl.pallas_call(place_kernel, grid_spec=pltpu.PrefetchScalarGridSpec(num_s...  24.7 us
  transfers between devices with their start and end apart: 10, of which 9 were waited for; matrix products, arithmetic and copies ran while one was open for 0% of the time, Pallas kernels for 20%

profile of v6, /device:TPU:0, one launch (start us, length us, event | category | flops | bytes accessed | tf_op | source)
XLA Modules:
  0.0 1092.2 jit_solution(13136754637417394649)
XLA Ops:
  0.0 360.1 %opening.1 = (f32[2048,2816]{1,0:T(8,128)}, f32[1024,768]{1,0:T(8,128)}, f32[1024,768]{1,0:T(8,128)}, bf16[2048,2048]{1,0:T(8,128)(2,1)}, bf16[2048,32]{1,0:T(8,128)(2,1)}, /*index=5*/f32[2048,1]{1,0:T(8,128)}) custom-call(f32[1024,7168]{1,0:T(8,128)} %theta_ref.1, f32[1,7168]{1,0:T(1,128)} %bitcast.19, bf16[32,7168]{1,0:T(8,128)(2,1)} %bitcast.4), custom_call_target="tpu_custom_call" | custom-call | tf_op jit(solution)/shard_map/opening/pallas_call | solution.py:780
  360.1 1.2 collective-permute-start
  361.3 65.8 %shard_map.46 = (f32[2048,3584]{1,0:T(8,128)}, bf16[2048,3584]{1,0:T(8,128)(2,1)}, f32[32,2048]{1,0:T(8,128)}) custom-call(f32[2048,2816]{1,0:T(8,128)} %get-tuple-element.50.refs_0_.refs_1_, f32[2048,2816]{1,0:T(8,128)} %get-tuple-element.50.refs_0_.refs_1_, bf16[2048,2048]{1,0:T(8,128)(2,1)} %get-tuple-element.47.refs_2_.refs_4_, ...), custom_call_target="tpu_custom_call" | custom-call | flops 47244640256 | bytes 57671680 | tf_op jit(solution)/shard_map/pallas_call | solution.py:287
  427.1 3.2 collective-permute-done.refs_2_.refs_3_
  430.3 24.0 %shard_map.47 = (f32[2048,3584]{1,0:T(8,128)}, bf16[2048,3584]{1,0:T(8,128)(2,1)}, f32[32,2048]{1,0:T(8,128)}) custom-call(f32[1024,768]{1,0:T(8,128)} %get-tuple-element.45.refs_0_.refs_1_, f32[1024,768]{1,0:T(8,128)} %get-tuple-element.45.refs_0_.refs_1_, ...), custom_call_target="tpu_custom_call", output_to_operand_aliasing={{1}: (11, {}), {0}: (12, {})} | custom-call | flops 12884901888 | bytes 15728640 | tf_op jit(solution)/shard_map/pallas_call | solution.py:287
  454.3 78.4 %shard_map.48 = (bf16[2048,2048]{1,0:T(8,128)(2,1)}, bf16[2048,32]{1,0:T(8,128)(2,1)}, f32[2048,1]{1,0:T(8,128)}) custom-call(bf16[2048,3584]{1,0:T(8,128)(2,1)} %get-tuple-element.55.src_ref, f32[32,2048]{1,0:T(8,128)} %get-tuple-element.56.proj_ref), custom_call_target="tpu_custom_call" | custom-call | tf_op jit(solution)/shard_map/pallas_call | solution.py:758
  532.8 17.7 %shard_map.49 = (f32[2048,512]{1,0:T(8,128)}, bf16[2048,3584]{1,0:T(8,128)(2,1)}, f32[32,2048]{1,0:T(8,128)}) custom-call(f32[2048,3584]{1,0:T(8,128)} %get-tuple-element.54.refs_0_.refs_1_, f32[2048,3584]{1,0:T(8,128)} %get-tuple-element.54.refs_0_.refs_1_, bf16[2048,2048]{1,0:T(8,128)(2,1)} %get-tuple-element.57.refs_2_, ...), custom_call_target="tpu_custom_call" | custom-call | flops 8589934592 | bytes 10485760 | tf_op jit(solution)/shard_map/pallas_call | solution.py:287
  550.5 71.3 %shard_map.50 = (f32[2048,3584]{1,0:T(8,128)}, bf16[2048,3584]{1,0:T(8,128)(2,1)}, f32[32,2048]{1,0:T(8,128)}) custom-call(f32[2048,3584]{1,0:T(8,128)} %get-tuple-element.54.refs_0_.refs_1_, f32[2048,3584]{1,0:T(8,128)} %get-tuple-element.54.refs_0_.refs_1_, bf16[2048,2048]{1,0:T(8,128)(2,1)} %get-tuple-element.57.refs_2_, ...), custom_call_target="tpu_custom_call", output_to_operand_aliasing={{1}: (9, {})} | custom-call | flops 51539607552 | bytes 62914560 | tf_op jit(solution)/shard_map/pallas_call | solution.py:287
  621.8 78.3 %shard_map.51 = (bf16[2048,2048]{1,0:T(8,128)(2,1)}, bf16[2048,32]{1,0:T(8,128)(2,1)}, f32[2048,1]{1,0:T(8,128)}) custom-call(bf16[2048,3584]{1,0:T(8,128)(2,1)} %get-tuple-element.63.src_ref, f32[32,2048]{1,0:T(8,128)} %get-tuple-element.64.proj_ref), custom_call_target="tpu_custom_call" | custom-call | tf_op jit(solution)/shard_map/pallas_call | solution.py:758
  700.1 8.7 shard_map.52
  708.8 19.4 %shard_map.53 = (f32[1024,7168]{1,0:T(8,128)}, f32[1024,512]{1,0:T(8,128)}) custom-call(s32[1]{0:T(128)} %bitcast.pos_ref, f32[2048,3584]{1,0:T(8,128)} %get-tuple-element.62.theta_ref, bf16[2048,2048]{1,0:T(8,128)(2,1)} %get-tuple-element.65.kern_hbm.kern_ref, f32[2048,1]{1,0:T(8,128)} %get-tuple-element.66.mass_ref, ...), custom_call_target="tpu_custom_call", output_to_operand_aliasing={{0}: (8, {})} | custom-call | flops 8589934592 | bytes 10485760 | tf_op jit(solution)/shard_map/pallas_call | solution.py:358
  728.3 1.5 collective-permute-start.9
  729.8 19.4 %shard_map.54 = (f32[1024,7168]{1,0:T(8,128)}, f32[1024,512]{1,0:T(8,128)}) custom-call(s32[1]{0:T(128)} %bitcast.pos_ref, f32[2048,3584]{1,0:T(8,128)} %get-tuple-element.62.theta_ref, bf16[2048,2048]{1,0:T(8,128)(2,1)} %get-tuple-element.65.kern_hbm.kern_ref, f32[2048,1]{1,0:T(8,128)} %get-tuple-element.66.mass_ref, ...), custom_call_target="tpu_custom_call", output_to_operand_aliasing={{0}: (8, {})} | custom-call | flops 8589934592 | bytes 10485760 | tf_op jit(solution)/shard_map/pallas_call | solution.py:358
  749.2 0.5 collective-permute-start.8
  749.8 1.5 collective-permute-start.7
  751.3 0.5 collective-permute-start.6
  751.8 19.4 %shard_map.55 = (f32[1024,7168]{1,0:T(8,128)}, f32[1024,512]{1,0:T(8,128)}) custom-call(s32[1]{0:T(128)} %bitcast.pos_ref, f32[2048,3584]{1,0:T(8,128)} %get-tuple-element.62.theta_ref, bf16[2048,2048]{1,0:T(8,128)(2,1)} %get-tuple-element.65.kern_hbm.kern_ref, f32[2048,1]{1,0:T(8,128)} %get-tuple-element.66.mass_ref, ...), custom_call_target="tpu_custom_call", output_to_operand_aliasing={{0}: (8, {})} | custom-call | flops 8589934592 | bytes 10485760 | tf_op jit(solution)/shard_map/pallas_call | solution.py:358
  771.2 19.4 %shard_map.56 = (f32[1024,7168]{1,0:T(8,128)}, f32[1024,512]{1,0:T(8,128)}) custom-call(s32[1]{0:T(128)} %bitcast.pos_ref, f32[2048,3584]{1,0:T(8,128)} %get-tuple-element.62.theta_ref, bf16[2048,2048]{1,0:T(8,128)(2,1)} %get-tuple-element.65.kern_hbm.kern_ref, f32[2048,1]{1,0:T(8,128)} %get-tuple-element.66.mass_ref, ...), custom_call_target="tpu_custom_call", output_to_operand_aliasing={{0}: (8, {})} | custom-call | flops 8589934592 | bytes 10485760 | tf_op jit(solution)/shard_map/pallas_call | solution.py:358
  790.6 1.5 collective-permute-start.5
  792.2 41.0 %collective-permute-done.8.recv_ref = f32[1024,128]{1,0:T(8,128)S(1)} collective-permute-done((f32[1024,128]{1,0:T(8,128)}, f32[1024,128]{1,0:T(8,128)S(1)}, u32[]{:S(2)}, u32[]{:S(2)}) %collective-permute-start.8) | collective-permute-done | bytes 524320 | tf_op jit(solution)/shard_map/ppermute | solution.py:831
  833.2 0.0 copy-start
  833.2 1.5 collective-permute-start.4
  834.7 19.4 %shard_map.57 = (f32[1024,7168]{1,0:T(8,128)}, f32[1024,512]{1,0:T(8,128)}) custom-call(s32[1]{0:T(128)} %bitcast.pos_ref, f32[2048,3584]{1,0:T(8,128)} %get-tuple-element.62.theta_ref, bf16[2048,2048]{1,0:T(8,128)(2,1)} %get-tuple-element.65.kern_hbm.kern_ref, f32[2048,1]{1,0:T(8,128)} %get-tuple-element.66.mass_ref, ...), custom_call_target="tpu_custom_call", output_to_operand_aliasing={{0}: (8, {})} | custom-call | flops 8589934592 | bytes 10485760 | tf_op jit(solution)/shard_map/pallas_call | solution.py:358
  854.1 0.0 copy-done
  854.1 24.1 %collective-permute-done.7.recv_ref = f32[1024,512]{1,0:T(8,128)} collective-permute-done((f32[1024,512]{1,0:T(8,128)}, f32[1024,512]{1,0:T(8,128)}, u32[]{:S(2)}, u32[]{:S(2)}) %collective-permute-start.7) | collective-permute-done | bytes 2097184 | tf_op jit(solution)/shard_map/ppermute | solution.py:831
  878.2 1.5 collective-permute-start.3
  879.7 13.3 %shard_map.58 = (f32[1024,7168]{1,0:T(8,128)}, f32[1024,256]{1,0:T(8,128)}) custom-call(s32[1]{0:T(128)} %bitcast.pos_ref, f32[2048,3584]{1,0:T(8,128)} %get-tuple-element.62.theta_ref, bf16[2048,2048]{1,0:T(8,128)(2,1)} %get-tuple-element.65.kern_hbm.kern_ref, f32[2048,1]{1,0:T(8,128)} %get-tuple-element.66.mass_ref, ...), custom_call_target="tpu_custom_call", output_to_operand_aliasing={{0}: (8, {})} | custom-call | flops 4294967296 | bytes 5242880 | tf_op jit(solution)/shard_map/pallas_call | solution.py:358
  893.0 8.7 shard_map.59
  901.7 21.4 %collective-permute-done.6.recv_ref = f32[1024,512]{1,0:T(8,128)} collective-permute-done((f32[1024,512]{1,0:T(8,128)}, f32[1024,512]{1,0:T(8,128)}, u32[]{:S(2)}, u32[]{:S(2)}) %collective-permute-start.6) | collective-permute-done | bytes 2097184 | tf_op jit(solution)/shard_map/ppermute | solution.py:831
  923.2 1.5 collective-permute-start.2
  924.7 14.0 %own_shared.1.base_ref = f32[1024,7168]{1,0:T(8,128)} custom-call(s32[1]{0:T(128)} %bitcast.pos_ref, f32[2048,512]{1,0:T(8,128)} %get-tuple-element.83.theta_ref, bf16[2048,2048]{1,0:T(8,128)(2,1)} %get-tuple-element.65.kern_hbm.kern_ref, f32[2048,1]{1,0:T(8,128)} %get-tuple-element.66.mass_ref, ...), custom_call_target="tpu_custom_call", output_to_operand_aliasing={{}: (8, {})} | custom-call | flops 4294967296 | bytes 10485760 | tf_op jit(solution)/shard_map/own_shared/pallas_call | solution.py:395
  938.6 0.0 collective-permute-done.9.theta_ref
  938.6 0.5 collective-permute-start.1
  939.2 14.0 %own_foreign.1.base_ref = f32[1024,7168]{1,0:T(8,128)} custom-call(s32[1]{0:T(128)} %bitcast.pos_ref, f32[2048,512]{1,0:T(8,128)} %collective-permute-done.9.theta_ref, bf16[2048,2048]{1,0:T(8,128)(2,1)} %get-tuple-element.65.kern_hbm.kern_ref, f32[2048,1]{1,0:T(8,128)} %get-tuple-element.66.mass_ref, ...), custom_call_target="tpu_custom_call", output_to_operand_aliasing={{}: (8, {})} | custom-call | flops 4294967296 | bytes 10485760 | tf_op jit(solution)/shard_map/own_foreign/pallas_call | solution.py:395
  953.2 1.9 shard_map.60.base_ref
  955.0 3.8 shard_map.61.base_ref
  958.8 3.8 shard_map.62.base_ref
  962.6 5.5 collective-permute-done.5.recv_ref
  968.1 3.8 shard_map.63.base_ref
  971.9 41.2 %collective-permute-done.4.recv_ref = f32[1024,512]{1,0:T(8,128)} collective-permute-done((f32[1024,512]{1,0:T(8,128)}, f32[1024,512]{1,0:T(8,128)}, u32[]{:S(2)}, u32[]{:S(2)}) %collective-permute-start.4) | collective-permute-done | bytes 2097184 | tf_op jit(solution)/shard_map/ppermute | solution.py:831
  1013.1 3.8 shard_map.64.base_ref
  1016.8 41.2 %collective-permute-done.3.recv_ref = f32[1024,512]{1,0:T(8,128)} collective-permute-done((f32[1024,512]{1,0:T(8,128)}, f32[1024,512]{1,0:T(8,128)}, u32[]{:S(2)}, u32[]{:S(2)}) %collective-permute-start.3) | collective-permute-done | bytes 2097184 | tf_op jit(solution)/shard_map/ppermute | solution.py:831
  1058.0 3.8 shard_map.65.base_ref
  1061.8 18.7 %collective-permute-done.2.recv_ref = f32[1024,256]{1,0:T(8,128)} collective-permute-done((f32[1024,256]{1,0:T(8,128)}, f32[1024,256]{1,0:T(8,128)}, u32[]{:S(2)}, u32[]{:S(2)}) %collective-permute-start.2) | collective-permute-done | bytes 1048608 | tf_op jit(solution)/shard_map/ppermute | solution.py:831
  1080.5 2.0 shard_map.66.base_ref
  1082.5 7.0 collective-permute-done.1.recv_ref
  1089.5 0.8 copy-done.1
  1090.3 1.9 shard_map.67
  (1 shorter events, 0.0 us)
Async XLA Ops:
  360.1 70.2 %collective-permute-start = (f32[1024,768]{1,0:T(8,128)}, f32[1024,768]{1,0:T(8,128)}, u32[]{:S(2)}, u32[]{:S(2)}) collective-permute-start(f32[1024,768]{1,0:T(8,128)} %get-tuple-element.46), channel_id=1, source_target_pairs={{0,4},{4,0},{1,5},{5,1},{2,6},{6,2},{3,7},{7,3}} | collective-permute-start | bytes 9437192 | tf_op jit(solution)/shard_map/ppermute | solution.py:819
  728.3 210.4 %collective-permute-start.9 = (f32[2048,512]{1,0:T(8,128)}, f32[2048,512]{1,0:T(8,128)}, u32[]{:S(2)}, u32[]{:S(2)}) collective-permute-start(f32[2048,512]{1,0:T(8,128)} %get-tuple-element.83.theta_ref), channel_id=1, source_target_pairs={{0,4},{4,0},{1,5},{5,1},{2,6},{6,2},{3,7},{7,3}} | collective-permute-start | bytes 12582920 | tf_op jit(solution)/shard_map/ppermute | solution.py:824
  749.2 84.0 %collective-permute-start.8 = (f32[1024,128]{1,0:T(8,128)}, f32[1024,128]{1,0:T(8,128)S(1)}, u32[]{:S(2)}, u32[]{:S(2)}) collective-permute-start(f32[1024,128]{1,0:T(8,128)} %get-tuple-element.82), channel_id=1, source_target_pairs={{0,4},{4,0},{1,5},{5,1},{2,6},{6,2},{3,7},{7,3}} | collective-permute-start | bytes 1572872 | tf_op jit(solution)/shard_map/ppermute | solution.py:831
  749.8 128.5 %collective-permute-start.7 = (f32[1024,512]{1,0:T(8,128)}, f32[1024,512]{1,0:T(8,128)}, u32[]{:S(2)}, u32[]{:S(2)}) collective-permute-start(f32[1024,512]{1,0:T(8,128)} %get-tuple-element.81), channel_id=1, source_target_pairs={{0,4},{4,0},{1,5},{5,1},{2,6},{6,2},{3,7},{7,3}} | collective-permute-start | bytes 6291464 | tf_op jit(solution)/shard_map/ppermute | solution.py:831
  751.3 171.9 %collective-permute-start.6 = (f32[1024,512]{1,0:T(8,128)}, f32[1024,512]{1,0:T(8,128)}, u32[]{:S(2)}, u32[]{:S(2)}) collective-permute-start(f32[1024,512]{1,0:T(8,128)} %get-tuple-element.80), channel_id=1, source_target_pairs={{0,4},{4,0},{1,5},{5,1},{2,6},{6,2},{3,7},{7,3}} | collective-permute-start | bytes 6291464 | tf_op jit(solution)/shard_map/ppermute | solution.py:831
  790.6 177.5 %collective-permute-start.5 = (f32[1024,512]{1,0:T(8,128)}, f32[1024,512]{1,0:T(8,128)}, u32[]{:S(2)}, u32[]{:S(2)}) collective-permute-start(f32[1024,512]{1,0:T(8,128)} %get-tuple-element.79), channel_id=1, source_target_pairs={{0,4},{4,0},{1,5},{5,1},{2,6},{6,2},{3,7},{7,3}} | collective-permute-start | bytes 6291464 | tf_op jit(solution)/shard_map/ppermute | solution.py:831
  833.2 20.9 %copy-start = (f32[1024,128]{1,0:T(8,128)}, f32[1024,128]{1,0:T(8,128)S(1)}, u32[]{:S(2)}) copy-start(f32[1024,128]{1,0:T(8,128)S(1)} %collective-permute-done.8.recv_ref) | copy-start | bytes 1572868
  833.2 179.9 %collective-permute-start.4 = (f32[1024,512]{1,0:T(8,128)}, f32[1024,512]{1,0:T(8,128)}, u32[]{:S(2)}, u32[]{:S(2)}) collective-permute-start(f32[1024,512]{1,0:T(8,128)} %get-tuple-element.78), channel_id=1, source_target_pairs={{0,4},{4,0},{1,5},{5,1},{2,6},{6,2},{3,7},{7,3}} | collective-permute-start | bytes 6291464 | tf_op jit(solution)/shard_map/ppermute | solution.py:831
  878.2 179.8 %collective-permute-start.3 = (f32[1024,512]{1,0:T(8,128)}, f32[1024,512]{1,0:T(8,128)}, u32[]{:S(2)}, u32[]{:S(2)}) collective-permute-start(f32[1024,512]{1,0:T(8,128)} %get-tuple-element.77), channel_id=1, source_target_pairs={{0,4},{4,0},{1,5},{5,1},{2,6},{6,2},{3,7},{7,3}} | collective-permute-start | bytes 6291464 | tf_op jit(solution)/shard_map/ppermute | solution.py:831
  923.2 157.3 %collective-permute-start.2 = (f32[1024,256]{1,0:T(8,128)}, f32[1024,256]{1,0:T(8,128)}, u32[]{:S(2)}, u32[]{:S(2)}) collective-permute-start(f32[1024,256]{1,0:T(8,128)} %get-tuple-element.76), channel_id=1, source_target_pairs={{0,4},{4,0},{1,5},{5,1},{2,6},{6,2},{3,7},{7,3}} | collective-permute-start | bytes 3145736 | tf_op jit(solution)/shard_map/ppermute | solution.py:831
  938.6 150.8 %collective-permute-start.1 = (f32[1024,128]{1,0:T(8,128)}, f32[1024,128]{1,0:T(8,128)S(1)}, u32[]{:S(2)}, u32[]{:S(2)}) collective-permute-start(f32[1024,128]{1,0:T(8,128)} %get-tuple-element.75), channel_id=1, source_target_pairs={{0,4},{4,0},{1,5},{5,1},{2,6},{6,2},{3,7},{7,3}} | collective-permute-start | bytes 1572872 | tf_op jit(solution)/shard_map/ppermute | solution.py:831
  1089.5 0.8 copy-start.1

commit v7 on v6

--- a/solution.py
+++ b/solution.py
@@ -28,7 +28,7 @@
     return jnp.concatenate([rows[:, HALF * g:HALF * (g + 1)] for g in range(8)], axis=0)
 
 
-def band_pieces(rows_at, b, n_blk):
+def band_pieces(rows_at, b, n_blk, ready=lambda n: None):
     def dot(left, right):
         return lax.dot_general(left, right, NT, preferred_element_type=F32)
 
@@ -36,15 +36,21 @@
         return j % n_blk if isinstance(j, int) else lax.rem(j, n_blk)
 
     main = slice(0, HALF)
+    ready(0)
     both = rows_at(b * BLK, BLK)
     for k in range(4):
+        if k > 0:
+            ready(k)
         val = dot(both, rows_at(wrap(b + k) * BLK, BLK))
         yield 0, main, slice(k * BLK, (k + 1) * BLK), val[:HALF]
         if k == 0:
             yield 1, main, slice(0, HALF), val[HALF:, HALF:]
         else:
             yield 1, main, slice(k * BLK - HALF, k * BLK + HALF), val[HALF:]
+    ready(4)
     yield 1, main, slice(WIDE - HALF, WIDE), dot(rows_at(b * BLK + HALF, HALF), rows_at(wrap(b + 4) * BLK, HALF))
+    for n in range(5, n_blk):
+        ready(n)
     far = dot(rows_at(b * HALF, HALF), rows_at((b + n_blk) * HALF, HALF))
     for h in range(2):
         yield h, slice(HALF, TALL), slice(0, WIDE), fold(far[h * (HALF // 2):(h + 1) * (HALF // 2)])
@@ -467,9 +473,13 @@
         return pltpu.make_async_remote_copy(src_ref=src, dst_ref=dst, send_sem=ssem, recv_sem=rsem,
                                             device_id=dev, device_id_type=MESH)
 
-    def load(b):
-        rs = pl.ds(b * BLK, BLK)
-        return pltpu.make_async_copy(src_ref.at[rs, :], tb.at[rs, :], load_sem.at[b])
+    cy_far, cx_far = chip(3)
+    first_band = cy_far * 4 + cx_far * 2 + 1 - core
+
+    def load(n):
+        b = lax.rem(first_band + n, n_blk)
+        rs = pl.ds(pl.multiple_of(b * BLK, BLK), BLK)
+        return pltpu.make_async_copy(src_ref.at[rs, :], tb.at[rs, :], load_sem.at[n])
 
     if not from_gram:
         def load_all():
@@ -523,10 +533,11 @@
         def rows_at(at, n):
             return tb[pl.ds(pl.multiple_of(at, HALF), n), :]
 
-        for b in range(n_blk):
-            load(b).wait()
-
-        @pl.loop(0, 8)
+        for h, rows_, cols_, piece in band_pieces(rows_at, first_band, n_blk, lambda n: load(n).wait()):
+            gbuf[7, h, rows_, cols_] = piece
+        sib_copy(3).start()
+
+        @pl.loop(1, 8)
         def _(i):
             rel, own = 3 - i // 2, lax.rem(i, 2)
             cy, cx = lax.rem(part + rel // 2, 2), lax.rem(x + lax.rem(rel, 2), 2)

time: 1090 us -> 1100 us (level)
  no operation moved by 1% of the time
where the time goes in v7:
time: 1100 us; the launch traced here: 1090 us
  Pallas kernels  875 us (80%)
  waiting for transfers between devices  204 us (19%)
  starting transfers between devices  11.4 us (1%)
    pallas_call x1, Pallas kernels, opening(): pl.pallas_call(functools.partial(opening_kernel, n_early, n_late, two_ove...  360 us
    ppermute x8, waiting for transfers between devices, local_steps(): received.append(lax.ppermute(send, 'part', swap))  201 us
    pallas_call x4, Pallas kernels, update(): pl.pallas_call(functools.partial(update_kernel, consts, first, split, bef...  179 us
    pallas_call x2, Pallas kernels, kernel_matrix(): pl.pallas_call(functools.partial(kmat_body, False, two_over_h), out_shape...  156 us
    pallas_call x8, Pallas kernels, last_update(): pl.pallas_call(functools.partial(last_kernel, consts, start), grid_spec=p...  128 us
    pallas_call x2, Pallas kernels, own_update(): pl.pallas_call(functools.partial(own_kernel, consts, foreign), grid_spec=...  28 us
    pallas_call x8, Pallas kernels, place(): pl.pallas_call(place_kernel, grid_spec=pltpu.PrefetchScalarGridSpec(num_s...  24.7 us
  transfers between devices with their start and end apart: 10, of which 9 were waited for; matrix products, arithmetic and copies ran while one was open for 0% of the time, Pallas kernels for 20%

profile of v7, /device:TPU:0, one launch (start us, length us, event | category | flops | bytes accessed | tf_op | source)
XLA Modules:
  0.0 1092.0 jit_solution(16995902220414459621)
XLA Ops:
  0.0 360.1 %opening.1 = (f32[2048,2816]{1,0:T(8,128)}, f32[1024,768]{1,0:T(8,128)}, f32[1024,768]{1,0:T(8,128)}, bf16[2048,2048]{1,0:T(8,128)(2,1)}, bf16[2048,32]{1,0:T(8,128)(2,1)}, /*index=5*/f32[2048,1]{1,0:T(8,128)}) custom-call(f32[1024,7168]{1,0:T(8,128)} %theta_ref.1, f32[1,7168]{1,0:T(1,128)} %bitcast.19, bf16[32,7168]{1,0:T(8,128)(2,1)} %bitcast.4), custom_call_target="tpu_custom_call" | custom-call | tf_op jit(solution)/shard_map/opening/pallas_call | solution.py:791
  360.1 1.2 collective-permute-start
  361.3 65.8 %shard_map.46 = (f32[2048,3584]{1,0:T(8,128)}, bf16[2048,3584]{1,0:T(8,128)(2,1)}, f32[32,2048]{1,0:T(8,128)}) custom-call(f32[2048,2816]{1,0:T(8,128)} %get-tuple-element.50.refs_0_.refs_1_, f32[2048,2816]{1,0:T(8,128)} %get-tuple-element.50.refs_0_.refs_1_, bf16[2048,2048]{1,0:T(8,128)(2,1)} %get-tuple-element.47.refs_2_.refs_4_, ...), custom_call_target="tpu_custom_call" | custom-call | flops 47244640256 | bytes 57671680 | tf_op jit(solution)/shard_map/pallas_call | solution.py:293
  427.1 3.2 collective-permute-done.refs_2_.refs_3_
  430.3 24.0 %shard_map.47 = (f32[2048,3584]{1,0:T(8,128)}, bf16[2048,3584]{1,0:T(8,128)(2,1)}, f32[32,2048]{1,0:T(8,128)}) custom-call(f32[1024,768]{1,0:T(8,128)} %get-tuple-element.45.refs_0_.refs_1_, f32[1024,768]{1,0:T(8,128)} %get-tuple-element.45.refs_0_.refs_1_, ...), custom_call_target="tpu_custom_call", output_to_operand_aliasing={{1}: (11, {}), {0}: (12, {})} | custom-call | flops 12884901888 | bytes 15728640 | tf_op jit(solution)/shard_map/pallas_call | solution.py:293
  454.3 78.3 %shard_map.48 = (bf16[2048,2048]{1,0:T(8,128)(2,1)}, bf16[2048,32]{1,0:T(8,128)(2,1)}, f32[2048,1]{1,0:T(8,128)}) custom-call(bf16[2048,3584]{1,0:T(8,128)(2,1)} %get-tuple-element.55.src_ref, f32[32,2048]{1,0:T(8,128)} %get-tuple-element.56.proj_ref), custom_call_target="tpu_custom_call" | custom-call | tf_op jit(solution)/shard_map/pallas_call | solution.py:769
  532.6 17.7 %shard_map.49 = (f32[2048,512]{1,0:T(8,128)}, bf16[2048,3584]{1,0:T(8,128)(2,1)}, f32[32,2048]{1,0:T(8,128)}) custom-call(f32[2048,3584]{1,0:T(8,128)} %get-tuple-element.54.refs_0_.refs_1_, f32[2048,3584]{1,0:T(8,128)} %get-tuple-element.54.refs_0_.refs_1_, bf16[2048,2048]{1,0:T(8,128)(2,1)} %get-tuple-element.57.refs_2_, ...), custom_call_target="tpu_custom_call" | custom-call | flops 8589934592 | bytes 10485760 | tf_op jit(solution)/shard_map/pallas_call | solution.py:293
  550.4 71.3 %shard_map.50 = (f32[2048,3584]{1,0:T(8,128)}, bf16[2048,3584]{1,0:T(8,128)(2,1)}, f32[32,2048]{1,0:T(8,128)}) custom-call(f32[2048,3584]{1,0:T(8,128)} %get-tuple-element.54.refs_0_.refs_1_, f32[2048,3584]{1,0:T(8,128)} %get-tuple-element.54.refs_0_.refs_1_, bf16[2048,2048]{1,0:T(8,128)(2,1)} %get-tuple-element.57.refs_2_, ...), custom_call_target="tpu_custom_call", output_to_operand_aliasing={{1}: (9, {})} | custom-call | flops 51539607552 | bytes 62914560 | tf_op jit(solution)/shard_map/pallas_call | solution.py:293
  621.7 77.9 %shard_map.51 = (bf16[2048,2048]{1,0:T(8,128)(2,1)}, bf16[2048,32]{1,0:T(8,128)(2,1)}, f32[2048,1]{1,0:T(8,128)}) custom-call(bf16[2048,3584]{1,0:T(8,128)(2,1)} %get-tuple-element.63.src_ref, f32[32,2048]{1,0:T(8,128)} %get-tuple-element.64.proj_ref), custom_call_target="tpu_custom_call" | custom-call | tf_op jit(solution)/shard_map/pallas_call | solution.py:769
  699.5 8.7 shard_map.52
  708.3 19.4 %shard_map.53 = (f32[1024,7168]{1,0:T(8,128)}, f32[1024,512]{1,0:T(8,128)}) custom-call(s32[1]{0:T(128)} %bitcast.pos_ref, f32[2048,3584]{1,0:T(8,128)} %get-tuple-element.62.theta_ref, bf16[2048,2048]{1,0:T(8,128)(2,1)} %get-tuple-element.65.kern_hbm.kern_ref, f32[2048,1]{1,0:T(8,128)} %get-tuple-element.66.mass_ref, ...), custom_call_target="tpu_custom_call", output_to_operand_aliasing={{0}: (8, {})} | custom-call | flops 8589934592 | bytes 10485760 | tf_op jit(solution)/shard_map/pallas_call | solution.py:364
  727.7 1.4 collective-permute-start.9
  729.1 19.4 %shard_map.54 = (f32[1024,7168]{1,0:T(8,128)}, f32[1024,512]{1,0:T(8,128)}) custom-call(s32[1]{0:T(128)} %bitcast.pos_ref, f32[2048,3584]{1,0:T(8,128)} %get-tuple-element.62.theta_ref, bf16[2048,2048]{1,0:T(8,128)(2,1)} %get-tuple-element.65.kern_hbm.kern_ref, f32[2048,1]{1,0:T(8,128)} %get-tuple-element.66.mass_ref, ...), custom_call_target="tpu_custom_call", output_to_operand_aliasing={{0}: (8, {})} | custom-call | flops 8589934592 | bytes 10485760 | tf_op jit(solution)/shard_map/pallas_call | solution.py:364
  748.5 0.7 collective-permute-start.8
  749.2 1.3 collective-permute-start.7
  750.5 0.7 collective-permute-start.6
  751.2 19.4 %shard_map.55 = (f32[1024,7168]{1,0:T(8,128)}, f32[1024,512]{1,0:T(8,128)}) custom-call(s32[1]{0:T(128)} %bitcast.pos_ref, f32[2048,3584]{1,0:T(8,128)} %get-tuple-element.62.theta_ref, bf16[2048,2048]{1,0:T(8,128)(2,1)} %get-tuple-element.65.kern_hbm.kern_ref, f32[2048,1]{1,0:T(8,128)} %get-tuple-element.66.mass_ref, ...), custom_call_target="tpu_custom_call", output_to_operand_aliasing={{0}: (8, {})} | custom-call | flops 8589934592 | bytes 10485760 | tf_op jit(solution)/shard_map/pallas_call | solution.py:364
  770.6 19.4 %shard_map.56 = (f32[1024,7168]{1,0:T(8,128)}, f32[1024,512]{1,0:T(8,128)}) custom-call(s32[1]{0:T(128)} %bitcast.pos_ref, f32[2048,3584]{1,0:T(8,128)} %get-tuple-element.62.theta_ref, bf16[2048,2048]{1,0:T(8,128)(2,1)} %get-tuple-element.65.kern_hbm.kern_ref, f32[2048,1]{1,0:T(8,128)} %get-tuple-element.66.mass_ref, ...), custom_call_target="tpu_custom_call", output_to_operand_aliasing={{0}: (8, {})} | custom-call | flops 8589934592 | bytes 10485760 | tf_op jit(solution)/shard_map/pallas_call | solution.py:364
  790.1 1.4 collective-permute-start.5
  791.4 41.2 %collective-permute-done.8.recv_ref = f32[1024,128]{1,0:T(8,128)S(1)} collective-permute-done((f32[1024,128]{1,0:T(8,128)}, f32[1024,128]{1,0:T(8,128)S(1)}, u32[]{:S(2)}, u32[]{:S(2)}) %collective-permute-start.8) | collective-permute-done | bytes 524320 | tf_op jit(solution)/shard_map/ppermute | solution.py:842
  832.6 0.0 copy-start
  832.6 1.3 collective-permute-start.4
  834.0 19.4 %shard_map.57 = (f32[1024,7168]{1,0:T(8,128)}, f32[1024,512]{1,0:T(8,128)}) custom-call(s32[1]{0:T(128)} %bitcast.pos_ref, f32[2048,3584]{1,0:T(8,128)} %get-tuple-element.62.theta_ref, bf16[2048,2048]{1,0:T(8,128)(2,1)} %get-tuple-element.65.kern_hbm.kern_ref, f32[2048,1]{1,0:T(8,128)} %get-tuple-element.66.mass_ref, ...), custom_call_target="tpu_custom_call", output_to_operand_aliasing={{0}: (8, {})} | custom-call | flops 8589934592 | bytes 10485760 | tf_op jit(solution)/shard_map/pallas_call | solution.py:364
  853.4 0.0 copy-done
  853.4 24.3 %collective-permute-done.7.recv_ref = f32[1024,512]{1,0:T(8,128)} collective-permute-done((f32[1024,512]{1,0:T(8,128)}, f32[1024,512]{1,0:T(8,128)}, u32[]{:S(2)}, u32[]{:S(2)}) %collective-permute-start.7) | collective-permute-done | bytes 2097184 | tf_op jit(solution)/shard_map/ppermute | solution.py:842
  877.7 1.3 collective-permute-start.3
  879.0 13.3 %shard_map.58 = (f32[1024,7168]{1,0:T(8,128)}, f32[1024,256]{1,0:T(8,128)}) custom-call(s32[1]{0:T(128)} %bitcast.pos_ref, f32[2048,3584]{1,0:T(8,128)} %get-tuple-element.62.theta_ref, bf16[2048,2048]{1,0:T(8,128)(2,1)} %get-tuple-element.65.kern_hbm.kern_ref, f32[2048,1]{1,0:T(8,128)} %get-tuple-element.66.mass_ref, ...), custom_call_target="tpu_custom_call", output_to_operand_aliasing={{0}: (8, {})} | custom-call | flops 4294967296 | bytes 5242880 | tf_op jit(solution)/shard_map/pallas_call | solution.py:364
  892.3 8.7 shard_map.59
  901.0 21.6 %collective-permute-done.6.recv_ref = f32[1024,512]{1,0:T(8,128)} collective-permute-done((f32[1024,512]{1,0:T(8,128)}, f32[1024,512]{1,0:T(8,128)}, u32[]{:S(2)}, u32[]{:S(2)}) %collective-permute-start.6) | collective-permute-done | bytes 2097184 | tf_op jit(solution)/shard_map/ppermute | solution.py:842
  922.6 1.3 collective-permute-start.2
  923.9 14.0 %own_shared.1.base_ref = f32[1024,7168]{1,0:T(8,128)} custom-call(s32[1]{0:T(128)} %bitcast.pos_ref, f32[2048,512]{1,0:T(8,128)} %get-tuple-element.83.theta_ref, bf16[2048,2048]{1,0:T(8,128)(2,1)} %get-tuple-element.65.kern_hbm.kern_ref, f32[2048,1]{1,0:T(8,128)} %get-tuple-element.66.mass_ref, ...), custom_call_target="tpu_custom_call", output_to_operand_aliasing={{}: (8, {})} | custom-call | flops 4294967296 | bytes 10485760 | tf_op jit(solution)/shard_map/own_shared/pallas_call | solution.py:401
  937.9 0.0 collective-permute-done.9.theta_ref
  937.9 0.7 collective-permute-start.1
  938.6 14.0 %own_foreign.1.base_ref = f32[1024,7168]{1,0:T(8,128)} custom-call(s32[1]{0:T(128)} %bitcast.pos_ref, f32[2048,512]{1,0:T(8,128)} %collective-permute-done.9.theta_ref, bf16[2048,2048]{1,0:T(8,128)(2,1)} %get-tuple-element.65.kern_hbm.kern_ref, f32[2048,1]{1,0:T(8,128)} %get-tuple-element.66.mass_ref, ...), custom_call_target="tpu_custom_call", output_to_operand_aliasing={{}: (8, {})} | custom-call | flops 4294967296 | bytes 10485760 | tf_op jit(solution)/shard_map/own_foreign/pallas_call | solution.py:401
  952.6 1.9 shard_map.60.base_ref
  954.5 3.8 shard_map.61.base_ref
  958.3 3.8 shard_map.62.base_ref
  962.0 5.5 collective-permute-done.5.recv_ref
  967.5 3.8 shard_map.63.base_ref
  971.3 41.2 %collective-permute-done.4.recv_ref = f32[1024,512]{1,0:T(8,128)} collective-permute-done((f32[1024,512]{1,0:T(8,128)}, f32[1024,512]{1,0:T(8,128)}, u32[]{:S(2)}, u32[]{:S(2)}) %collective-permute-start.4) | collective-permute-done | bytes 2097184 | tf_op jit(solution)/shard_map/ppermute | solution.py:842
  1012.5 3.8 shard_map.64.base_ref
  1016.3 41.2 %collective-permute-done.3.recv_ref = f32[1024,512]{1,0:T(8,128)} collective-permute-done((f32[1024,512]{1,0:T(8,128)}, f32[1024,512]{1,0:T(8,128)}, u32[]{:S(2)}, u32[]{:S(2)}) %collective-permute-start.3) | collective-permute-done | bytes 2097184 | tf_op jit(solution)/shard_map/ppermute | solution.py:842
  1057.4 3.8 shard_map.65.base_ref
  1061.2 18.7 %collective-permute-done.2.recv_ref = f32[1024,256]{1,0:T(8,128)} collective-permute-done((f32[1024,256]{1,0:T(8,128)}, f32[1024,256]{1,0:T(8,128)}, u32[]{:S(2)}, u32[]{:S(2)}) %collective-permute-start.2) | collective-permute-done | bytes 1048608 | tf_op jit(solution)/shard_map/ppermute | solution.py:842
  1079.9 2.0 shard_map.66.base_ref
  1081.9 7.2 collective-permute-done.1.recv_ref
  1089.2 0.8 copy-done.1
  1090.0 1.9 shard_map.67
  (1 shorter events, 0.0 us)
Async XLA Ops:
  360.1 70.2 %collective-permute-start = (f32[1024,768]{1,0:T(8,128)}, f32[1024,768]{1,0:T(8,128)}, u32[]{:S(2)}, u32[]{:S(2)}) collective-permute-start(f32[1024,768]{1,0:T(8,128)} %get-tuple-element.46), channel_id=1, source_target_pairs={{0,4},{4,0},{1,5},{5,1},{2,6},{6,2},{3,7},{7,3}} | collective-permute-start | bytes 9437192 | tf_op jit(solution)/shard_map/ppermute | solution.py:830
  727.7 210.2 %collective-permute-start.9 = (f32[2048,512]{1,0:T(8,128)}, f32[2048,512]{1,0:T(8,128)}, u32[]{:S(2)}, u32[]{:S(2)}) collective-permute-start(f32[2048,512]{1,0:T(8,128)} %get-tuple-element.83.theta_ref), channel_id=1, source_target_pairs={{0,4},{4,0},{1,5},{5,1},{2,6},{6,2},{3,7},{7,3}} | collective-permute-start | bytes 12582920 | tf_op jit(solution)/shard_map/ppermute | solution.py:835
  748.5 84.1 %collective-permute-start.8 = (f32[1024,128]{1,0:T(8,128)}, f32[1024,128]{1,0:T(8,128)S(1)}, u32[]{:S(2)}, u32[]{:S(2)}) collective-permute-start(f32[1024,128]{1,0:T(8,128)} %get-tuple-element.82), channel_id=1, source_target_pairs={{0,4},{4,0},{1,5},{5,1},{2,6},{6,2},{3,7},{7,3}} | collective-permute-start | bytes 1572872 | tf_op jit(solution)/shard_map/ppermute | solution.py:842
  749.2 128.5 %collective-permute-start.7 = (f32[1024,512]{1,0:T(8,128)}, f32[1024,512]{1,0:T(8,128)}, u32[]{:S(2)}, u32[]{:S(2)}) collective-permute-start(f32[1024,512]{1,0:T(8,128)} %get-tuple-element.81), channel_id=1, source_target_pairs={{0,4},{4,0},{1,5},{5,1},{2,6},{6,2},{3,7},{7,3}} | collective-permute-start | bytes 6291464 | tf_op jit(solution)/shard_map/ppermute | solution.py:842
  750.5 172.1 %collective-permute-start.6 = (f32[1024,512]{1,0:T(8,128)}, f32[1024,512]{1,0:T(8,128)}, u32[]{:S(2)}, u32[]{:S(2)}) collective-permute-start(f32[1024,512]{1,0:T(8,128)} %get-tuple-element.80), channel_id=1, source_target_pairs={{0,4},{4,0},{1,5},{5,1},{2,6},{6,2},{3,7},{7,3}} | collective-permute-start | bytes 6291464 | tf_op jit(solution)/shard_map/ppermute | solution.py:842
  790.1 177.5 %collective-permute-start.5 = (f32[1024,512]{1,0:T(8,128)}, f32[1024,512]{1,0:T(8,128)}, u32[]{:S(2)}, u32[]{:S(2)}) collective-permute-start(f32[1024,512]{1,0:T(8,128)} %get-tuple-element.79), channel_id=1, source_target_pairs={{0,4},{4,0},{1,5},{5,1},{2,6},{6,2},{3,7},{7,3}} | collective-permute-start | bytes 6291464 | tf_op jit(solution)/shard_map/ppermute | solution.py:842
  832.6 20.8 %copy-start = (f32[1024,128]{1,0:T(8,128)}, f32[1024,128]{1,0:T(8,128)S(1)}, u32[]{:S(2)}) copy-start(f32[1024,128]{1,0:T(8,128)S(1)} %collective-permute-done.8.recv_ref) | copy-start | bytes 1572868
  832.6 179.9 %collective-permute-start.4 = (f32[1024,512]{1,0:T(8,128)}, f32[1024,512]{1,0:T(8,128)}, u32[]{:S(2)}, u32[]{:S(2)}) collective-permute-start(f32[1024,512]{1,0:T(8,128)} %get-tuple-element.78), channel_id=1, source_target_pairs={{0,4},{4,0},{1,5},{5,1},{2,6},{6,2},{3,7},{7,3}} | collective-permute-start | bytes 6291464 | tf_op jit(solution)/shard_map/ppermute | solution.py:842
  877.7 179.8 %collective-permute-start.3 = (f32[1024,512]{1,0:T(8,128)}, f32[1024,512]{1,0:T(8,128)}, u32[]{:S(2)}, u32[]{:S(2)}) collective-permute-start(f32[1024,512]{1,0:T(8,128)} %get-tuple-element.77), channel_id=1, source_target_pairs={{0,4},{4,0},{1,5},{5,1},{2,6},{6,2},{3,7},{7,3}} | collective-permute-start | bytes 6291464 | tf_op jit(solution)/shard_map/ppermute | solution.py:842
  922.6 157.3 %collective-permute-start.2 = (f32[1024,256]{1,0:T(8,128)}, f32[1024,256]{1,0:T(8,128)}, u32[]{:S(2)}, u32[]{:S(2)}) collective-permute-start(f32[1024,256]{1,0:T(8,128)} %get-tuple-element.76), channel_id=1, source_target_pairs={{0,4},{4,0},{1,5},{5,1},{2,6},{6,2},{3,7},{7,3}} | collective-permute-start | bytes 3145736 | tf_op jit(solution)/shard_map/ppermute | solution.py:842
  937.9 151.3 %collective-permute-start.1 = (f32[1024,128]{1,0:T(8,128)}, f32[1024,128]{1,0:T(8,128)S(1)}, u32[]{:S(2)}, u32[]{:S(2)}) collective-permute-start(f32[1024,128]{1,0:T(8,128)} %get-tuple-element.75), channel_id=1, source_target_pairs={{0,4},{4,0},{1,5},{5,1},{2,6},{6,2},{3,7},{7,3}} | collective-permute-start | bytes 1572872 | tf_op jit(solution)/shard_map/ppermute | solution.py:842
  1089.2 0.8 copy-start.1

commit v8 on v6

--- a/solution.py
+++ b/solution.py
@@ -369,10 +369,50 @@
     )(pos, *args)
 
 
-def own_kernel(consts, foreign, pos_ref, theta_ref, kern_ref, mass_ref, zb_ref, mean_ref, prec_ref, fact_ref, base_ref, out_ref, rhs):
+def send_kernel(consts, start, pos_ref, theta_ref, kern_hbm, mass_ref, zb_ref, mean_ref, prec_ref, fact_ref, send_ref, rhs, kern_ref, kern_sem):
+    rows = send_ref.shape[0]
+    theirs = pl.ds(pl.multiple_of((1 - pos_ref[0]) * rows, BLK), rows)
+    fetch = pltpu.make_async_copy(kern_hbm.at[theirs, :], kern_ref, kern_sem)
+    fetch.start()
+    now = columns(pos_ref[0], start, theta_ref.shape[1], (mean_ref, prec_ref, fact_ref))
+
+    @pl.loop(0, 2)
+    def _(b):
+        rs = pl.ds(pl.multiple_of(b * rows, BLK), rows)
+        build_rhs(theta_ref[rs, :], *now, zb_ref, rhs, rs)
+
+    fetch.wait()
+
+    @pl.loop(0, rows // BLK)
+    def _(b):
+        at = pl.ds(pl.multiple_of(b * BLK, BLK), BLK)
+        rs = pl.ds(pl.multiple_of((1 - pos_ref[0]) * rows + b * BLK, BLK), BLK)
+        acc = jnp.dot(kern_ref[at, :], rhs[...], preferred_element_type=F32)
+        send_ref[at, :] = stepped(theta_ref[rs, :], acc, mass_ref, rs, *consts)
+
+
+def send_update(consts, pos, theta, kern, mass, zb, mean, prec, fact_t, start, tile):
+    n_rows = theta.shape[0]
+    rows = n_rows // 2
+    return pl.pallas_call(
+        functools.partial(send_kernel, consts, start),
+        grid_spec=pltpu.PrefetchScalarGridSpec(
+            num_scalar_prefetch=1, grid=(1,),
+            in_specs=[pl.BlockSpec((n_rows, tile), lambda i, pos: (0, start // tile)), ANY] + [VMEM] * 5,
+            out_specs=pl.BlockSpec((rows, tile), lambda i, pos: (0, 0)),
+            scratch_shapes=[pltpu.VMEM((n_rows, 2 * tile), BF16), pltpu.VMEM((rows, n_rows), BF16), pltpu.SemaphoreType.DMA]),
+        out_shape=jax.ShapeDtypeStruct((rows, tile), F32),
+        compiler_params=pltpu.CompilerParams(vmem_limit_bytes=VMEM_LIMIT),
+        cost_estimate=pl.CostEstimate(flops=4 * n_rows * rows * tile, bytes_accessed=10 * n_rows * tile, transcendentals=0),
+        name="send_first",
+    )(pos, theta, kern, mass, zb, mean, prec, fact_t)
+
+
+def own_kernel(consts, foreign, start, pos_ref, theta_ref, kern_ref, mass_ref, zb_ref, mean_ref, prec_ref, fact_ref, base_ref, out_ref, rhs):
     rows = out_ref.shape[0]
     half = 1 - pos_ref[0] if foreign else pos_ref[0]
-    now = columns(half, pl.program_id(0) * BLK, BLK, (mean_ref, prec_ref, fact_ref))
+    tile = theta_ref.shape[1]
+    now = columns(half, start + pl.program_id(0) * tile, tile, (mean_ref, prec_ref, fact_ref))
 
     @pl.loop(0, theta_ref.shape[0] // BLK)
     def _(b):
@@ -386,24 +426,24 @@
         out_ref[pl.ds(pl.multiple_of(b * BLK, BLK), BLK), :] = stepped(theta_ref[rs, :], acc, mass_ref, rs, *consts)
 
 
-def own_update(consts, pos, theta, kern, mass, zb, mean, prec, fact_t, out, foreign):
-    n_rows, cols = theta.shape
+def own_update(consts, pos, theta, kern, mass, zb, mean, prec, fact_t, out, foreign, start, cols, tile):
+    n_rows = theta.shape[0]
+    first = start // tile
     rows, feat = out.shape
-    per = feat // (2 * BLK)
-    col = lambda r: pl.BlockSpec((r, BLK), lambda i, pos: (0, i))
-    where = (lambda i, pos: (0, (1 - pos[0]) * per + i)) if foreign else (lambda i, pos: (0, pos[0] * per + i))
+    per = feat // (2 * tile)
+    col = lambda r: pl.BlockSpec((r, tile), lambda i, pos: (0, first + i))
+    where = (lambda i, pos: (0, (1 - pos[0]) * per + first + i)) if foreign else (lambda i, pos: (0, pos[0] * per + first + i))
     return pl.pallas_call(
-        functools.partial(own_kernel, consts, foreign),
+        functools.partial(own_kernel, consts, foreign, start),
         grid_spec=pltpu.PrefetchScalarGridSpec(
-            num_scalar_prefetch=1, grid=(cols // BLK,),
+            num_scalar_prefetch=1, grid=(cols // tile,),
             in_specs=[col(n_rows), VMEM, VMEM, VMEM, VMEM, VMEM, VMEM, ANY],
-            out_specs=pl.BlockSpec((rows, BLK), where),
-            scratch_shapes=[pltpu.VMEM((n_rows, 2 * BLK), BF16)]),
+            out_specs=pl.BlockSpec((rows, tile), where),
+            scratch_shapes=[pltpu.VMEM((n_rows, 2 * tile), BF16)]),
         out_shape=jax.ShapeDtypeStruct(out.shape, F32),
         input_output_aliases={8: 0},
         compiler_params=pltpu.CompilerParams(vmem_limit_bytes=VMEM_LIMIT),
         cost_estimate=pl.CostEstimate(flops=4 * rows * n_rows * cols, bytes_accessed=10 * n_rows * cols, transcendentals=0),
-        name="own_foreign" if foreign else "own_shared",
     )(pos, theta, kern, mass, zb, mean, prec, fact_t, out)
 
 
@@ -826,11 +866,15 @@
         kern, zb, mass = kernel_matrix(tb, proj, consts[1], 3)
         out = None
         received = []
-        for start, tile in chunks:
-            out, send = last_update(consts, pos, cur, kern, mass, zb, *params, out, start, tile)
+        for i, (start, tile) in enumerate(chunks):
+            if i == 0:
+                send = send_update(consts, pos, cur, kern, mass, zb, *params, start, tile)
+            else:
+                out, send = last_update(consts, pos, cur, kern, mass, zb, *params, out, start, tile)
             received.append(lax.ppermute(send, "part", swap))
-        out = own_update(consts, pos, both, kern, mass, zb, *params, out, False)
-        out = own_update(consts, pos, foreign, kern, mass, zb, *params, out, True)
+        out = own_update(consts, pos, cur, kern, mass, zb, *params, out, False, chunks[0][0], chunks[0][1], chunks[0][1])
+        out = own_update(consts, pos, both, kern, mass, zb, *params, out, False, 0, shared, BLK)
+        out = own_update(consts, pos, foreign, kern, mass, zb, *params, out, True, 0, shared, BLK)
         for (start, tile), recv in zip(chunks, received):
             out = place(pos, recv, out, start)
         return out

time: 1090 us -> 1030 us (0.945)
  waiting for transfers between devices: 203 us -> 127 us
  Pallas kernels: 876 us -> 890 us
    ppermute x8, waiting for transfers between devices: 200 us -> 124 us  [local_steps(): received.append(lax.ppermute(send, 'part', swap))]
    pallas_call x2 -> x4, Pallas kernels: 28 us -> 42.5 us  [the longest x3 35.9 us: own_update(): pl.pallas_call(functools.partial(own_kernel, consts, foreign, start), gri...]
    pallas_call x8 -> x7, Pallas kernels: 128 us -> 119 us  [last_update(): pl.pallas_call(functools.partial(last_kernel, consts, start), grid_spec=p...]
  transfers between devices with their start and end apart: 10 -> 10, of which waited for: 9 -> 7; matrix products, arithmetic and copies ran while one was open for 0% -> 0% of each run, Pallas kernels for 20% -> 40%
where the time goes in v8:
time: 1030 us
  Pallas kernels  890 us (86%)
  waiting for transfers between devices  127 us (12%)
  starting transfers between devices  11 us (1%)
    pallas_call x1, Pallas kernels, opening(): pl.pallas_call(functools.partial(opening_kernel, n_early, n_late, two_ove...  360 us
    pallas_call x4, Pallas kernels, update(): pl.pallas_call(functools.partial(update_kernel, consts, first, split, bef...  179 us
    pallas_call x2, Pallas kernels, kernel_matrix(): pl.pallas_call(functools.partial(kmat_body, False, two_over_h), out_shape...  165 us
    ppermute x8, waiting for transfers between devices, local_steps(): received.append(lax.ppermute(send, 'part', swap))  124 us
    pallas_call x7, Pallas kernels, last_update(): pl.pallas_call(functools.partial(last_kernel, consts, start), grid_spec=p...  119 us
    pallas_call x3, Pallas kernels, own_update(): pl.pallas_call(functools.partial(own_kernel, consts, foreign, start), gri...  35.9 us
    pallas_call x8, Pallas kernels, place(): pl.pallas_call(place_kernel, grid_spec=pltpu.PrefetchScalarGridSpec(num_s...  24.7 us
  transfers between devices with their start and end apart: 10, of which 7 were waited for; matrix products, arithmetic and copies ran while one was open for 0% of the time, Pallas kernels for 40%

profile of v8, /device:TPU:0, one launch (start us, length us, event | category | flops | bytes accessed | tf_op | source)
XLA Modules:
  0.0 1029.1 jit_solution(14322057898742769236)
XLA Ops:
  0.0 360.1 %opening.1 = (f32[2048,2816]{1,0:T(8,128)}, f32[1024,768]{1,0:T(8,128)}, f32[1024,768]{1,0:T(8,128)}, bf16[2048,2048]{1,0:T(8,128)(2,1)}, bf16[2048,32]{1,0:T(8,128)(2,1)}, /*index=5*/f32[2048,1]{1,0:T(8,128)}) custom-call(f32[1024,7168]{1,0:T(8,128)} %theta_ref.1, f32[1,7168]{1,0:T(1,128)} %bitcast.20, bf16[32,7168]{1,0:T(8,128)(2,1)} %bitcast.4), custom_call_target="tpu_custom_call" | custom-call | tf_op jit(solution)/shard_map/opening/pallas_call | solution.py:820
  360.1 1.2 collective-permute-start
  361.3 65.8 %shard_map.46 = (f32[2048,3584]{1,0:T(8,128)}, bf16[2048,3584]{1,0:T(8,128)(2,1)}, f32[32,2048]{1,0:T(8,128)}) custom-call(f32[2048,2816]{1,0:T(8,128)} %get-tuple-element.48.refs_0_.refs_1_, f32[2048,2816]{1,0:T(8,128)} %get-tuple-element.48.refs_0_.refs_1_, bf16[2048,2048]{1,0:T(8,128)(2,1)} %get-tuple-element.45.refs_2_.refs_4_, ...), custom_call_target="tpu_custom_call" | custom-call | flops 47244640256 | bytes 57671680 | tf_op jit(solution)/shard_map/pallas_call | solution.py:287
  427.1 3.2 collective-permute-done.refs_2_.refs_3_
  430.3 24.0 %shard_map.47 = (f32[2048,3584]{1,0:T(8,128)}, bf16[2048,3584]{1,0:T(8,128)(2,1)}, f32[32,2048]{1,0:T(8,128)}) custom-call(f32[1024,768]{1,0:T(8,128)} %get-tuple-element.43.refs_0_.refs_1_, f32[1024,768]{1,0:T(8,128)} %get-tuple-element.43.refs_0_.refs_1_, ...), custom_call_target="tpu_custom_call", output_to_operand_aliasing={{1}: (11, {}), {0}: (12, {})} | custom-call | flops 12884901888 | bytes 15728640 | tf_op jit(solution)/shard_map/pallas_call | solution.py:287
  454.3 78.5 %shard_map.48 = (bf16[2048,2048]{1,0:T(8,128)(2,1)}, bf16[2048,32]{1,0:T(8,128)(2,1)}, f32[2048,1]{1,0:T(8,128)}) custom-call(bf16[2048,3584]{1,0:T(8,128)(2,1)} %get-tuple-element.53.src_ref, f32[32,2048]{1,0:T(8,128)} %get-tuple-element.54.proj_ref), custom_call_target="tpu_custom_call" | custom-call | tf_op jit(solution)/shard_map/pallas_call | solution.py:798
  532.8 17.6 %shard_map.49 = (f32[2048,512]{1,0:T(8,128)}, bf16[2048,3584]{1,0:T(8,128)(2,1)}, f32[32,2048]{1,0:T(8,128)}) custom-call(f32[2048,3584]{1,0:T(8,128)} %get-tuple-element.52.refs_0_.refs_1_, f32[2048,3584]{1,0:T(8,128)} %get-tuple-element.52.refs_0_.refs_1_, bf16[2048,2048]{1,0:T(8,128)(2,1)} %get-tuple-element.55.refs_2_, ...), custom_call_target="tpu_custom_call" | custom-call | flops 8589934592 | bytes 10485760 | tf_op jit(solution)/shard_map/pallas_call | solution.py:287
  550.4 1.6 collective-permute-start.9
  552.0 71.2 %shard_map.50 = (f32[2048,3584]{1,0:T(8,128)}, bf16[2048,3584]{1,0:T(8,128)(2,1)}, f32[32,2048]{1,0:T(8,128)}) custom-call(f32[2048,3584]{1,0:T(8,128)} %get-tuple-element.52.refs_0_.refs_1_, f32[2048,3584]{1,0:T(8,128)} %get-tuple-element.52.refs_0_.refs_1_, bf16[2048,2048]{1,0:T(8,128)(2,1)} %get-tuple-element.55.refs_2_, ...), custom_call_target="tpu_custom_call", output_to_operand_aliasing={{1}: (9, {})} | custom-call | flops 51539607552 | bytes 62914560 | tf_op jit(solution)/shard_map/pallas_call | solution.py:287
  623.3 86.3 %shard_map.51 = (bf16[2048,2048]{1,0:T(8,128)(2,1)}, bf16[2048,32]{1,0:T(8,128)(2,1)}, f32[2048,1]{1,0:T(8,128)}) custom-call(bf16[2048,3584]{1,0:T(8,128)(2,1)} %get-tuple-element.61.src_ref, f32[32,2048]{1,0:T(8,128)} %get-tuple-element.62.proj_ref), custom_call_target="tpu_custom_call" | custom-call | tf_op jit(solution)/shard_map/pallas_call | solution.py:798
  709.6 19.4 %shard_map.52 = (f32[1024,7168]{1,0:T(8,128)}, f32[1024,512]{1,0:T(8,128)}) custom-call(s32[1]{0:T(128)} %bitcast.pos_ref, f32[2048,3584]{1,0:T(8,128)} %get-tuple-element.60.theta_ref, bf16[2048,2048]{1,0:T(8,128)(2,1)} %get-tuple-element.63.kern_hbm.kern_ref, f32[2048,1]{1,0:T(8,128)} %get-tuple-element.64.mass_ref, ...), custom_call_target="tpu_custom_call" | custom-call | flops 8589934592 | bytes 10485760 | tf_op jit(solution)/shard_map/pallas_call | solution.py:358
  729.0 19.4 %shard_map.53 = (f32[1024,7168]{1,0:T(8,128)}, f32[1024,512]{1,0:T(8,128)}) custom-call(s32[1]{0:T(128)} %bitcast.pos_ref, f32[2048,3584]{1,0:T(8,128)} %get-tuple-element.60.theta_ref, bf16[2048,2048]{1,0:T(8,128)(2,1)} %get-tuple-element.63.kern_hbm.kern_ref, f32[2048,1]{1,0:T(8,128)} %get-tuple-element.64.mass_ref, ...), custom_call_target="tpu_custom_call", output_to_operand_aliasing={{0}: (8, {})} | custom-call | flops 8589934592 | bytes 10485760 | tf_op jit(solution)/shard_map/pallas_call | solution.py:358
  748.4 6.7 send_first.1
  755.1 1.0 collective-permute-start.8
  756.1 1.0 collective-permute-start.7
  757.2 1.0 collective-permute-start.6
  758.1 19.4 %shard_map.54 = (f32[1024,7168]{1,0:T(8,128)}, f32[1024,512]{1,0:T(8,128)}) custom-call(s32[1]{0:T(128)} %bitcast.pos_ref, f32[2048,3584]{1,0:T(8,128)} %get-tuple-element.60.theta_ref, bf16[2048,2048]{1,0:T(8,128)(2,1)} %get-tuple-element.63.kern_hbm.kern_ref, f32[2048,1]{1,0:T(8,128)} %get-tuple-element.64.mass_ref, ...), custom_call_target="tpu_custom_call", output_to_operand_aliasing={{0}: (8, {})} | custom-call | flops 8589934592 | bytes 10485760 | tf_op jit(solution)/shard_map/pallas_call | solution.py:358
  777.6 19.4 %shard_map.55 = (f32[1024,7168]{1,0:T(8,128)}, f32[1024,512]{1,0:T(8,128)}) custom-call(s32[1]{0:T(128)} %bitcast.pos_ref, f32[2048,3584]{1,0:T(8,128)} %get-tuple-element.60.theta_ref, bf16[2048,2048]{1,0:T(8,128)(2,1)} %get-tuple-element.63.kern_hbm.kern_ref, f32[2048,1]{1,0:T(8,128)} %get-tuple-element.64.mass_ref, ...), custom_call_target="tpu_custom_call", output_to_operand_aliasing={{0}: (8, {})} | custom-call | flops 8589934592 | bytes 10485760 | tf_op jit(solution)/shard_map/pallas_call | solution.py:358
  797.0 1.1 collective-permute-start.5
  798.1 0.0 collective-permute-done.8.recv_ref
  798.1 1.0 collective-permute-start.4
  799.1 19.4 %shard_map.56 = (f32[1024,7168]{1,0:T(8,128)}, f32[1024,512]{1,0:T(8,128)}) custom-call(s32[1]{0:T(128)} %bitcast.pos_ref, f32[2048,3584]{1,0:T(8,128)} %get-tuple-element.60.theta_ref, bf16[2048,2048]{1,0:T(8,128)(2,1)} %get-tuple-element.63.kern_hbm.kern_ref, f32[2048,1]{1,0:T(8,128)} %get-tuple-element.64.mass_ref, ...), custom_call_target="tpu_custom_call", output_to_operand_aliasing={{0}: (8, {})} | custom-call | flops 8589934592 | bytes 10485760 | tf_op jit(solution)/shard_map/pallas_call | solution.py:358
  818.5 0.0 copy-done
  818.5 0.0 collective-permute-done.7.recv_ref
  818.5 1.1 collective-permute-start.3
  819.6 13.2 %shard_map.57 = (f32[1024,7168]{1,0:T(8,128)}, f32[1024,256]{1,0:T(8,128)}) custom-call(s32[1]{0:T(128)} %bitcast.pos_ref, f32[2048,3584]{1,0:T(8,128)} %get-tuple-element.60.theta_ref, bf16[2048,2048]{1,0:T(8,128)(2,1)} %get-tuple-element.63.kern_hbm.kern_ref, f32[2048,1]{1,0:T(8,128)} %get-tuple-element.64.mass_ref, ...), custom_call_target="tpu_custom_call", output_to_operand_aliasing={{0}: (8, {})} | custom-call | flops 4294967296 | bytes 5242880 | tf_op jit(solution)/shard_map/pallas_call | solution.py:358
  832.8 8.7 shard_map.58
  841.5 8.0 shard_map.59.base_ref
  849.6 10.5 %collective-permute-done.6.recv_ref = f32[1024,512]{1,0:T(8,128)} collective-permute-done((f32[1024,512]{1,0:T(8,128)}, f32[1024,512]{1,0:T(8,128)}, u32[]{:S(2)}, u32[]{:S(2)}) %collective-permute-start.6) | collective-permute-done | bytes 2097184 | tf_op jit(solution)/shard_map/ppermute | solution.py:874
  860.1 1.0 collective-permute-start.2
  861.1 13.9 %shard_map.60.base_ref = f32[1024,7168]{1,0:T(8,128)} custom-call(s32[1]{0:T(128)} %bitcast.pos_ref, f32[2048,512]{1,0:T(8,128)} %get-tuple-element.79.theta_ref, bf16[2048,2048]{1,0:T(8,128)(2,1)} %get-tuple-element.63.kern_hbm.kern_ref, f32[2048,1]{1,0:T(8,128)} %get-tuple-element.64.mass_ref, ...), custom_call_target="tpu_custom_call", output_to_operand_aliasing={{}: (8, {})} | custom-call | flops 4294967296 | bytes 10485760 | tf_op jit(solution)/shard_map/pallas_call | solution.py:436
  875.0 0.0 collective-permute-done.9.theta_ref
  875.0 1.0 collective-permute-start.1
  876.1 13.9 %shard_map.61.base_ref = f32[1024,7168]{1,0:T(8,128)} custom-call(s32[1]{0:T(128)} %bitcast.pos_ref, f32[2048,512]{1,0:T(8,128)} %collective-permute-done.9.theta_ref, bf16[2048,2048]{1,0:T(8,128)(2,1)} %get-tuple-element.63.kern_hbm.kern_ref, f32[2048,1]{1,0:T(8,128)} %get-tuple-element.64.mass_ref, ...), custom_call_target="tpu_custom_call", output_to_operand_aliasing={{}: (8, {})} | custom-call | flops 4294967296 | bytes 10485760 | tf_op jit(solution)/shard_map/pallas_call | solution.py:436
  890.0 1.9 shard_map.62.base_ref
  891.9 3.8 shard_map.63.base_ref
  895.6 3.8 shard_map.64.base_ref
  899.4 5.7 collective-permute-done.5.recv_ref
  905.1 3.8 shard_map.65.base_ref
  908.8 41.2 %collective-permute-done.4.recv_ref = f32[1024,512]{1,0:T(8,128)} collective-permute-done((f32[1024,512]{1,0:T(8,128)}, f32[1024,512]{1,0:T(8,128)}, u32[]{:S(2)}, u32[]{:S(2)}) %collective-permute-start.4) | collective-permute-done | bytes 2097184 | tf_op jit(solution)/shard_map/ppermute | solution.py:874
  950.0 3.8 shard_map.66.base_ref
  953.8 41.2 %collective-permute-done.3.recv_ref = f32[1024,512]{1,0:T(8,128)} collective-permute-done((f32[1024,512]{1,0:T(8,128)}, f32[1024,512]{1,0:T(8,128)}, u32[]{:S(2)}, u32[]{:S(2)}) %collective-permute-start.3) | collective-permute-done | bytes 2097184 | tf_op jit(solution)/shard_map/ppermute | solution.py:874
  995.0 3.8 shard_map.67.base_ref
  998.7 18.7 %collective-permute-done.2.recv_ref = f32[1024,256]{1,0:T(8,128)} collective-permute-done((f32[1024,256]{1,0:T(8,128)}, f32[1024,256]{1,0:T(8,128)}, u32[]{:S(2)}, u32[]{:S(2)}) %collective-permute-start.2) | collective-permute-done | bytes 1048608 | tf_op jit(solution)/shard_map/ppermute | solution.py:874
  1017.4 2.0 shard_map.68.base_ref
  1019.5 7.0 collective-permute-done.1.recv_ref
  1026.5 0.8 copy-done.1
  1027.3 1.9 shard_map.69
  (2 shorter events, 0.0 us)
Async XLA Ops:
  360.1 70.2 %collective-permute-start = (f32[1024,768]{1,0:T(8,128)}, f32[1024,768]{1,0:T(8,128)}, u32[]{:S(2)}, u32[]{:S(2)}) collective-permute-start(f32[1024,768]{1,0:T(8,128)} %get-tuple-element.44), channel_id=1, source_target_pairs={{0,4},{4,0},{1,5},{5,1},{2,6},{6,2},{3,7},{7,3}} | collective-permute-start | bytes 9437192 | tf_op jit(solution)/shard_map/ppermute | solution.py:859
  550.4 324.6 %collective-permute-start.9 = (f32[2048,512]{1,0:T(8,128)}, f32[2048,512]{1,0:T(8,128)}, u32[]{:S(2)}, u32[]{:S(2)}) collective-permute-start(f32[2048,512]{1,0:T(8,128)} %get-tuple-element.79.theta_ref), channel_id=1, source_target_pairs={{0,4},{4,0},{1,5},{5,1},{2,6},{6,2},{3,7},{7,3}} | collective-permute-start | bytes 12582920 | tf_op jit(solution)/shard_map/ppermute | solution.py:864
  755.1 43.0 %collective-permute-start.8 = (f32[1024,128]{1,0:T(8,128)}, f32[1024,128]{1,0:T(8,128)S(1)}, u32[]{:S(2)}, u32[]{:S(2)}) collective-permute-start(f32[1024,128]{1,0:T(8,128)} %send_first.1), channel_id=1, source_target_pairs={{0,4},{4,0},{1,5},{5,1},{2,6},{6,2},{3,7},{7,3}} | collective-permute-start | bytes 1572872 | tf_op jit(solution)/shard_map/ppermute | solution.py:874
  756.1 62.4 %collective-permute-start.7 = (f32[1024,512]{1,0:T(8,128)}, f32[1024,512]{1,0:T(8,128)}, u32[]{:S(2)}, u32[]{:S(2)}) collective-permute-start(f32[1024,512]{1,0:T(8,128)} %get-tuple-element.78), channel_id=1, source_target_pairs={{0,4},{4,0},{1,5},{5,1},{2,6},{6,2},{3,7},{7,3}} | collective-permute-start | bytes 6291464 | tf_op jit(solution)/shard_map/ppermute | solution.py:874
  757.2 103.0 %collective-permute-start.6 = (f32[1024,512]{1,0:T(8,128)}, f32[1024,512]{1,0:T(8,128)}, u32[]{:S(2)}, u32[]{:S(2)}) collective-permute-start(f32[1024,512]{1,0:T(8,128)} %get-tuple-element.77), channel_id=1, source_target_pairs={{0,4},{4,0},{1,5},{5,1},{2,6},{6,2},{3,7},{7,3}} | collective-permute-start | bytes 6291464 | tf_op jit(solution)/shard_map/ppermute | solution.py:874
  797.0 108.1 %collective-permute-start.5 = (f32[1024,512]{1,0:T(8,128)}, f32[1024,512]{1,0:T(8,128)}, u32[]{:S(2)}, u32[]{:S(2)}) collective-permute-start(f32[1024,512]{1,0:T(8,128)} %get-tuple-element.76), channel_id=1, source_target_pairs={{0,4},{4,0},{1,5},{5,1},{2,6},{6,2},{3,7},{7,3}} | collective-permute-start | bytes 6291464 | tf_op jit(solution)/shard_map/ppermute | solution.py:874
  798.1 20.4 %copy-start = (f32[1024,128]{1,0:T(8,128)}, f32[1024,128]{1,0:T(8,128)S(1)}, u32[]{:S(2)}) copy-start(f32[1024,128]{1,0:T(8,128)S(1)} %collective-permute-done.8.recv_ref) | copy-start | bytes 1572868
  798.1 151.9 %collective-permute-start.4 = (f32[1024,512]{1,0:T(8,128)}, f32[1024,512]{1,0:T(8,128)}, u32[]{:S(2)}, u32[]{:S(2)}) collective-permute-start(f32[1024,512]{1,0:T(8,128)} %get-tuple-element.75), channel_id=1, source_target_pairs={{0,4},{4,0},{1,5},{5,1},{2,6},{6,2},{3,7},{7,3}} | collective-permute-start | bytes 6291464 | tf_op jit(solution)/shard_map/ppermute | solution.py:874
  818.5 176.4 %collective-permute-start.3 = (f32[1024,512]{1,0:T(8,128)}, f32[1024,512]{1,0:T(8,128)}, u32[]{:S(2)}, u32[]{:S(2)}) collective-permute-start(f32[1024,512]{1,0:T(8,128)} %get-tuple-element.74), channel_id=1, source_target_pairs={{0,4},{4,0},{1,5},{5,1},{2,6},{6,2},{3,7},{7,3}} | collective-permute-start | bytes 6291464 | tf_op jit(solution)/shard_map/ppermute | solution.py:874
  860.1 157.3 %collective-permute-start.2 = (f32[1024,256]{1,0:T(8,128)}, f32[1024,256]{1,0:T(8,128)}, u32[]{:S(2)}, u32[]{:S(2)}) collective-permute-start(f32[1024,256]{1,0:T(8,128)} %get-tuple-element.73), channel_id=1, source_target_pairs={{0,4},{4,0},{1,5},{5,1},{2,6},{6,2},{3,7},{7,3}} | collective-permute-start | bytes 3145736 | tf_op jit(solution)/shard_map/ppermute | solution.py:874
  875.0 151.4 %collective-permute-start.1 = (f32[1024,128]{1,0:T(8,128)}, f32[1024,128]{1,0:T(8,128)S(1)}, u32[]{:S(2)}, u32[]{:S(2)}) collective-permute-start(f32[1024,128]{1,0:T(8,128)} %get-tuple-element.72), channel_id=1, source_target_pairs={{0,4},{4,0},{1,5},{5,1},{2,6},{6,2},{3,7},{7,3}} | collective-permute-start | bytes 1572872 | tf_op jit(solution)/shard_map/ppermute | solution.py:874
  1026.5 0.8 copy-start.1
